TPU v7x, 16 devices: a whole 2x2x2 slice. The times are simulated.
16 devices in a mesh: dp: 2 (over z), fsdp: 8 (over y, x, core).
Axes of the slice: x: 2, y: 2, z: 2, core: 2. Of those that a mesh axis runs over, the one named last changes fastest.
Arguments:
- tokens: int32 [256, 256], P(('dp', 'fsdp'))
- grad_y: bfloat16 [256, 256, 1024], P(('dp', 'fsdp'))
- embedding: bfloat16 [33, 1024], P(None, 'fsdp')
- ln1_gain: bfloat16 [1024], P('fsdp')
- ln1_bias: bfloat16 [1024], P('fsdp')
- w_qkv: bfloat16 [1024, 3072], P('fsdp')
- b_qkv: bfloat16 [3072], P('fsdp')
- w_out: bfloat16 [1024, 1024], P('fsdp')
- b_out: bfloat16 [1024], P('fsdp')
- ln2_gain: bfloat16 [1024], P('fsdp')
- ln2_bias: bfloat16 [1024], P('fsdp')
- w_fc1: bfloat16 [1024, 4096], P('fsdp')
- b_fc1: bfloat16 [4096], P('fsdp')
- w_fc2: bfloat16 [4096, 1024], P('fsdp')
- b_fc2: bfloat16 [1024], P('fsdp')
Outputs:
- output 1: bfloat16 [256, 256, 1024], P(('dp', 'fsdp'))
- output 2: float32 [33, 1024], P(None, 'fsdp')
- output 3: float32 [1024], P('fsdp')
- output 4: float32 [1024], P('fsdp')
- output 5: float32 [1024, 3072], P('fsdp')
- output 6: float32 [3072], P('fsdp')
- output 7: float32 [1024, 1024], P('fsdp')
- output 8: float32 [1024], P('fsdp')
- output 9: float32 [1024], P('fsdp')
- output 10: float32 [1024], P('fsdp')
- output 11: float32 [1024, 4096], P('fsdp')
- output 12: float32 [4096], P('fsdp')
- output 13: float32 [4096, 1024], P('fsdp')
- output 14: float32 [1024], P('fsdp')
All inputs are finite; a program needn't handle non-finite values.
Results may differ from a plain program's by a relative error of at most 0.0115973.
Values are sent between devices in bfloat16 or wider.
A program may use at most 1 GiB of HBM per device.

v0:
```python
import functools
import jax
import jax.numpy as jnp
from jax import lax
from jax.sharding import PartitionSpec as P

HEAD_DIM = 64
MASK_ID = 32
PAD_ID = 1
MASK_RATIO = 0.15 * 0.8
LN_EPS = 1e-5
ROPE_BASE = 10000.0


def f32_einsum(form, lhs, rhs):
    return jnp.einsum(form, lhs, rhs, preferred_element_type=jnp.float32)


def norm_fwd(x_val, gain, bias):
    centered = x_val - jnp.mean(x_val, axis=-1, keepdims=True)
    inv_std = lax.rsqrt(jnp.mean(centered * centered, axis=-1, keepdims=True) + LN_EPS)
    x_hat = centered * inv_std
    return x_hat * gain.astype(jnp.float32) + bias.astype(jnp.float32), x_hat, inv_std


def norm_bwd(d_out, x_hat, inv_std, gain):
    d_hat = d_out * gain.astype(jnp.float32)
    d_x = inv_std * (d_hat - jnp.mean(d_hat, axis=-1, keepdims=True)
                     - x_hat * jnp.mean(d_hat * x_hat, axis=-1, keepdims=True))
    return d_x, jnp.sum(d_out * x_hat, axis=(0, 1)), jnp.sum(d_out, axis=(0, 1))


def rope_tables(seq_len):
    inv_freq = 1.0 / (ROPE_BASE ** (jnp.arange(0, HEAD_DIM, 2, dtype=jnp.float32) / HEAD_DIM))
    angles = jnp.arange(seq_len, dtype=jnp.float32)[:, None] * inv_freq[None, :]
    return jnp.cos(angles)[:, None, :], jnp.sin(angles)[:, None, :]


def rotate(x_val, cos_tab, sin_tab):
    half_dim = x_val.shape[-1] // 2
    low_half = x_val[..., :half_dim]
    high_half = x_val[..., half_dim:]
    return jnp.concatenate([low_half * cos_tab - high_half * sin_tab, high_half * cos_tab + low_half * sin_tab], axis=-1)


def layer_step(tokens, grad_y, weights):
    (embedding, ln1_gain, ln1_bias, w_qkv, b_qkv, w_out, b_out,
     ln2_gain, ln2_bias, w_fc1, b_fc1, w_fc2, b_fc2) = weights
    batch_rows, seq_len = tokens.shape
    vocab_size, model_dim = embedding.shape
    num_heads = model_dim // HEAD_DIM
    one_hot = tokens[:, :, None] == jnp.arange(vocab_size)[None, None, :]
    is_mask = tokens == MASK_ID
    is_pad = tokens == PAD_ID
    mask_count = jnp.sum(is_mask, axis=1).astype(jnp.float32)
    real_count = jnp.sum(jnp.logical_not(is_pad), axis=1).astype(jnp.float32)
    factor = (1.0 - MASK_RATIO) / (1.0 - mask_count / real_count)
    keep_scale = jnp.where(is_mask | is_pad, 0.0, factor[:, None])[:, :, None]
    looked_up = f32_einsum('blv,vd->bld', one_hot.astype(jnp.bfloat16), embedding)
    x_res = (looked_up * keep_scale).astype(jnp.bfloat16).astype(jnp.float32)
    norm_one, hat_one, inv_one = norm_fwd(x_res, ln1_gain, ln1_bias)
    h_one = norm_one.astype(jnp.bfloat16)
    qkv_proj = f32_einsum('bld,de->ble', h_one, w_qkv) + b_qkv.astype(jnp.float32)
    qkv_proj = qkv_proj.reshape(batch_rows, seq_len, 3, num_heads, HEAD_DIM)
    cos_tab, sin_tab = rope_tables(seq_len)
    queries = rotate(qkv_proj[:, :, 0] * HEAD_DIM ** -0.5, cos_tab, sin_tab).astype(jnp.bfloat16)
    key_rows = rotate(qkv_proj[:, :, 1], cos_tab, sin_tab).astype(jnp.bfloat16)
    values = qkv_proj[:, :, 2].astype(jnp.bfloat16)
    scores = f32_einsum('bqhd,bkhd->bhqk', queries, key_rows)
    scores = jnp.where(is_pad[:, None, None, :], -1e30, scores)
    attn_prob = jax.nn.softmax(scores, axis=-1)
    prob_b16 = attn_prob.astype(jnp.bfloat16)
    context = f32_einsum('bhqk,bkhd->bqhd', prob_b16, values).astype(jnp.bfloat16)
    context = context.reshape(batch_rows, seq_len, model_dim)
    x_mid = x_res + f32_einsum('bld,de->ble', context, w_out) + b_out.astype(jnp.float32)
    norm_two, hat_two, inv_two = norm_fwd(x_mid, ln2_gain, ln2_bias)
    h_two = norm_two.astype(jnp.bfloat16)
    pre_act = f32_einsum('bld,df->blf', h_two, w_fc1) + b_fc1.astype(jnp.float32)
    hidden_act, gelu_pull = jax.vjp(functools.partial(jax.nn.gelu, approximate=False), pre_act)
    act_b16 = hidden_act.astype(jnp.bfloat16)
    hidden = (x_mid + f32_einsum('blf,fd->bld', act_b16, w_fc2) + b_fc2.astype(jnp.float32)).astype(jnp.bfloat16)

    grad_res = grad_y.astype(jnp.float32)
    g_b_fc2 = jnp.sum(grad_res, axis=(0, 1))
    g_w_fc2 = f32_einsum('blf,bld->fd', act_b16, grad_y)
    d_pre = gelu_pull(f32_einsum('bld,fd->blf', grad_y, w_fc2))[0]
    g_b_fc1 = jnp.sum(d_pre, axis=(0, 1))
    d_pre = d_pre.astype(jnp.bfloat16)
    g_w_fc1 = f32_einsum('bld,blf->df', h_two, d_pre)
    d_two, g_ln2_gain, g_ln2_bias = norm_bwd(f32_einsum('blf,df->bld', d_pre, w_fc1), hat_two, inv_two, ln2_gain)
    d_mid = grad_res + d_two
    g_b_out = jnp.sum(d_mid, axis=(0, 1))
    d_mid_b16 = d_mid.astype(jnp.bfloat16)
    g_w_out = f32_einsum('bld,ble->de', context, d_mid_b16)
    d_ctx = f32_einsum('ble,de->bld', d_mid_b16, w_out).astype(jnp.bfloat16)
    d_ctx = d_ctx.reshape(batch_rows, seq_len, num_heads, HEAD_DIM)
    d_prob = f32_einsum('bqhd,bkhd->bhqk', d_ctx, values)
    d_val = f32_einsum('bhqk,bqhd->bkhd', prob_b16, d_ctx)
    d_scores = attn_prob * (d_prob - jnp.sum(d_prob * attn_prob, axis=-1, keepdims=True))
    d_scores = d_scores.astype(jnp.bfloat16)
    d_query = rotate(f32_einsum('bhqk,bkhd->bqhd', d_scores, key_rows), cos_tab, -sin_tab) * HEAD_DIM ** -0.5
    d_key = rotate(f32_einsum('bhqk,bqhd->bkhd', d_scores, queries), cos_tab, -sin_tab)
    d_qkv = jnp.stack([d_query, d_key, d_val], axis=2).reshape(batch_rows, seq_len, 3 * model_dim)
    g_b_qkv = jnp.sum(d_qkv, axis=(0, 1))
    d_qkv = d_qkv.astype(jnp.bfloat16)
    g_w_qkv = f32_einsum('bld,ble->de', h_one, d_qkv)
    d_one, g_ln1_gain, g_ln1_bias = norm_bwd(f32_einsum('ble,de->bld', d_qkv, w_qkv), hat_one, inv_one, ln1_gain)
    d_in = d_mid + d_one
    g_embedding = f32_einsum('blv,bld->vd', one_hot.astype(jnp.float32), d_in * keep_scale)
    full_grads = (g_embedding, g_ln1_gain, g_ln1_bias, g_w_qkv, g_b_qkv, g_w_out, g_b_out,
                  g_ln2_gain, g_ln2_bias, g_w_fc1, g_b_fc1, g_w_fc2, g_b_fc2)
    return hidden, full_grads


def solution(mesh):
    row_spec = P(('dp', 'fsdp'), None)
    act_spec = P(('dp', 'fsdp'), None, None)
    param_specs = (P(None, 'fsdp'),) + (P('fsdp'),) * 12

    def local_step(tokens, grad_y, *shards):
        full_params = [lax.all_gather(shards[0], 'fsdp', axis=1, tiled=True)]
        full_params += [lax.all_gather(shard, 'fsdp', axis=0, tiled=True) for shard in shards[1:]]
        hidden, full_grads = layer_step(tokens, grad_y, full_params)
        grad_parts = [lax.psum(lax.psum_scatter(full_grads[0], 'fsdp', scatter_dimension=1, tiled=True), 'dp')]
        grad_parts += [lax.psum(lax.psum_scatter(full_grad, 'fsdp', scatter_dimension=0, tiled=True), 'dp')
                       for full_grad in full_grads[1:]]
        return (hidden,) + tuple(grad_parts)

    return jax.shard_map(local_step, mesh=mesh, in_specs=(row_spec, act_spec) + param_specs,
                         out_specs=(act_spec,) + param_specs, check_vma=False)
```

profile of v0, /device:TPU:0, one launch (start us, length us, event | category | flops | bytes accessed | tf_op | source)
XLA Modules:
  0.0 1555.9 jit_solution(15329814339271676963)
XLA Ops:
  7.3 0.7 all-gather.13.cloned.1.call-update
  8.0 0.7 all-gather.15.cloned.1.call-update
  8.8 0.7 all-gather.17.cloned.1.call-update
  10.1 0.8 convert_reduce_fusion.2
  10.9 10.8 all_gather.39
  21.9 3.7 convert_reduce_fusion
  25.6 3.4 copy-done
  29.0 2.8 fusion.30
  31.9 9.0 all-gather
  40.8 7.9 all-gather.1
  48.8 8.9 all-gather.2
  57.6 0.8 fusion.92
  58.5 7.8 all-gather.3
  66.3 0.6 convert_element_type.134
  66.9 8.9 all-gather.4
  75.8 0.6 convert_element_type.135
  76.4 7.7 all-gather.6
  84.1 0.6 convert_element_type.137
  84.8 9.5 all-gather.5
  94.3 0.6 convert_element_type.136
  94.9 35.6 %convolution_add_fusion = f32[16,256,3072]{2,1,0:T(8,128)} fusion(f32[3072]{0:T(1024)S(1)} %bitcast.125, bf16[1024,3072]{1,0:T(8,128)(2,1)} %all-gather.13.cloned.1.call-done, bf16[16,256,1024]{2,1,0:T(8,128)(2,1)} %copy-done, f32[1024]{0:T(1024)S(1)} %bitcast.126, f32[1024]{0:T(1024)S(1)} %bitcast.121, f32[16,256]{1,0:T(8,128)S(1)} %add_rsqrt_fusion.1, ...), kind=kOutput, calls=%fused_computation.35 | convolution fusion | flops 25807552512 | bytes 65064960 | tf_op jit(solution)/shard_map/bld,de->ble/dot_general | solution.py:16
  130.5 48.8 %copy.58 = f32[16,256,3072]{1,2,0:T(8,128)} copy(f32[16,256,3072]{2,1,0:T(8,128)} %convolution_add_fusion) | data formatting | bytes 100663296 | tf_op jit(solution)/shard_map/add | solution.py:63
  179.3 17.7 %fusion.102 = (f32[16,256,1,16,64]{1,4,3,2,0:T(8,128)S(1)}, f32[16,256,1,16,64]{1,4,3,2,0:T(8,128)}) fusion(f32[16,256,3,16,64]{1,4,3,2,0:T(8,128)} %bitcast.107), kind=kLoop, calls=%fused_computation.155 | loop fusion | bytes 67108864 | tf_op jit(solution)/shard_map/slice | solution.py:66
  197.0 17.0 %copy_bitcast_fusion = (f32[16,256,16,64]{1,3,2,0:T(8,128)}, f32[16,256,16,64]{1,3,2,0:T(8,128)}) fusion(f32[16,256,1,16,64]{1,4,3,2,0:T(8,128)} %get-tuple-element.54, f32[16,256,1,16,64]{1,4,3,2,0:T(8,128)S(1)} %get-tuple-element.53), kind=kLoop, calls=%fused_computation.57 | loop fusion | flops 4194304 | bytes 67108864 | tf_op jit(solution)/shard_map/squeeze | solution.py:67
  214.0 19.1 %subtract_convert_fusion.1 = (bf16[16,256,16,32]{1,3,2,0:T(8,128)(2,1)}, bf16[16,256,16,32]{1,3,2,0:T(8,128)(2,1)}, bf16[16,256,16,32]{1,3,2,0:T(8,128)(2,1)}, bf16[16,256,16,32]{1,3,2,0:T(8,128)(2,1)}) fusion(f32[16,256,16,64]{1,3,2,0:T(8,128)} %get-tuple-element.87, f32[256,32]{0,1:T(8,128)S(1)} %get-tuple-element.71, ...), kind=kLoop, calls=%fused_computation.104 | loop fusion | flops 33554432 | bytes 50397184 | tf_op jit(solution)/shard_map/convert.2
  233.1 32.0 %fusion.103 = (f32[16,16,256]{2,1,0:T(8,128)S(1)}, f32[16,16,256,256]{2,3,1,0:T(8,128)}) fusion(pred[16,256]{1,0:T(8,128)(4,1)S(1)} %get-tuple-element.52, bf16[16,256,16,32]{1,3,2,0:T(8,128)(2,1)} %get-tuple-element.66, bf16[16,256,16,32]{1,3,2,0:T(8,128)(2,1)} %get-tuple-element.67, bf16[16,256,16,32]{1,3,2,0:T(8,128)(2,1)} %get-tuple-element.60, ...), kind=kOutput, calls=%fused_computation.156 | convolution fusion | flops 2231369984 | bytes 84152320 | tf_op jit(solution)/shard_map/sub | solution.py:71
  265.1 30.3 %fusion.62 = bf16[16,16,64,256]{3,2,1,0:T(8,128)(2,1)} fusion(f32[16,16,256,256]{2,3,1,0:T(8,128)} %get-tuple-element.76, f32[16,16,256]{2,1,0:T(8,128)S(1)} %get-tuple-element.75, f32[16,256,3,16,64]{1,4,3,2,0:T(8,128)} %bitcast.108), kind=kOutput, calls=%fused_computation.110 | convolution fusion | flops 2185232384 | bytes 84148224 | tf_op jit(solution)/shard_map/bhqk,bkhd->bqhd/dot_general | solution.py:16
  295.4 18.2 %fusion.104 = (f32[16,256]{1,0:T(8,128)S(1)}, f32[16,256,1024]{2,1,0:T(8,128)}) fusion(f32[1024]{0:T(1024)S(1)} %bitcast.131, bf16[16,256,1024]{1,2,0:T(8,128)(2,1)} %bitcast.138, bf16[1024,1024]{1,0:T(8,128)(2,1)} %all-gather.15.cloned.1.call-done, bf16[16,256,1024]{2,1,0:T(8,128)(2,1)} %copy-done), kind=kOutput, calls=%fused_computation.157 | convolution fusion | flops 8606707712 | bytes 35672064 | tf_op jit(solution)/shard_map/bld,de->ble/dot_general | solution.py:16
  313.6 7.0 multiply_reduce_fusion.3
  320.8 71.4 %fusion.14 = (u16[256,4096]{1,0:T(8,128)(2,1)S(1)}, u16[256,4096]{1,0:T(8,128)(2,1)}, f32[16,256,4096]{2,1,0:T(8,128)}) fusion(f32[4096]{0:T(1024)S(1)} %bitcast.114, bf16[1024,4096]{1,0:T(8,128)(2,1)} %all-gather.17.cloned.1.call-done, f32[16,256,1024]{2,1,0:T(8,128)} %get-tuple-element.78, f32[1024]{0:T(1024)S(1)} %bitcast.128, f32[1024]{0:T(1024)S(1)} %bitcast.117, ...), kind=kOutput, calls=%fused_computation.33 | convolution fusion | flops 34613493760 | bytes 96526336 | tf_op jit(solution)/shard_map/bld,df->blf/dot_general | solution.py:16
  392.2 157.1 %multiply_convert_fusion.1 = (bf16[16,256,4096]{2,1,0:T(8,128)(2,1)}, f32[16,256,4096]{2,1,0:T(8,128)}) fusion(f32[16,256,4096]{2,1,0:T(8,128)} %get-tuple-element.79, f32[4096]{0:T(1024)S(1)} %bitcast.115, u16[256,4096]{1,0:T(8,128)(2,1)} %get-tuple-element.15, u16[256,4096]{1,0:T(8,128)(2,1)S(1)} %get-tuple-element.14), kind=kLoop, calls=%fused_computation.11 | loop fusion | flops 1191182336 | bytes 171982848 | tf_op jit(solution)/shard_map/convert_element_type | solution.py:80
  549.4 85.9 %fusion.105 = (f32[4096]{0:T(1024)}, bf16[16,256,4096]{2,1,0:T(8,128)(2,1)}) fusion(f32[16,256,4096]{2,1,0:T(8,128)} %get-tuple-element.48, bf16[16,256,1024]{2,1,0:T(8,128)(2,1)} %param.16, bf16[4096,1024]{1,0:T(8,128)(2,1)} %all-gather.19.cloned.1.call-done, f32[16,256,4096]{2,1,0:T(8,128)} %get-tuple-element.79, f32[4096]{0:T(1024)S(1)} %bitcast.116), kind=kOutput, calls=%fused_computation.158 | convolution fusion | flops 34628169728 | bytes 184582144 | tf_op jit(solution)/shard_map/bld,fd->blf/dot_general | solution.py:16
  635.3 47.4 %multiply_reduce_fusion.1 = (f32[1024]{0:T(1024)}, f32[16,256]{1,0:T(8,128)S(1)}, f32[16,256]{1,0:T(8,128)S(1)}, f32[1024]{0:T(1024)}, f32[16,256,1024]{2,1,0:T(8,128)}) fusion(f32[16,256,1024]{2,1,0:T(8,128)} %get-tuple-element.78, f32[16,256]{1,0:T(8,128)S(1)} %copy-done.19, f32[16,256]{1,0:T(8,128)S(1)} %copy-done.10, f32[1024]{0:T(1024)S(1)} %bitcast.118, ...), kind=kOutput, calls=%fused_computation.63 | convolution fusion | flops 34397478912 | bytes 75575296 | tf_op jit(solution)/shard_map/blf,df->bld/dot_general | solution.py:16
  682.7 18.7 %fusion.100 = (f32[1024]{0:T(1024)}, f32[16,256,1024]{2,1,0:T(8,128)}, f32[1024]{0:T(1024)}) fusion(f32[16,256]{1,0:T(8,128)S(1)} %broadcast_multiply_fusion.2, f32[16,256,1024]{2,1,0:T(8,128)} %get-tuple-element.78, f32[16,256]{1,0:T(8,128)S(1)} %copy-done.10, f32[16,256]{1,0:T(8,128)S(1)} %broadcast_multiply_fusion.3, ...), kind=kLoop, calls=%fused_computation.154 | loop fusion | flops 46135296 | bytes 58798080 | tf_op jit(solution)/shard_map/reduce_sum | solution.py:92
  701.5 17.0 %convolution_convert_fusion = bf16[16,256,1024]{2,1,0:T(8,128)(2,1)} fusion(f32[16,256,1024]{2,1,0:T(8,128)} %get-tuple-element.46, bf16[1024,1024]{1,0:T(8,128)(2,1)S(1)} %copy-done.45), kind=kOutput, calls=%fused_computation.109 | convolution fusion | flops 8598323200 | bytes 27262976 | tf_op jit(solution)/shard_map/ble,de->bld/dot_general | solution.py:16
  718.5 12.3 copy.64
  730.8 51.2 %multiply_reduce_fusion = (f32[16,16,256]{2,1,0:T(8,128)S(1)}, f32[16,16,256,256]{2,3,1,0:T(8,128)}) fusion(f32[16,16,256,256]{2,3,1,0:T(8,128)} %get-tuple-element.76, f32[16,16,256]{2,1,0:T(8,128)S(1)} %copy-done.6, bf16[16,256,16,64]{1,3,2,0:T(8,128)(2,1)} %bitcast.112, f32[16,256,3,16,64]{1,4,3,2,0:T(8,128)} %bitcast.109), kind=kOutput, calls=%fused_computation.9 | convolution fusion | flops 2197749760 | bytes 151519232 | tf_op jit(solution)/shard_map/bqhd,bkhd->bhqk/dot_general | solution.py:16
  782.0 52.8 %multiply_convert_fusion = bf16[16,16,256,256]{2,3,1,0:T(8,128)(2,1)} fusion(f32[16,16,256,256]{2,3,1,0:T(8,128)} %get-tuple-element.82, f32[16,16,256]{2,1,0:T(8,128)S(1)} %get-tuple-element.81, f32[16,16,256,256]{2,3,1,0:T(8,128)} %get-tuple-element.76, f32[16,16,256]{2,1,0:T(8,128)S(1)} %copy-done.6), kind=kLoop, calls=%fused_computation.8 | loop fusion | flops 67108864 | bytes 168296448 | tf_op jit(solution)/shard_map/convert_element_type | solution.py:100
  834.8 23.5 %convolution_bitcast_fusion.1 = f32[16,256,16,64]{1,3,2,0:T(8,128)} fusion(bf16[16,16,256,256]{2,3,1,0:T(8,128)(2,1)} %multiply_convert_fusion, bf16[16,256,16,32]{1,3,2,0:T(8,128)(2,1)} %get-tuple-element.60, bf16[16,256,16,32]{1,3,2,0:T(8,128)(2,1)} %get-tuple-element.59), kind=kOutput, calls=%fused_computation.85 | convolution fusion | flops 2164260864 | bytes 58720256 | tf_op jit(solution)/shard_map/bhqk,bqhd->bkhd/dot_general | solution.py:16
  858.3 20.3 %convolution_bitcast_fusion.2 = f32[16,256,16,64]{1,3,2,0:T(8,128)} fusion(bf16[16,16,256,256]{2,3,1,0:T(8,128)(2,1)} %multiply_convert_fusion, bf16[16,256,16,32]{1,3,2,0:T(8,128)(2,1)} %get-tuple-element.66, bf16[16,256,16,32]{1,3,2,0:T(8,128)(2,1)} %get-tuple-element.67), kind=kOutput, calls=%fused_computation.86 | convolution fusion | flops 2164260864 | bytes 58720256 | tf_op jit(solution)/shard_map/bhqk,bkhd->bqhd/dot_general | solution.py:16
  878.5 30.9 %fusion.47 = f32[16,256,1,16,64]{1,4,3,0,2:T(8,128)} fusion(bf16[16,256,16,64]{1,3,2,0:T(8,128)(2,1)} %bitcast.113, f32[16,16,256,256]{2,3,1,0:T(8,128)} %get-tuple-element.76, f32[16,16,256]{2,1,0:T(8,128)S(1)} %copy-done.6), kind=kOutput, calls=%fused_computation.84 | convolution fusion | flops 2181038080 | bytes 92536832 | tf_op jit(solution)/shard_map/bhqk,bqhd->bkhd/dot_general | solution.py:16
  909.5 16.1 %fusion.79 = f32[1024,1024]{1,0:T(8,128)} fusion(bf16[16,256,1024]{1,2,0:T(8,128)(2,1)} %bitcast.139, f32[16,256,1024]{2,1,0:T(8,128)} %get-tuple-element.46), kind=kOutput, calls=%fused_computation.121 | convolution fusion | flops 8594128896 | bytes 29360128 | tf_op jit(solution)/shard_map/bld,ble->de/dot_general | solution.py:16
  925.7 17.6 %subtract_bitcast_fusion = (f32[16,256,1,16,32]{1,4,3,0,2:T(8,128)}, f32[16,256,1,16,32]{1,4,3,0,2:T(8,128)}, f32[16,256,16,32]{1,3,2,0:T(8,128)S(1)}, f32[16,256,16,32]{1,3,2,0:T(8,128)S(1)}) fusion(f32[16,256,16,64]{1,3,2,0:T(8,128)} %convolution_bitcast_fusion.2, f32[256,32]{0,1:T(8,128)S(1)} %copy-done.12, f32[256,32]{0,1:T(8,128)S(1)} %copy-done.4, ...), kind=kLoop, calls=%fused_computation.100 | loop fusion | flops 25165824 | bytes 67174400 | tf_op jit(solution)/shard_map/concatenate | solution.py:43
  943.4 12.0 maximum_multiply_fusion
  955.3 6.1 maximum_bitcast_fusion
  961.4 24.9 %fusion.11 = bf16[16,256,3,16,64]{1,4,3,0,2:T(8,128)(2,1)} fusion(f32[16,256,1,16,64]{1,4,3,0,2:T(8,128)} %fusion.47, f32[16,256,1,16,64]{1,4,3,0,2:T(8,128)} %maximum_bitcast_fusion, f32[16,256,1,16,64]{1,4,3,0,2:T(8,128)} %maximum_multiply_fusion), kind=kLoop, calls=%fused_computation.29 | loop fusion | flops 25165824 | bytes 75497472 | tf_op jit(solution)/shard_map/convert_element_type | solution.py:105
  986.3 12.6 copy.68
  998.9 8.3 copy-done.1
  1007.3 35.4 %convolution_bitcast_fusion.3 = f32[1024,3072]{1,0:T(8,128)} fusion(bf16[16,256,3072]{1,2,0:T(8,128)(2,1)S(1)} %bitcast.110, bf16[16,256,1024]{2,1,0:T(8,128)(2,1)} %copy-done, f32[1024]{0:T(1024)S(1)} %bitcast.127, f32[1024]{0:T(1024)S(1)} %bitcast.122, f32[16,256]{1,0:T(8,128)S(1)} %copy-done.17, f32[16,256]{1,0:T(8,128)S(1)} %copy-done.8), kind=kOutput, calls=%fused_computation.111 | convolution fusion | flops 25794969600 | bytes 46178304 | tf_op jit(solution)/shard_map/bld,ble->de/dot_general | solution.py:16
  1042.8 48.9 %fusion.44 = f32[1024,4096]{1,0:T(8,128)} fusion(bf16[16,256,4096]{2,1,0:T(8,128)(2,1)} %get-tuple-element.85, f32[16,256,1024]{2,1,0:T(8,128)} %get-tuple-element.78, f32[1024]{0:T(1024)S(1)} %bitcast.129, f32[1024]{0:T(1024)S(1)} %bitcast.120, f32[16,256]{1,0:T(8,128)S(1)} %copy-done.20, f32[16,256]{1,0:T(8,128)S(1)} %copy-done.11), kind=kOutput, calls=%fused_computation.82 | convolution fusion | flops 34380709888 | bytes 67149824 | tf_op jit(solution)/shard_map/bld,blf->df/dot_general | solution.py:16
  1091.7 43.7 %convolution_bitcast_fusion = f32[4096,1024]{1,0:T(8,128)} fusion(bf16[16,256,4096]{2,1,0:T(8,128)(2,1)} %get-tuple-element.47, bf16[16,256,1024]{2,1,0:T(8,128)(2,1)} %param.16), kind=kOutput, calls=%fused_computation.83 | convolution fusion | flops 34359738368 | bytes 58720256 | tf_op jit(solution)/shard_map/blf,bld->fd/dot_general | solution.py:16
  1138.6 7.7 all-gather.7
  1146.3 38.9 %fusion.29 = (f32[1024]{0:T(1024)S(1)}, f32[16,256]{1,0:T(8,128)S(1)}, f32[16,256]{1,0:T(8,128)S(1)}, f32[1024]{0:T(1024)S(1)}, f32[16,256,1024]{2,1,0:T(8,128)}) fusion(bf16[16,256,1024]{2,1,0:T(8,128)(2,1)} %copy-done, f32[16,256]{1,0:T(8,128)S(1)} %copy-done.17, f32[16,256]{1,0:T(8,128)S(1)} %copy-done.8, f32[1024]{0:T(1024)S(1)} %bitcast.123, ...), kind=kOutput, calls=%fused_computation.54 | convolution fusion | flops 25811738624 | bytes 56700928 | tf_op jit(solution)/shard_map/ble,de->bld/dot_general | solution.py:16
  1185.3 15.6 %fusion.84 = f32[33,1024]{1,0:T(8,128)} fusion(f32[16,256,1024]{2,1,0:T(8,128)} %get-tuple-element.46, bf16[16,256,1024]{2,1,0:T(8,128)(2,1)} %copy-done, f32[16,256,1024]{2,1,0:T(8,128)} %get-tuple-element.83, f32[16,256]{1,0:T(8,128)S(1)} %broadcast_multiply_fusion, f32[16,256]{1,0:T(8,128)S(1)} %broadcast_multiply_fusion.1, f32[1024]{0:T(1024)S(1)} %bitcast.124, ...), kind=kOutput, calls=%fused_computation.124 | convolution fusion | flops 318902272 | bytes 42180608 | tf_op jit(solution)/shard_map/blv,bld->vd/dot_general | solution.py:16
  1201.0 15.8 %fusion.10 = f32[3,16,64]{2,1,0:T(8,128)S(1)} fusion(f32[16,256,1,16,64]{1,4,3,0,2:T(8,128)} %fusion.47, f32[16,256,1,16,64]{1,4,3,0,2:T(8,128)} %maximum_bitcast_fusion, f32[16,256,1,16,64]{1,4,3,0,2:T(8,128)} %maximum_multiply_fusion), kind=kLoop, calls=%fused_computation.28 | loop fusion | flops 37745664 | bytes 50343936 | tf_op jit(solution)/shard_map/reduce_sum | solution.py:104
  1217.0 25.6 %all-reduce.8 = (f32[1024]{0:T(1024)S(1)}, f32[1024]{0:T(1024)S(1)}, f32[3072]{0:T(1024)S(1)}, f32[1024]{0:T(1024)S(1)}, f32[1024]{0:T(1024)S(1)}, /*index=5*/f3...) all-reduce(f32[1024]{0:T(1024)S(1)} %get-tuple-element.18, ...), channel_id=3, replica_groups=mesh['dp'=2,'fsdp'=8] {'fsdp'}, use_global_device_ids=true, to_apply=%region_16.17.clone | all-reduce | flops 13312 | bytes 106496
  1243.2 112.5 %reduce-scatter.14.cloned.1.call-done = f32[512,1024]{1,0:T(8,128)} async-done(((f32[4096,1024]{1,0:T(8,128)}), f32[512,1024]{1,0:T(8,128)}) %reduce-scatter.14.cloned.1.call-update) | async-done | bytes 2097168 | tf_op jit(solution)/shard_map/reduce_scatter | solution.py:125
  1355.8 43.6 %add_convert_fusion = bf16[16,256,1024]{2,1,0:T(8,128)(2,1)} fusion(f32[16,256,1024]{2,1,0:T(8,128)} %get-tuple-element.78, bf16[16,256,4096]{2,1,0:T(8,128)(2,1)} %get-tuple-element.47, bf16[4096,1024]{1,0:T(8,128)(2,1)} %all-gather.19.cloned.1.call-done, f32[1024]{0:T(1024)S(1)} %bitcast.130), kind=kOutput, calls=%fused_computation.69 | convolution fusion | flops 34372321280 | bytes 67112960 | tf_op jit(solution)/shard_map/blf,fd->bld/dot_general | solution.py:16
  1399.4 10.3 all-reduce.9
  1409.7 128.3 %all-reduce.13.cloned.1.call-done = (f32[128,3072]{1,0:T(8,128)}, f32[128,1024]{1,0:T(8,128)}, f32[128,4096]{1,0:T(8,128)}, f32[512,1024]{1,0:T(8,128)}) async-done(((f32[128,3072]{1,0:T(8,128)}, f32[128,1024]{1,0:T(8,128)}, f32[128,4096]{1,0:T(8,128)}, f32[512,1024]{1,0:T(8,128)}), (f32[128,3072]{1,0:T(8,128)}, f32[128,1024]{1,0:T(8,128)}, f32[128,4096]{1,0:T(8,128)}, ...) | async-done | bytes 6291472 | tf_op jit(solution)/shard_map/psum | solution.py:125
  1538.0 2.7 copy.104
  1540.7 1.9 copy.105
  1542.6 3.1 copy.106
  1545.7 3.2 copy.107
  (144 shorter events, 3.2 us)
Async XLA Ops:
  7.2 24.7 %copy-start.39 = (bf16[128]{0:T(256)(128)(2,1)S(1)}, bf16[128]{0:T(256)(128)(2,1)}, u32[]{:S(2)}) copy-start(bf16[128]{0:T(256)(128)(2,1)} %param.18) | copy-start | bytes 772
  7.2 33.7 %copy-start.40 = (bf16[128]{0:T(256)(128)(2,1)S(1)}, bf16[128]{0:T(256)(128)(2,1)}, u32[]{:S(2)}) copy-start(bf16[128]{0:T(256)(128)(2,1)} %param.19) | copy-start | bytes 772
  7.2 41.5 %copy-start.38 = (bf16[384]{0:T(512)(128)(2,1)S(1)}, bf16[384]{0:T(512)(128)(2,1)}, u32[]{:S(2)}) copy-start(bf16[384]{0:T(512)(128)(2,1)} %param.21) | copy-start | bytes 2308
  7.2 51.2 %copy-start.41 = (bf16[128]{0:T(256)(128)(2,1)S(1)}, bf16[128]{0:T(256)(128)(2,1)}, u32[]{:S(2)}) copy-start(bf16[128]{0:T(256)(128)(2,1)} %param.23) | copy-start | bytes 772
  7.2 59.7 %copy-start.42 = (bf16[128]{0:T(256)(128)(2,1)S(1)}, bf16[128]{0:T(256)(128)(2,1)}, u32[]{:S(2)}) copy-start(bf16[128]{0:T(256)(128)(2,1)} %param.24) | copy-start | bytes 772
  7.2 69.2 %copy-start.37 = (bf16[512]{0:T(512)(128)(2,1)S(1)}, bf16[512]{0:T(512)(128)(2,1)}, u32[]{:S(2)}) copy-start(bf16[512]{0:T(512)(128)(2,1)} %param.27) | copy-start | bytes 3076
  7.2 77.5 %copy-start.43 = (bf16[128]{0:T(256)(128)(2,1)S(1)}, bf16[128]{0:T(256)(128)(2,1)}, u32[]{:S(2)}) copy-start(bf16[128]{0:T(256)(128)(2,1)} %param.25) | copy-start | bytes 772
  7.3 87.6 %all-gather.13.cloned.1.call-start = ((), (), s32[]{:S(2)}) async-start(), calls=%async_computation.5 | async-start | bytes 7077888 | tf_op jit(solution)/shard_map/all_gather | solution.py:122
  8.0 287.4 %all-gather.15.cloned.1.call-start = ((), (), s32[]{:S(2)}) async-start(), calls=%async_computation.6 | async-start | bytes 2359296 | tf_op jit(solution)/shard_map/all_gather | solution.py:122
  8.7 312.0 %all-gather.17.cloned.1.call-start = ((), (), s32[]{:S(2)}) async-start(), calls=%async_computation.7 | async-start | bytes 9437184 | tf_op jit(solution)/shard_map/all_gather | solution.py:122
  9.5 539.9 %all-gather.19.cloned.1.call-start = ((), (), s32[]{:S(2)}) async-start(), calls=%async_computation.8 | async-start | bytes 9437184 | tf_op jit(solution)/shard_map/all_gather | solution.py:122
  10.0 1233.2 %reduce-scatter.10.cloned.1.call-start = ((), (), s32[]{:S(2)}) async-start(), calls=%async_computation.11 | async-start | bytes 4718592 | tf_op jit(solution)/shard_map/reduce_scatter | solution.py:125
  21.9 35.7 %copy-start.14 = (f32[16,256]{1,0:T(8,128)}, f32[16,256]{1,0:T(8,128)S(1)}, u32[]{:S(2)}) copy-start(f32[16,256]{1,0:T(8,128)S(1)} %or_select_fusion) | copy-start | bytes 49156
  25.6 3.4 copy-start
  25.6 104.8 %copy-start.7 = (f32[16,256]{1,0:T(8,128)}, f32[16,256]{1,0:T(8,128)S(1)}, u32[]{:S(2)}) copy-start(f32[16,256]{1,0:T(8,128)S(1)} %broadcast_multiply_fusion.5) | copy-start | bytes 49156
  31.8 98.6 %copy-start.16 = (f32[16,256]{1,0:T(8,128)}, f32[16,256]{1,0:T(8,128)S(1)}, u32[]{:S(2)}) copy-start(f32[16,256]{1,0:T(8,128)S(1)} %add_rsqrt_fusion.1) | copy-start | bytes 49156
  40.8 89.6 %copy-start.28 = (f32[8,1,128]{2,1,0:T(1,128)}, f32[8,1,128]{2,1,0:T(1,128)S(1)}, u32[]{:S(2)}) copy-start(f32[8,1,128]{2,1,0:T(1,128)S(1)} %convert_element_type.131) | copy-start | bytes 12292
  48.7 81.7 %copy-start.30 = (f32[8,1,128]{2,1,0:T(1,128)}, f32[8,1,128]{2,1,0:T(1,128)S(1)}, u32[]{:S(2)}) copy-start(f32[8,1,128]{2,1,0:T(1,128)S(1)} %convert_element_type.132) | copy-start | bytes 12292
  58.5 155.5 %copy-start.3 = (f32[256,32]{0,1:T(8,128)}, f32[256,32]{0,1:T(8,128)S(1)}, u32[]{:S(2)}) copy-start(f32[256,32]{0,1:T(8,128)S(1)} %get-tuple-element.72) | copy-start | bytes 98308
  265.1 30.3 %copy-start.5 = (f32[16,16,256]{2,1,0:T(8,128)}, f32[16,16,256]{2,1,0:T(8,128)S(1)}, u32[]{:S(2)}) copy-start(f32[16,16,256]{2,1,0:T(8,128)S(1)} %get-tuple-element.75) | copy-start | bytes 786436
  265.1 30.3 %copy-start.34 = (f32[8,1,128]{2,1,0:T(1,128)S(1)}, f32[8,1,128]{2,1,0:T(1,128)}, u32[]{:S(2)}) copy-start(f32[8,1,128]{2,1,0:T(1,128)} %convert_element_type.134) | copy-start | bytes 12292
  313.6 7.1 copy-start.21
  313.6 7.1 copy-start.22
  313.6 7.2 copy-start.32
  313.6 78.6 %copy-start.9 = (f32[16,256]{1,0:T(8,128)}, f32[16,256]{1,0:T(8,128)S(1)}, u32[]{:S(2)}) copy-start(f32[16,256]{1,0:T(8,128)S(1)} %broadcast_multiply_fusion.4) | copy-start | bytes 49156
  320.7 71.5 %copy-start.18 = (f32[16,256]{1,0:T(8,128)}, f32[16,256]{1,0:T(8,128)S(1)}, u32[]{:S(2)}) copy-start(f32[16,256]{1,0:T(8,128)S(1)} %add_rsqrt_fusion) | copy-start | bytes 49156
  549.4 85.9 %copy-start.10 = (f32[16,256]{1,0:T(8,128)S(1)}, f32[16,256]{1,0:T(8,128)}, u32[]{:S(2)}) copy-start(f32[16,256]{1,0:T(8,128)} %copy-done.9) | copy-start | bytes 49156
  549.4 85.9 %copy-start.19 = (f32[16,256]{1,0:T(8,128)S(1)}, f32[16,256]{1,0:T(8,128)}, u32[]{:S(2)}) copy-start(f32[16,256]{1,0:T(8,128)} %copy-done.18) | copy-start | bytes 49156
  549.4 85.9 %copy-start.23 = (f32[8,1,128]{2,1,0:T(1,128)S(1)}, f32[8,1,128]{2,1,0:T(1,128)}, u32[]{:S(2)}) copy-start(f32[8,1,128]{2,1,0:T(1,128)} %convert_element_type.135) | copy-start | bytes 12292
  635.3 47.4 %copy-start.2 = (bf16[16,256,1024]{2,1,0:T(8,128)(2,1)S(1)}, bf16[16,256,1024]{2,1,0:T(8,128)(2,1)}, u32[]{:S(2)}) copy-start(bf16[16,256,1024]{2,1,0:T(8,128)(2,1)} %param.16) | copy-start | bytes 25165828
  682.7 18.7 %copy-start.45 = (bf16[1024,1024]{1,0:T(8,128)(2,1)S(1)}, bf16[1024,1024]{1,0:T(8,128)(2,1)}, u32[]{:S(2)}) copy-start(bf16[1024,1024]{1,0:T(8,128)(2,1)} %all-gather.15.cloned.1.call-done) | copy-start | bytes 6291460
  718.5 12.3 copy-start.6
  909.5 16.2 %copy-start.4 = (f32[256,32]{0,1:T(8,128)S(1)}, f32[256,32]{0,1:T(8,128)}, u32[]{:S(2)}) copy-start(f32[256,32]{0,1:T(8,128)} %copy-done.3) | copy-start | bytes 98308
  909.5 16.2 %copy-start.12 = (f32[256,32]{0,1:T(8,128)S(1)}, f32[256,32]{0,1:T(8,128)}, u32[]{:S(2)}) copy-start(f32[256,32]{0,1:T(8,128)} %get-tuple-element.70) | copy-start | bytes 98308
  925.6 317.6 %reduce-scatter.8.cloned.1.call-start = ((), (), s32[]{:S(2)}) async-start(), calls=%async_computation.10 | async-start | bytes 14155776 | tf_op jit(solution)/shard_map/reduce_scatter | solution.py:125
  986.3 20.9 %copy-start.8 = (f32[16,256]{1,0:T(8,128)S(1)}, f32[16,256]{1,0:T(8,128)}, u32[]{:S(2)}) copy-start(f32[16,256]{1,0:T(8,128)} %copy-done.7) | copy-start | bytes 49156
  986.3 20.9 %copy-start.17 = (f32[16,256]{1,0:T(8,128)S(1)}, f32[16,256]{1,0:T(8,128)}, u32[]{:S(2)}) copy-start(f32[16,256]{1,0:T(8,128)} %copy-done.16) | copy-start | bytes 49156
  986.3 20.9 %copy-start.29 = (f32[8,1,128]{2,1,0:T(1,128)S(1)}, f32[8,1,128]{2,1,0:T(1,128)}, u32[]{:S(2)}) copy-start(f32[8,1,128]{2,1,0:T(1,128)} %copy-done.28) | copy-start | bytes 12292
  986.3 20.9 %copy-start.31 = (f32[8,1,128]{2,1,0:T(1,128)S(1)}, f32[8,1,128]{2,1,0:T(1,128)}, u32[]{:S(2)}) copy-start(f32[8,1,128]{2,1,0:T(1,128)} %copy-done.30) | copy-start | bytes 12292
  998.9 8.3 copy-start.1
  1007.2 35.5 %copy-start.11 = (f32[16,256]{1,0:T(8,128)S(1)}, f32[16,256]{1,0:T(8,128)}, u32[]{:S(2)}) copy-start(f32[16,256]{1,0:T(8,128)} %copy-done.9) | copy-start | bytes 49156
  1007.2 35.5 %copy-start.20 = (f32[16,256]{1,0:T(8,128)S(1)}, f32[16,256]{1,0:T(8,128)}, u32[]{:S(2)}) copy-start(f32[16,256]{1,0:T(8,128)} %copy-done.18) | copy-start | bytes 49156
  1007.2 35.5 %copy-start.24 = (f32[8,1,128]{2,1,0:T(1,128)S(1)}, f32[8,1,128]{2,1,0:T(1,128)}, u32[]{:S(2)}) copy-start(f32[8,1,128]{2,1,0:T(1,128)} %convert_element_type.135) | copy-start | bytes 12292
  1007.2 35.5 %copy-start.33 = (f32[8,1,128]{2,1,0:T(1,128)S(1)}, f32[8,1,128]{2,1,0:T(1,128)}, u32[]{:S(2)}) copy-start(f32[8,1,128]{2,1,0:T(1,128)} %convert_element_type.136) | copy-start | bytes 12292
  1042.7 200.6 %reduce-scatter.12.cloned.1.call-start = ((), (), s32[]{:S(2)}) async-start(), calls=%async_computation.12 | async-start | bytes 18874368 | tf_op jit(solution)/shard_map/reduce_scatter | solution.py:125
  1091.6 264.2 %reduce-scatter.14.cloned.1.call-start = ((), (), s32[]{:S(2)}) async-start(), calls=%async_computation.13 | async-start | bytes 18874368 | tf_op jit(solution)/shard_map/reduce_scatter | solution.py:125
  1135.4 0.7 copy-start.46
  1135.4 3.2 copy-start.44
  1135.4 264.0 %reduce-scatter.6.cloned.1.call-start = ((), (), s32[]{:S(2)}) async-start(), calls=%async_computation.9 | async-start | bytes 184320 | tf_op jit(solution)/shard_map/reduce_scatter | solution.py:124
  1146.3 38.9 %copy-start.13 = (s32[16,256]{1,0:T(8,128)S(1)}, s32[16,256]{1,0:T(8,128)}, u32[]{:S(2)}) copy-start(s32[16,256]{1,0:T(8,128)} %param.15) | copy-start | bytes 49156
  1146.3 38.9 %copy-start.15 = (f32[16,256]{1,0:T(8,128)S(1)}, f32[16,256]{1,0:T(8,128)}, u32[]{:S(2)}) copy-start(f32[16,256]{1,0:T(8,128)} %copy-done.14) | copy-start | bytes 49156
  1200.9 16.0 %copy-start.25 = (f32[1024]{0:T(1024)S(1)}, f32[1024]{0:T(1024)}, u32[]{:S(2)}) copy-start(f32[1024]{0:T(1024)} %get-tuple-element.45) | copy-start | bytes 12292
  1200.9 16.0 %copy-start.26 = (f32[1024]{0:T(1024)S(1)}, f32[1024]{0:T(1024)}, u32[]{:S(2)}) copy-start(f32[1024]{0:T(1024)} %get-tuple-element.63) | copy-start | bytes 12292
  1201.0 16.0 %copy-start.27 = (f32[4096]{0:T(1024)S(1)}, f32[4096]{0:T(1024)}, u32[]{:S(2)}) copy-start(f32[4096]{0:T(1024)} %get-tuple-element.84) | copy-start | bytes 49156
  1201.0 16.0 %copy-start.35 = (f32[1024]{0:T(1024)S(1)}, f32[1024]{0:T(1024)}, u32[]{:S(2)}) copy-start(f32[1024]{0:T(1024)} %get-tuple-element.16) | copy-start | bytes 12292
  1201.0 16.0 %copy-start.36 = (f32[1024]{0:T(1024)S(1)}, f32[1024]{0:T(1024)}, u32[]{:S(2)}) copy-start(f32[1024]{0:T(1024)} %get-tuple-element.22) | copy-start | bytes 12292
  1201.0 337.0 %all-reduce.13.cloned.1.call-start = ((), (), s32[]{:S(2)}) async-start(), calls=%async_computation.14 | async-start | bytes 12582912 | tf_op jit(solution)/shard_map/psum | solution.py:125
Sparse Core Ops, SparseCore 0:
  9.9 44.3 all-gather.12
  56.2 23.8 all-gather.14
  81.9 50.1 all-gather.16
  133.8 50.1 all-gather.18
  925.8 45.2 reduce-scatter.9
  1042.8 85.2 reduce-scatter.7
  1131.6 110.8 reduce-scatter.11
  1246.1 109.6 reduce-scatter.13
  1359.4 25.9 reduce-scatter.5
  1388.0 149.9 all-reduce.12
where the time goes:
time: 1560 us
  matrix products  710 us (46%)
  other arithmetic  355 us (23%)
  waiting for transfers between devices  244 us (16%)
  local copies, waits for them, and re-layouts  116 us (7%)
  blocking collectives  114 us (7%)
  between operations  17 us (1%)
    dot_general x19, matrix products, f32_einsum(): return jnp.einsum(form, lhs, rhs, preferred_element_type=jnp.float32)  678 us
    convert_element_type x1, other arithmetic, layer_step(): act_b16 = hidden_act.astype(jnp.bfloat16)  157 us
    psum x1, waiting for transfers between devices, local_step(): lax.psum(lax.psum_scatter(full_grad, 'fsdp', scatter_dimension=0, tiled=T...  128 us
    reduce_scatter x4, waiting for transfers between devices, local_step(): lax.psum_scatter(full_grad, 'fsdp', scatter_dimension=0, tiled=True)  113 us
    all_gather x8, blocking collectives, local_step(): lax.all_gather(shard, 'fsdp', axis=0, tiled=True)  67.4 us
    convert_element_type x1, other arithmetic, layer_step(): d_scores = d_scores.astype(jnp.bfloat16)  52.8 us
    add x1, local copies, waits for them, and re-layouts, layer_step(): f32_einsum('bld,de->ble', h_one, w_qkv) + b_qkv.astype(jnp.float32)  48.8 us
    sub x1, matrix products, layer_step(): attn_prob = jax.nn.softmax(scores, axis=-1)  32 us
  transfers between devices with their start and end apart: 10, of which 2 were waited for; matrix products, arithmetic and copies ran while one was open for 50% of the time, Pallas kernels for 0%

commit v1 on v0

v1 whole, which is shorter than its diff:
```python
import functools
import jax
import jax.numpy as jnp
from jax import lax
from jax.experimental import pallas as pl
from jax.experimental.pallas import tpu as pltpu
from jax.sharding import PartitionSpec as P

HEAD_DIM = 64
HALF = 32
MASK_ID = 32
PAD_ID = 1
TAB = 32
MASK_RATIO = 0.15 * 0.8
LN_EPS = 1e-5
ROPE_BASE = 10000.0
F32 = jnp.float32
BF16 = jnp.bfloat16
NEG = -1e30
MIB = 1024 * 1024


def dot(lhs, rhs, lhs_dim=1, rhs_dim=0):
    return lax.dot_general(lhs, rhs, (((lhs_dim,), (rhs_dim,)), ((), ())), preferred_element_type=F32)


def split_two(val):
    high = val.astype(BF16)
    return high, (val - high.astype(F32)).astype(BF16)


def one_hot_t(tok_row, rows):
    index = lax.broadcasted_iota(jnp.int32, (rows, tok_row.shape[1]), 0) & (TAB - 1)
    return jnp.where(index == tok_row, 1.0, 0.0).astype(BF16)


def attn_fwd_kernel(len_ref, tok_ref, tab_ref, cos_ref, sin_ref, qkv_ref, ctx_ref, lse_ref, s_a, s_b, p_a, p_b):
    model = ctx_ref.shape[1]
    seq = ctx_ref.shape[0]
    split = seq // 2
    pairs = model // 128
    length = len_ref[pl.program_id(0)]
    hot = one_hot_t(tok_ref[0], 3 * TAB)
    cos_tab, sin_tab = cos_ref[...], sin_ref[...]
    wide = 256

    def expand(step, carry):
        offset = pl.multiple_of(step * wide, wide)
        part = tab_ref[0, :, pl.ds(offset, wide)]
        high = part.astype(BF16)
        rest = part - high.astype(F32)
        mid = rest.astype(BF16)
        low = (rest - mid.astype(F32)).astype(BF16)
        raw = dot(jnp.concatenate([high, mid, low], axis=0), hot, 0, 0)
        for head in range(wide // HEAD_DIM):
            low_half = raw[head * HEAD_DIM:head * HEAD_DIM + HALF]
            high_half = raw[head * HEAD_DIM + HALF:(head + 1) * HEAD_DIM]
            turned = jnp.concatenate([low_half * cos_tab - high_half * sin_tab,
                                      high_half * cos_tab + low_half * sin_tab], axis=0).astype(BF16)
            qkv_ref[0, pl.ds(pl.multiple_of(offset + head * HEAD_DIM, HEAD_DIM), HEAD_DIM), :] = turned
        return carry

    def expand_v(step, carry):
        offset = pl.multiple_of(2 * model + step * wide, wide)
        part = tab_ref[0, :, pl.ds(offset, wide)].astype(BF16)
        qkv_ref[0, pl.ds(offset, wide), :] = dot(part, hot[:TAB], 0, 0).astype(BF16)
        return carry

    lax.fori_loop(0, 2 * model // wide, expand, 0, unroll=4)
    lax.fori_loop(0, model // wide, expand_v, 0, unroll=4)

    def head_rows(part, step, sub):
        return pl.ds(pl.multiple_of(part * model + step * 128 + sub * HEAD_DIM, HEAD_DIM), HEAD_DIM)

    def score(dst, step):
        for sub in range(2):
            dst[sub] = dot(qkv_ref[0, head_rows(1, step, sub), :], qkv_ref[0, head_rows(0, step, sub), :], 0, 0)

    def soften(src, dst, step):
        key_ok = lax.broadcasted_iota(jnp.int32, (seq - split, seq), 0) + split < length
        for sub in range(2):
            first = src[sub, :split]
            last = jnp.where(key_ok, src[sub, split:], NEG)
            top = jnp.maximum(jnp.max(first, axis=0, keepdims=True), jnp.max(last, axis=0, keepdims=True))
            first, last = jnp.exp(first - top), jnp.exp(last - top)
            total = jnp.sum(first, axis=0, keepdims=True) + jnp.sum(last, axis=0, keepdims=True)
            inverse = 1.0 / total
            dst[sub, :split] = (first * inverse).astype(BF16)
            dst[sub, split:] = (last * inverse).astype(BF16)
            lse_ref[0, pl.ds(2 * step + sub, 1), :] = top + jnp.log(total)

    def context(src, step):
        outs = [dot(qkv_ref[0, head_rows(2, step, sub), :], src[sub]) for sub in range(2)]
        ctx_ref[:, pl.ds(pl.multiple_of(step * 128, 128), 128)] = jnp.concatenate(outs, axis=0).T.astype(BF16)

    score(s_a, 0)

    def two_pairs(step, carry):
        even = 2 * step
        score(s_b, even + 1)
        context(p_b, (even + pairs - 1) & (pairs - 1))
        soften(s_a, p_a, even)
        score(s_a, (even + 2) & (pairs - 1))
        context(p_a, even)
        soften(s_b, p_b, even + 1)
        return carry

    lax.fori_loop(0, pairs // 2, two_pairs, 0)
    context(p_b, pairs - 1)


def attn_bwd_kernel(len_ref, tok_ref, qkv_ref, lse_ref, dctx_ref, cos_ref, sin_ref, high_ref, low_ref, bias_ref,
                    s_a, s_b, d_a, d_b, p_a, p_b, g_a, g_b, dct):
    model = dctx_ref.shape[1]
    seq = dctx_ref.shape[0]
    split = seq // 2
    pairs = model // 128
    length = len_ref[pl.program_id(0)]
    hot = one_hot_t(tok_ref[0], TAB)
    cos_tab, sin_tab = cos_ref[...], sin_ref[...]

    @pl.when(pl.program_id(0) == 0)
    def _():
        bias_ref[...] = jnp.zeros_like(bias_ref)
        p_b[...] = jnp.zeros_like(p_b)
        g_b[...] = jnp.zeros_like(g_b)

    def flip(step, carry):
        offset = pl.multiple_of(step * 128, 128)
        dct[pl.ds(offset, 128), :] = dctx_ref[:, pl.ds(offset, 128)].T
        return carry

    lax.fori_loop(0, pairs, flip, 0, unroll=4)

    def head_rows(part, step, sub):
        return pl.ds(pl.multiple_of(part * model + step * 128 + sub * HEAD_DIM, HEAD_DIM), HEAD_DIM)

    def unrope(val):
        low, high = val[:HALF], val[HALF:]
        return jnp.concatenate([low * cos_tab + high * sin_tab, high * cos_tab - low * sin_tab], axis=0)

    def put(offset, grad, fresh):
        offset = pl.multiple_of(offset, 128)
        folded = grad[:, :128]
        for lane in range(128, seq, 128):
            folded += grad[:, lane:lane + 128]
        bias_ref[pl.ds(offset, 128), :] += folded * fresh
        sums = dot(hot, grad.astype(BF16), 1, 1)
        high, low = split_two(sums)
        high_ref[0, :, pl.ds(offset, 128)] = high
        low_ref[0, :, pl.ds(offset, 128)] = low

    def score(dst_s, dst_d, step):
        for sub in range(2):
            dst_s[sub] = dot(qkv_ref[0, head_rows(1, step, sub), :], qkv_ref[0, head_rows(0, step, sub), :], 0, 0)
            dst_d[sub] = dot(qkv_ref[0, head_rows(2, step, sub), :], dct[head_rows(0, step, sub), :], 0, 0)

    def soften(src_s, src_d, dst_p, dst_g, step):
        key_ok = lax.broadcasted_iota(jnp.int32, (seq - split, seq), 0) + split < length
        for sub in range(2):
            lse = lse_ref[0, pl.ds(2 * step + sub, 1), :]
            first = jnp.exp(src_s[sub, :split] - lse)
            last = jnp.exp(jnp.where(key_ok, src_s[sub, split:], NEG) - lse)
            dst_p[sub, :split] = first.astype(BF16)
            dst_p[sub, split:] = last.astype(BF16)
            d_first, d_last = src_d[sub, :split], src_d[sub, split:]
            delta = jnp.sum(d_first * first, axis=0, keepdims=True) + jnp.sum(d_last * last, axis=0, keepdims=True)
            dst_g[sub, :split] = (first * (d_first - delta)).astype(BF16)
            dst_g[sub, split:] = (last * (d_last - delta)).astype(BF16)

    def grads(src_p, src_g, step, fresh):
        dq, dk, dv = [], [], []
        for sub in range(2):
            dv.append(dot(dct[head_rows(0, step, sub), :], src_p[sub], 1, 1))
            dq.append(unrope(dot(qkv_ref[0, head_rows(1, step, sub), :], src_g[sub])) * (HEAD_DIM ** -0.5))
            dk.append(unrope(dot(qkv_ref[0, head_rows(0, step, sub), :], src_g[sub], 1, 1)))
        put(step * 128, jnp.concatenate(dq, axis=0), fresh)
        put(model + step * 128, jnp.concatenate(dk, axis=0), fresh)
        put(2 * model + step * 128, jnp.concatenate(dv, axis=0), fresh)

    score(s_a, d_a, 0)

    def two_pairs(step, carry):
        even = 2 * step
        score(s_b, d_b, even + 1)
        grads(p_b, g_b, (even + pairs - 1) & (pairs - 1), jnp.where(step == 0, 0.0, 1.0))
        soften(s_a, d_a, p_a, g_a, even)
        score(s_a, d_a, (even + 2) & (pairs - 1))
        grads(p_a, g_a, even, 1.0)
        soften(s_b, d_b, p_b, g_b, even + 1)
        return carry

    lax.fori_loop(0, pairs // 2, two_pairs, 0)
    grads(p_b, g_b, pairs - 1, 1.0)


def fold_rows(val):
    return jnp.sum(val.reshape(val.shape[0] // 8, 8, val.shape[1]), axis=0)


def row_stats(val):
    centered = val - jnp.mean(val, axis=-1, keepdims=True)
    inv_std = lax.rsqrt(jnp.mean(centered * centered, axis=-1, keepdims=True) + LN_EPS)
    return centered * inv_std, inv_std


def mid_kernel(tok_ref, ctx_ref, w_ref, tab_ref, bias_ref, gain_ref, shift_ref, xmid_ref, h_ref):
    seq = tok_ref.shape[2]
    for part in range(tok_ref.shape[0]):
        rows = slice(part * seq, (part + 1) * seq)
        hot = one_hot_t(tok_ref[part], TAB)
        x_in = dot(hot, tab_ref[part], 0, 0)
        x_mid = x_in + dot(ctx_ref[rows, :], w_ref[...]) + bias_ref[...]
        xmid_ref[rows, :] = x_mid
        x_hat, _ = row_stats(x_mid)
        h_ref[rows, :] = (x_hat * gain_ref[...] + shift_ref[...]).astype(BF16)


def mlp_kernel(h_ref, dy_ref, w1_ref, w2_ref, b1_ref, act_ref, dpre_ref, gb_ref):
    width = act_ref.shape[1]
    tile = 256

    @pl.when(pl.program_id(1) == 0)
    def _():
        gb_ref[...] = jnp.zeros_like(gb_ref)

    for start in range(0, width, tile):
        cols = slice(start, start + tile)
        pre = dot(h_ref[...], w1_ref[:, cols]) + b1_ref[:, cols]
        d_act = dot(dy_ref[...], w2_ref[cols, :], 1, 1)
        phi = 0.5 + 0.5 * lax.erf(pre * (2.0 ** -0.5))
        act_ref[:, cols] = (pre * phi).astype(BF16)
        slope = phi + pre * (jnp.exp(pre * pre * -0.5) * 0.3989422804014327)
        d_pre = d_act * slope
        gb_ref[:, cols] += fold_rows(d_pre)
        dpre_ref[:, cols] = d_pre.astype(BF16)


def back_kernel(tok_ref, dpre_ref, w1_ref, xmid_ref, dy_ref, wout_ref, gain_ref,
                dmid_ref, dctx_ref, seg_ref, ggain_ref, gshift_ref, gbout_ref, gbfc2_ref):
    seq = tok_ref.shape[2]

    @pl.when(pl.program_id(0) == 0)
    def _():
        for ref in (ggain_ref, gshift_ref, gbout_ref, gbfc2_ref):
            ref[...] = jnp.zeros_like(ref)

    for part in range(tok_ref.shape[0]):
        rows = slice(part * seq, (part + 1) * seq)
        d_two = dot(dpre_ref[rows, :], w1_ref[...], 1, 1)
        x_hat, inv_std = row_stats(xmid_ref[rows, :])
        grad_y = dy_ref[rows, :].astype(F32)
        d_hat = d_two * gain_ref[...]
        d_x = inv_std * (d_hat - jnp.mean(d_hat, axis=-1, keepdims=True)
                         - x_hat * jnp.mean(d_hat * x_hat, axis=-1, keepdims=True))
        d_mid = grad_y + d_x
        ggain_ref[...] += fold_rows(d_two * x_hat)
        gshift_ref[...] += fold_rows(d_two)
        gbout_ref[...] += fold_rows(d_mid)
        gbfc2_ref[...] += fold_rows(grad_y)
        high, low = split_two(d_mid)
        dmid_ref[rows, :] = high
        hot = one_hot_t(tok_ref[part], TAB)
        seg_ref[part] = dot(hot, high) + dot(hot, low)
        dctx_ref[rows, :] = dot(high, wout_ref[...], 1, 1).astype(BF16)


def whole(shape):
    return pl.BlockSpec(shape, lambda *_: (0,) * len(shape), pipeline_mode=pl.Buffered(1))


def cost(flops, nbytes):
    return pl.CostEstimate(flops=int(flops), bytes_accessed=int(nbytes), transcendentals=0)


def params(dims, limit=56):
    return pltpu.CompilerParams(dimension_semantics=dims, vmem_limit_bytes=limit * MIB)


def run_attn_fwd(lengths, tok_rows, tab, cos_tab, sin_tab, seq, model):
    batch = tok_rows.shape[0]
    heads = model // HEAD_DIM
    return pl.pallas_call(
        attn_fwd_kernel, grid=(batch,), name='attn_fwd',
        in_specs=[pl.BlockSpec(memory_space=pltpu.SMEM),
                  pl.BlockSpec((1, 1, seq), lambda b: (b, 0, 0)),
                  pl.BlockSpec((1, TAB, 3 * model), lambda b: (b, 0, 0)),
                  whole((HALF, seq)), whole((HALF, seq))],
        out_specs=[pl.BlockSpec((1, 3 * model, seq), lambda b: (b, 0, 0)),
                   pl.BlockSpec((seq, model), lambda b: (b, 0)),
                   pl.BlockSpec((1, heads, seq), lambda b: (b, 0, 0))],
        out_shape=[jax.ShapeDtypeStruct((batch, 3 * model, seq), BF16),
                   jax.ShapeDtypeStruct((batch * seq, model), BF16),
                   jax.ShapeDtypeStruct((batch, heads, seq), F32)],
        scratch_shapes=[pltpu.VMEM((2, seq, seq), F32)] * 2 + [pltpu.VMEM((2, seq, seq), BF16)] * 2,
        cost_estimate=cost(60e9 * 0.75, 60e6),
        compiler_params=params(('arbitrary',)))(lengths, tok_rows, tab, cos_tab, sin_tab)


def run_attn_bwd(lengths, tok_rows, qkv_t, lse, d_ctx, cos_tab, sin_tab, seq, model):
    batch = tok_rows.shape[0]
    heads = model // HEAD_DIM
    return pl.pallas_call(
        attn_bwd_kernel, grid=(batch,), name='attn_bwd',
        in_specs=[pl.BlockSpec(memory_space=pltpu.SMEM),
                  pl.BlockSpec((1, 1, seq), lambda b: (b, 0, 0)),
                  pl.BlockSpec((1, 3 * model, seq), lambda b: (b, 0, 0)),
                  pl.BlockSpec((1, heads, seq), lambda b: (b, 0, 0)),
                  pl.BlockSpec((seq, model), lambda b: (b, 0)),
                  whole((HALF, seq)), whole((HALF, seq))],
        out_specs=[pl.BlockSpec((1, TAB, 3 * model), lambda b: (b, 0, 0)),
                   pl.BlockSpec((1, TAB, 3 * model), lambda b: (b, 0, 0)),
                   pl.BlockSpec((3 * model, 128), lambda b: (0, 0))],
        out_shape=[jax.ShapeDtypeStruct((batch, TAB, 3 * model), BF16),
                   jax.ShapeDtypeStruct((batch, TAB, 3 * model), BF16),
                   jax.ShapeDtypeStruct((3 * model, 128), F32)],
        scratch_shapes=[pltpu.VMEM((2, seq, seq), F32)] * 4 + [pltpu.VMEM((2, seq, seq), BF16)] * 4
        + [pltpu.VMEM((model, seq), BF16)],
        cost_estimate=cost(110e9 * 0.75, 60e6),
        compiler_params=params(('arbitrary',)))(lengths, tok_rows, qkv_t, lse, d_ctx, cos_tab, sin_tab)


def run_mid(tok_rows, ctx, w_out, x_tab, b_out, gain, shift, seq, model):
    batch = tok_rows.shape[0]
    rows = batch * seq
    group = 2
    tile = group * seq
    return pl.pallas_call(
        mid_kernel, grid=(batch // group,), name='mid',
        in_specs=[pl.BlockSpec((group, 1, seq), lambda b: (b, 0, 0)),
                  pl.BlockSpec((tile, model), lambda b: (b, 0)),
                  whole((model, model)),
                  pl.BlockSpec((group, TAB, model), lambda b: (b, 0, 0)),
                  whole((1, model)), whole((1, model)), whole((1, model))],
        out_specs=[pl.BlockSpec((tile, model), lambda b: (b, 0)),
                   pl.BlockSpec((tile, model), lambda b: (b, 0))],
        out_shape=[jax.ShapeDtypeStruct((rows, model), F32), jax.ShapeDtypeStruct((rows, model), BF16)],
        cost_estimate=cost(2 * rows * model * model, rows * model * 8),
        compiler_params=params(('arbitrary',)))(tok_rows, ctx, w_out, x_tab, b_out, gain, shift)


def run_mlp(h_two, grad_y, w_fc1, w_fc2, b_fc1):
    rows, model = h_two.shape
    width = w_fc1.shape[1]
    tile, cols = 512, 1024
    return pl.pallas_call(
        mlp_kernel, grid=(width // cols, rows // tile), name='mlp',
        in_specs=[pl.BlockSpec((tile, model), lambda f, r: (r, 0)),
                  pl.BlockSpec((tile, model), lambda f, r: (r, 0)),
                  pl.BlockSpec((model, cols), lambda f, r: (0, f)),
                  pl.BlockSpec((cols, model), lambda f, r: (f, 0)),
                  pl.BlockSpec((1, cols), lambda f, r: (0, f))],
        out_specs=[pl.BlockSpec((tile, cols), lambda f, r: (r, f)),
                   pl.BlockSpec((tile, cols), lambda f, r: (r, f)),
                   pl.BlockSpec((8, cols), lambda f, r: (0, f))],
        out_shape=[jax.ShapeDtypeStruct((rows, width), BF16), jax.ShapeDtypeStruct((rows, width), BF16),
                   jax.ShapeDtypeStruct((8, width), F32)],
        cost_estimate=cost(4 * rows * model * width, 134e6),
        compiler_params=params(('arbitrary', 'arbitrary')))(h_two, grad_y, w_fc1, w_fc2, b_fc1)


def run_back(tok_rows, d_pre, w_fc1, x_mid, grad_y, w_out, gain, seq, model):
    batch = tok_rows.shape[0]
    rows, width = d_pre.shape
    group = 2
    tile = group * seq
    vec = jax.ShapeDtypeStruct((8, model), F32)
    vec_spec = pl.BlockSpec((8, model), lambda b: (0, 0))
    row_spec = pl.BlockSpec((tile, model), lambda b: (b, 0))
    return pl.pallas_call(
        back_kernel, grid=(batch // group,), name='back',
        in_specs=[pl.BlockSpec((group, 1, seq), lambda b: (b, 0, 0)),
                  pl.BlockSpec((tile, width), lambda b: (b, 0)),
                  whole((model, width)), row_spec, row_spec, whole((model, model)), whole((1, model))],
        out_specs=[row_spec, row_spec, pl.BlockSpec((group, TAB, model), lambda b: (b, 0, 0)),
                   vec_spec, vec_spec, vec_spec, vec_spec],
        out_shape=[jax.ShapeDtypeStruct((rows, model), BF16), jax.ShapeDtypeStruct((rows, model), BF16),
                   jax.ShapeDtypeStruct((batch, TAB, model), F32), vec, vec, vec, vec],
        cost_estimate=cost(2 * rows * model * (width + model), 90e6),
        compiler_params=params(('arbitrary',)))(tok_rows, d_pre, w_fc1, x_mid, grad_y, w_out, gain)


def solution(mesh):
    row_spec = P(('dp', 'fsdp'), None)
    act_spec = P(('dp', 'fsdp'), None, None)
    param_specs = (P(None, 'fsdp'),) + (P('fsdp'),) * 12
    swap = [(0, 1), (1, 0)]

    def local_step(tokens, grad_y3, *shards):
        (e_part, gain1_part, shift1_part, wqkv_part, bqkv_part, wout_part, bout_part,
         gain2_part, shift2_part, wfc1_part, bfc1_part, wfc2_part, bfc2_part) = shards
        batch, seq = tokens.shape
        vocab = e_part.shape[0]
        model = grad_y3.shape[2]

        def gather(part):
            return lax.all_gather(part, 'fsdp', axis=0, tiled=True)

        smalls = (gain1_part, shift1_part, bout_part, gain2_part, shift2_part, bfc2_part, bqkv_part, bfc1_part)
        packed = jnp.concatenate([e_part] + [part.reshape(-1, 128) for part in smalls], axis=0)
        packed = lax.all_gather(packed, 'fsdp', axis=0, tiled=False)
        w_qkv, w_out, w_fc1, w_fc2 = (gather(part) for part in (wqkv_part, wout_part, wfc1_part, wfc2_part))
        table = packed[:, :vocab].transpose(1, 0, 2).reshape(vocab, model)[:TAB]
        vecs, at = [], vocab
        for part in smalls:
            count = part.shape[0] // 128
            vecs.append(packed[:, at:at + count].reshape(1, -1).astype(F32))
            at += count
        gain1, shift1, b_out, gain2, shift2, b_fc2, b_qkv, b_fc1 = vecs
        grad_y = grad_y3.reshape(batch * seq, model)

        is_mask, is_pad = tokens == MASK_ID, tokens == PAD_ID
        lengths = jnp.sum(jnp.logical_not(is_pad), axis=1).astype(jnp.int32)
        factor = (1.0 - MASK_RATIO) / (1.0 - jnp.sum(is_mask, axis=1).astype(F32) / lengths.astype(F32))
        tok_rows = jnp.where(is_mask, PAD_ID, tokens)[:, None, :]
        keep = jnp.where(jnp.arange(TAB) == PAD_ID, 0.0, factor[:, None])[:, :, None]
        x_tab = (table.astype(F32)[None] * keep).astype(BF16)
        hat_one, inv_one = row_stats(x_tab.astype(F32))
        h_tab = (hat_one * gain1 + shift1).astype(BF16).reshape(batch * TAB, model)
        scale = jnp.where(jnp.arange(3 * model) < model, HEAD_DIM ** -0.5, 1.0)[None]
        qkv_tab = ((dot(h_tab, w_qkv) + b_qkv) * scale).reshape(batch, TAB, 3 * model)

        inv_freq = 1.0 / (ROPE_BASE ** (jnp.arange(0, HEAD_DIM, 2, dtype=F32) / HEAD_DIM))
        angles = inv_freq[:, None] * jnp.arange(seq, dtype=F32)[None, :]
        cos_tab, sin_tab = jnp.cos(angles), jnp.sin(angles)

        qkv_t, ctx, lse = run_attn_fwd(lengths, tok_rows, qkv_tab, cos_tab, sin_tab, seq, model)
        x_mid, h_two = run_mid(tok_rows, ctx, w_out, x_tab, b_out, gain2, shift2, seq, model)
        act, d_pre, gb_fc1 = run_mlp(h_two, grad_y, w_fc1, w_fc2, b_fc1)

        me = lax.axis_index('fsdp')
        spot = {1: me & 1, 2: (me >> 1) & 1, 4: me >> 2}

        def over_dp(part):
            return part + lax.ppermute(part, 'dp', swap)

        def scatter(grad):
            return lax.psum_scatter(grad, 'fsdp', scatter_dimension=0, tiled=True)

        def parts_of(val, bit, axis):
            send = lax.dynamic_index_in_dim(val, 1 - spot[bit], axis, keepdims=False)
            return send, lax.dynamic_index_in_dim(val, spot[bit], axis, keepdims=False)

        def trade(send, bit):
            return lax.ppermute(send, 'fsdp', [(dev, dev ^ bit) for dev in range(8)])

        after = lax.optimization_barrier
        raw_fc2 = dot(act, grad_y, 0, 0)
        part_fc2 = scatter(raw_fc2)
        h_two, d_pre, raw_fc2 = after((h_two, d_pre, raw_fc2))
        raw_fc1 = dot(h_two, d_pre, 0, 0)
        rows = raw_fc1.shape[0] // 8
        send, held = parts_of(raw_fc1.reshape(2, 2, 2, rows, raw_fc1.shape[1]), 1, 2)
        d_pre, send = after((d_pre, send))
        got = trade(send, 1)
        d_mid, d_ctx, seg_mid, gg2, gs2, gb_out, gb_fc2 = run_back(
            tok_rows, d_pre, w_fc1, x_mid, grad_y, w_out, gain2, seq, model)
        d_mid, got = after((d_mid, got))
        total = held + got
        send_a, held_a = parts_of(total[:, :, :rows // 2], 2, 1)
        send_b, held_b = parts_of(total[:, :, rows // 2:], 4, 0)
        d_mid, send_a, send_b = after((d_mid, send_a, send_b))
        got_a, got_b = trade(send_a, 2), trade(send_b, 4)
        raw_out = dot(ctx, d_mid, 0, 0)
        part_out = scatter(raw_out)
        d_ctx, raw_out, part_fc2 = after((d_ctx, raw_out, part_fc2))
        g_w_fc2 = over_dp(part_fc2)
        d_high, d_low, gb_qkv = run_attn_bwd(lengths, tok_rows, qkv_t, lse, d_ctx, cos_tab, sin_tab, seq, model)
        d_high, got_a, got_b, part_out, g_w_fc2 = after((d_high, got_a, got_b, part_out, g_w_fc2))
        g_w_out = over_dp(part_out)
        send_a, held_a = parts_of(held_a + got_a, 4, 0)
        send_b, held_b = parts_of(held_b + got_b, 2, 0)
        d_high, send_a, send_b = after((d_high, send_a, send_b))
        got_a, got_b = trade(send_a, 4), trade(send_b, 2)
        d_tab = jnp.concatenate([d_high, d_low], axis=0).reshape(2 * batch * TAB, 3 * model)
        raw_qkv = dot(jnp.concatenate([h_tab, h_tab], axis=0), d_tab, 0, 0)
        part_qkv = scatter(raw_qkv)
        d_tab, raw_qkv, got_a, got_b = after((d_tab, raw_qkv, got_a, got_b))
        part_fc1 = jnp.concatenate([held_a + got_a, held_b + got_b], axis=0)
        d_tab, part_fc1, act = after((d_tab, part_fc1, act))
        g_w_fc1 = over_dp(part_fc1)
        d_one = dot(d_tab, w_qkv, 1, 1).reshape(2, batch, TAB, model)
        d_one = d_one[0] + d_one[1]
        d_hat = d_one * gain1
        d_x = inv_one * (d_hat - jnp.mean(d_hat, axis=-1, keepdims=True)
                         - hat_one * jnp.mean(d_hat * hat_one, axis=-1, keepdims=True))
        g_table = jnp.sum((seg_mid + d_x) * keep, axis=0)
        g_table = jnp.concatenate([g_table, jnp.zeros((vocab - TAB, model), F32)], axis=0)
        vec_grads = (jnp.sum(d_one * hat_one, axis=(0, 1)), jnp.sum(d_one, axis=(0, 1)), jnp.sum(gb_out, axis=0),
                     jnp.sum(gg2, axis=0), jnp.sum(gs2, axis=0), jnp.sum(gb_fc2, axis=0),
                     jnp.sum(gb_qkv, axis=1), jnp.sum(gb_fc1, axis=0))
        small = jnp.concatenate(
            [g_table.reshape(vocab, 8, 128).transpose(1, 0, 2)]
            + [vec.reshape(8, -1, 128) for vec in vec_grads], axis=1)
        small = lax.psum(small, ('dp', 'fsdp'))
        small = lax.dynamic_index_in_dim(small, me, 0, keepdims=False)
        g_small, at = [], vocab
        for part in smalls:
            count = part.shape[0] // 128
            g_small.append(small[at:at + count].reshape(-1))
            at += count
        gg1, gs1, gbo, ggn2, gsh2, gb2, gbq, gb1 = g_small
        hidden = (x_mid + dot(act, w_fc2) + b_fc2).astype(BF16)
        hidden, part_qkv = after((hidden, part_qkv))
        g_w_qkv = over_dp(part_qkv)
        hidden = hidden.reshape(grad_y3.shape)
        return (hidden, small[:vocab], gg1, gs1, g_w_qkv, gbq, g_w_out, gbo, ggn2, gsh2, g_w_fc1, gb1, g_w_fc2, gb2)

    return jax.shard_map(local_step, mesh=mesh, in_specs=(row_spec, act_spec) + param_specs,
                         out_specs=(act_spec,) + param_specs, check_vma=False)
```

time: 1560 us -> 791 us (0.51)
  matrix products: 710 us -> 171 us
  Pallas kernels: 0 us -> 341 us
  other arithmetic: 355 us -> 42.6 us
  blocking collectives: 114 us -> 11 us
  waiting for transfers between devices: 244 us -> 159 us
  local copies, waits for them, and re-layouts: 116 us -> 34.4 us
    dot_general x19 -> x7, matrix products: 678 us -> 171 us  [dot(): lax.dot_general(lhs, rhs, (((lhs_dim,), (rhs_dim,)), ((), ())), preferred...]
    pallas_call x0 -> x5, Pallas kernels: none -> 341 us  [the longest x1 102 us: run_mlp(): pl.pallas_call(mlp_kernel, grid=(width // cols, rows // tile), name='mlp'...]
    convert_element_type x11 -> x6, other arithmetic: 237 us -> 3.17 us  [the longest x2 1.36 us: local_step(): x_tab = (table.astype(F32)[None] * keep).astype(BF16)]
    reduce_scatter x5 -> x3, waiting for transfers between devices: 113 us -> 0.05 us  [scatter(): return lax.psum_scatter(grad, 'fsdp', scatter_dimension=0, tiled=True)]
    all_gather x4, waiting for transfers between devices: 0.05 us -> 71.2 us  [gather(): return lax.all_gather(part, 'fsdp', axis=0, tiled=True)]
    all_gather x9 -> x1, blocking collectives: 78.2 us -> 11 us  [local_step(): packed = lax.all_gather(packed, 'fsdp', axis=0, tiled=False)]
    psum x1, waiting for transfers between devices: 128 us -> 63 us  [local_step(): small = lax.psum(small, ('dp', 'fsdp'))]
    add x1 -> x0, local copies, waits for them, and re-layouts: 48.8 us -> none  [layer_step(): f32_einsum('bld,de->ble', h_one, w_qkv) + b_qkv.astype(jnp.float32)]
  transfers between devices with their start and end apart: 10 -> 17, of which waited for: 2 -> 5; matrix products, arithmetic and copies ran while one was open for 50% -> 21% of each run, Pallas kernels for 0% -> 31%
where the time goes in v1:
time: 791 us; the launch traced here: 783 us
  Pallas kernels  341 us (43%)
  matrix products  171 us (22%)
  waiting for transfers between devices  159 us (20%)
  other arithmetic  42.6 us (5%)
  local copies, waits for them, and re-layouts  34.4 us (4%)
  between operations  15.3 us (2%)
  blocking collectives  11 us (1%)
  starting transfers between devices  8.87 us (1%)
    dot_general x7, matrix products, dot(): lax.dot_general(lhs, rhs, (((lhs_dim,), (rhs_dim,)), ((), ())), preferred...  171 us
    pallas_call x1, Pallas kernels, run_mlp(): pl.pallas_call(mlp_kernel, grid=(width // cols, rows // tile), name='mlp'...  102 us
    pallas_call x1, Pallas kernels, run_attn_bwd(): pl.pallas_call(attn_bwd_kernel, grid=(batch,), name='attn_bwd', in_specs=...  92.8 us
    all_gather x4, waiting for transfers between devices, gather(): return lax.all_gather(part, 'fsdp', axis=0, tiled=True)  71.2 us
    pallas_call x1, Pallas kernels, run_back(): pl.pallas_call(back_kernel, grid=(batch // group,), name='back', in_specs...  68.9 us
    psum x1, waiting for transfers between devices, local_step(): small = lax.psum(small, ('dp', 'fsdp'))  63 us
    pallas_call x1, Pallas kernels, run_attn_fwd(): pl.pallas_call(attn_fwd_kernel, grid=(batch,), name='attn_fwd', in_specs=...  58.2 us
    ppermute x5, waiting for transfers between devices, trade(): return lax.ppermute(send, 'fsdp', [(dev, dev ^ bit) for dev in range(8)])  22.1 us
  transfers between devices with their start and end apart: 17, of which 5 were waited for; matrix products, arithmetic and copies ran while one was open for 21% of the time, Pallas kernels for 31%

profile of v1, /device:TPU:0, one launch (start us, length us, event | category | flops | bytes accessed | tf_op | source)
XLA Modules:
  0.0 783.2 jit_solution(10692781928642122781)
XLA Ops:
  7.3 0.7 all-gather.7.cloned.1.call-update
  8.1 0.7 all-gather.9.cloned.1.call-update
  8.8 0.7 all-gather.11.cloned.1.call-update
  10.5 0.6 broadcast_in_dim.54.tok_ref
  11.4 11.0 %all-gather.1 = bf16[8,46,128]{2,1,0:T(8,128)(2,1)S(1)} all-gather(bf16[1,46,128]{2,1,0:T(8,128)(2,1)S(1)} %bitcast.134), channel_id=2, replica_groups=mesh['dp'=2,'fsdp'=8] {'fsdp'}, dimensions={0}, use_global_device_ids=true | all-gather | bytes 105984 | tf_op jit(solution)/shard_map/all_gather | solution.py:401
  22.9 1.3 multiply_convert_fusion
  24.3 0.6 slice_convert_fusion.2
  25.5 0.7 slice_convert_fusion
  26.2 0.8 fusion.15
  27.0 27.2 %all-gather.7.cloned.1.call-done = bf16[1024,3072]{1,0:T(8,128)(2,1)} async-done(((bf16[128,3072]{1,0:T(8,128)(2,1)}), bf16[1024,3072]{1,0:T(8,128)(2,1)}) %all-gather.7.cloned.1.call-update) | async-done | bytes 6291472 | tf_op jit(solution)/shard_map/all_gather | solution.py:397
  54.2 8.1 %add_multiply_fusion = f32[512,3072]{1,0:T(8,128)} fusion(bf16[512,1024]{1,0:T(8,128)(2,1)S(1)} %add_convert_fusion.1, bf16[1024,3072]{1,0:T(8,128)(2,1)} %all-gather.7.cloned.1.call-done, f32[3072]{0:T(1024)S(1)} %fusion.18, f32[3072]{0:T(1024)S(1)} %reshape.394), kind=kOutput, calls=%fused_computation.4 | convolution fusion | flops 3224371200 | bytes 13656064 | tf_op jit(solution)/shard_map/dot_general | solution.py:24
  62.3 58.2 %attn_fwd.1 = (bf16[16,3072,256]{2,1,0:T(8,128)(2,1)}, bf16[4096,1024]{1,0:T(8,128)(2,1)}, f32[16,16,256]{2,1,0:T(8,128)}) custom-call(s32[16]{0:T(128)} %copy-done.45, s32[16,1,256]{2,1,0:T(1,128)} %broadcast_in_dim.54.tok_ref, f32[16,32,3072]{2,1,0:T(8,128)} %bitcast.153, f32[32,256]{1,0:T(8,128)} %get-tuple-element.129.cos_ref, ...), custom_call_target="tpu_custom_call" | custom-call | flops 44999999488 | bytes 60000000 | tf_op jit(solution)/shard_map/attn_fwd/pallas_call | solution.py:283
  120.4 19.5 %mid.1 = (f32[4096,1024]{1,0:T(8,128)}, bf16[4096,1024]{1,0:T(8,128)(2,1)}) custom-call(s32[16,1,256]{2,1,0:T(1,128)} %broadcast_in_dim.54.tok_ref, bf16[4096,1024]{1,0:T(8,128)(2,1)} %get-tuple-element.59.ctx_ref, bf16[1024,1024]{1,0:T(8,128)(2,1)} %all-gather.9.cloned.1.call-done.w_ref.wout_ref, bf16[16,32,1024]{2,1,0:T(8,128)(2,1)} %get-tuple-element.119.tab_ref, ...), custom_call_target="tpu_custom_call" | custom-call | flops 8589934592 | bytes 33554432 | tf_op jit(solution)/shard_map/mid/pallas_call | solution.py:328
  140.0 44.0 %all-gather.13.cloned.1.call-done.w2_ref = bf16[4096,1024]{1,0:T(8,128)(2,1)} async-done(((bf16[512,1024]{1,0:T(8,128)(2,1)}), bf16[4096,1024]{1,0:T(8,128)(2,1)}) %all-gather.13.cloned.1.call-update) | async-done | bytes 8388624 | tf_op jit(solution)/shard_map/all_gather | solution.py:397
  184.0 101.6 %mlp.1 = (bf16[4096,4096]{1,0:T(8,128)(2,1)}, bf16[4096,4096]{1,0:T(8,128)(2,1)}, f32[8,4096]{1,0:T(8,128)}) custom-call(bf16[4096,1024]{1,0:T(8,128)(2,1)} %get-tuple-element.67.h_ref, bf16[4096,1024]{1,0:T(8,128)(2,1)} %bitcast.149, bf16[1024,4096]{1,0:T(8,128)(2,1)} %all-gather.11.cloned.1.call-done.w1_ref, ...), custom_call_target="tpu_custom_call" | custom-call | flops 68719476736 | bytes 134000000 | tf_op jit(solution)/shard_map/mlp/pallas_call | solution.py:346
  285.6 43.9 %fusion.31 = f32[4096,1024]{1,0:T(8,128)} fusion(bf16[4096,4096]{1,0:T(8,128)(2,1)} %get-tuple-element.90, bf16[4096,1024]{1,0:T(8,128)(2,1)} %bitcast.150), kind=kOutput, calls=%fused_computation.100 | convolution fusion | flops 34359738368 | bytes 58720256 | tf_op jit(solution)/shard_map/dot_general | solution.py:24
  329.5 43.7 %fusion.32 = f32[1024,4096]{1,0:T(8,128)S(1)} fusion(bf16[4096,1024]{1,0:T(8,128)(2,1)} %get-tuple-element.67.h_ref, bf16[4096,4096]{1,0:T(8,128)(2,1)} %get-tuple-element.68.dpre_ref), kind=kOutput, calls=%fused_computation.101 | convolution fusion | flops 34359738368 | bytes 58720256 | tf_op jit(solution)/shard_map/dot_general | solution.py:24
  373.3 4.1 dynamic-slice_bitcast_fusion
  377.4 4.1 copy-done
  381.8 68.9 %back.1 = (bf16[4096,1024]{1,0:T(8,128)(2,1)}, bf16[4096,1024]{1,0:T(8,128)(2,1)}, f32[16,32,1024]{2,1,0:T(8,128)}, f32[8,1024]{1,0:T(8,128)}, f32[8,1024]{1,0:T...) custom-call(s32[16,1,256]{2,1,0:T(1,128)} %broadcast_in_dim.54.tok_ref, bf16[4096,4096]{1,0:T(8,128)(2,1)} %get-tuple-element.68.dpre_ref, ...), custom_call_target="tpu_custom_call" | custom-call | flops 42949672960 | bytes 90000000 | tf_op jit(solution)/shard_map/back/pallas_call | solution.py:370
  450.7 11.2 %bitcast_add_fusion = f32[2,2,128,4096]{3,2,1,0:T(8,128)} fusion(f32[2,2,128,4096]{3,2,1,0:T(8,128)} %collective-permute-done, f32[2,2,2,128,4096]{4,3,2,1,0:T(8,128)} %bitcast.124, s32[]{:T(128)S(6)} %select_n.58), kind=kLoop, calls=%fused_computation.1 | loop fusion | flops 2097152 | bytes 25165828 | tf_op jit(solution)/shard_map/add | solution.py:459
  461.9 4.0 fusion.30
  465.9 1.5 dynamic-slice_bitcast_fusion.1
  467.4 1.4 dynamic-slice_bitcast_fusion.2
  468.9 1.2 copy-done.1
  470.0 2.0 copy-done.2
  472.0 1.5 collective-permute-start.1
  473.5 0.6 collective-permute-start.2
  474.1 12.7 %fusion.33 = f32[1024,1024]{1,0:T(8,128)} fusion(bf16[4096,1024]{1,0:T(8,128)(2,1)} %get-tuple-element.59.ctx_ref, bf16[4096,1024]{1,0:T(8,128)(2,1)S(1)} %copy-done.46), kind=kOutput, calls=%fused_computation.102 | convolution fusion | flops 8589934592 | bytes 20971520 | tf_op jit(solution)/shard_map/dot_general | solution.py:24
  486.9 1.5 collective-permute-start.3
  488.4 92.8 %attn_bwd.1 = (bf16[16,32,3072]{2,1,0:T(8,128)(2,1)}, bf16[16,32,3072]{2,1,0:T(8,128)(2,1)}, f32[3072,128]{1,0:T(8,128)}) custom-call(s32[16]{0:T(128)} %copy-done.45, s32[16,1,256]{2,1,0:T(1,128)} %broadcast_in_dim.54.tok_ref, bf16[16,3072,256]{2,1,0:T(8,128)(2,1)} %get-tuple-element.61.qkv_ref, f32[16,16,256]{2,1,0:T(8,128)} %get-tuple-element.62.lse_ref, ...), custom_call_target="tpu_custom_call" | custom-call | flops 82500001792 | bytes 60000000 | tf_op jit(solution)/shard_map/attn_bwd/pallas_call | solution.py:303
  581.1 1.9 add.135
  583.1 1.3 copy-done.10
  584.3 3.9 bitcast_add_fusion.1
  588.3 1.3 copy-done.3
  589.7 1.0 dynamic-slice_bitcast_fusion.4
  590.7 0.6 copy-done.8
  591.3 2.4 pad_maximum_fusion
  593.8 2.7 copy-done.4
  596.5 10.7 %fusion.9 = f32[1024,3072]{1,0:T(8,128)} fusion(bf16[1024,3072]{1,0:T(8,128)(2,1)S(1)} %bitcast.126, bf16[512,1024]{1,0:T(8,128)(2,1)} %copy-done.12), kind=kOutput, calls=%fused_computation.17 | convolution fusion | flops 6446645248 | bytes 19922944 | tf_op jit(solution)/shard_map/dot_general | solution.py:24
  607.3 1.5 collective-permute-start.4
  608.8 0.6 collective-permute-start.5
  609.5 1.9 reduce_sum.148
  611.4 0.6 collective-permute-start.7
  612.0 19.9 %collective-permute-done.4 = f32[64,4096]{1,0:T(8,128)} collective-permute-done((f32[64,4096]{1,0:T(8,128)}, f32[64,4096]{1,0:T(8,128)}, u32[]{:S(2)}, u32[]{:S(2)}) %collective-permute-start.4) | collective-permute-done | bytes 1048608 | tf_op jit(solution)/shard_map/ppermute | solution.py:445
  631.9 2.2 collective-permute-done.5
  634.1 1.6 bitcast_add_fusion.3
  635.8 1.5 bitcast_add_fusion.4
  637.4 1.5 copy-done.5
  638.9 9.1 %fusion.34 = f32[1024,1024]{1,0:T(8,128)S(1)} fusion(bf16[1024,3072]{1,0:T(8,128)(2,1)S(1)} %bitcast.127, bf16[1024,3072]{1,0:T(8,128)(2,1)} %all-gather.7.cloned.1.call-done), kind=kOutput, calls=%fused_computation.103 | convolution fusion | flops 6442450944 | bytes 16777216 | tf_op jit(solution)/shard_map/dot_general | solution.py:24
  648.0 2.4 multiply_reduce_fusion
  650.6 3.1 fusion.8
  653.8 43.0 %add_convert_fusion = bf16[4096,1024]{1,0:T(8,128)(2,1)} fusion(f32[4096,1024]{1,0:T(8,128)} %get-tuple-element.60.xmid_ref, bf16[4096,4096]{1,0:T(8,128)(2,1)} %get-tuple-element.90, bf16[4096,1024]{1,0:T(8,128)(2,1)} %all-gather.13.cloned.1.call-done.w2_ref, f32[1024]{0:T(1024)S(1)} %bitcast.138), kind=kOutput, calls=%fused_computation | convolution fusion | flops 34372321280 | bytes 67112960 | tf_op jit(solution)/shard_map/dot_general | solution.py:24
  696.8 2.0 collective-permute-start.6
  698.9 0.7 copy-done.13
  699.6 1.9 add.150
  701.5 63.0 %all-reduce.3.cloned.1.call-done = f32[8,46,128]{2,0,1:T(8,128)} async-done(((f32[8,46,128]{2,0,1:T(8,128)}), f32[8,46,128]{2,0,1:T(8,128)}) %all-reduce.3.cloned.1.call-update) | async-done | bytes 188432 | tf_op jit(solution)/shard_map/psum | solution.py:495
  764.5 0.9 constant_dynamic-slice_fusion.7
  765.5 0.6 copy.44
  766.1 1.3 fusion.22
  767.4 1.3 constant_dynamic-slice_fusion
  768.7 1.2 fusion.23
  769.9 3.3 add.151
  773.2 2.7 add.149
  (157 shorter events, 3.6 us)
Async XLA Ops:
  7.2 3.1 copy-start.34
  7.2 4.0 copy-start.44
  7.2 4.0 copy-start.38
  7.2 4.0 copy-start.43
  7.2 3.9 copy-start.42
  7.2 3.9 copy-start.41
  7.2 3.9 copy-start.37
  7.3 3.9 copy-start.40
  7.3 3.9 copy-start.39
  7.3 3.9 copy-start.35
  7.3 46.9 %all-gather.7.cloned.1.call-start = ((), (), s32[]{:S(2)}) async-start(), calls=%async_computation.3 | async-start | bytes 7077888 | tf_op jit(solution)/shard_map/all_gather | solution.py:397
  8.0 112.4 %all-gather.9.cloned.1.call-start = ((), (), s32[]{:S(2)}) async-start(), calls=%async_computation.4 | async-start | bytes 2359296 | tf_op jit(solution)/shard_map/all_gather | solution.py:397
  8.8 131.2 %all-gather.11.cloned.1.call-start = ((), (), s32[]{:S(2)}) async-start(), calls=%async_computation.5 | async-start | bytes 9437184 | tf_op jit(solution)/shard_map/all_gather | solution.py:397
  9.5 174.5 %all-gather.13.cloned.1.call-start = ((), (), s32[]{:S(2)}) async-start(), calls=%async_computation.6 | async-start | bytes 9437184 | tf_op jit(solution)/shard_map/all_gather | solution.py:397
  10.1 476.8 %reduce-scatter.4.cloned.1.call-start = ((), (), s32[]{:S(2)}) async-start(), calls=%async_computation.7 | async-start | bytes 18874368 | tf_op jit(solution)/shard_map/reduce_scatter | solution.py:438
  10.4 51.9 %copy-start.45 = (s32[16]{0:T(128)}, s32[16]{0:T(128)S(1)}, u32[]{:S(2)}) copy-start(s32[16]{0:T(128)S(1)} %get-tuple-element.109.len_ref) | copy-start | bytes 196
  22.4 2.5 copy-start.15
  22.5 39.8 %copy-start.6 = (f32[32,1024]{1,0:T(8,128)}, f32[32,1024]{1,0:T(8,128)S(1)}, u32[]{:S(2)}) copy-start(f32[32,1024]{1,0:T(8,128)S(1)} %copy_bitcast_fusion) | copy-start | bytes 393220
  22.8 2.2 copy-start.17
  22.9 39.4 %copy-start.28 = (f32[512]{0:T(512)}, f32[512]{0:T(512)S(1)}, u32[]{:S(2)}) copy-start(f32[512]{0:T(512)S(1)} %div.49) | copy-start | bytes 6148
  24.2 0.7 copy-start.20
  24.3 38.0 %copy-start.30 = (f32[512]{0:T(512)}, f32[512]{0:T(512)S(1)}, u32[]{:S(2)}) copy-start(f32[512]{0:T(512)S(1)} %rsqrt.13) | copy-start | bytes 6148
  24.3 1.9 copy-start.32
  24.9 1.3 copy-start.22
  25.5 36.8 %copy-start.12 = (bf16[512,1024]{1,0:T(8,128)(2,1)}, bf16[512,1024]{1,0:T(8,128)(2,1)S(1)}, u32[]{:S(2)}) copy-start(bf16[512,1024]{1,0:T(8,128)(2,1)S(1)} %add_convert_fusion.1) | copy-start | bytes 3145732
  329.5 253.6 %reduce-scatter.6.cloned.1.call-start = ((), (), s32[]{:S(2)}) async-start(), calls=%async_computation.8 | async-start | bytes 4718592 | tf_op jit(solution)/shard_map/reduce_scatter | solution.py:438
  373.2 8.3 %copy-start = (f32[1024,4096]{1,0:T(8,128)}, f32[1024,4096]{1,0:T(8,128)S(1)}, u32[]{:S(2)}) copy-start(f32[1024,4096]{1,0:T(8,128)S(1)} %fusion.32) | copy-start | bytes 50331652
  381.5 69.2 %collective-permute-start = (f32[2,2,128,4096]{3,2,1,0:T(8,128)}, f32[2,2,128,4096]{3,2,1,0:T(8,128)}, u32[]{:S(2)}, u32[]{:S(2)}) collective-permute-start(f32[2,2,128,4096]{3,2,1,0:T(8,128)} %dynamic-slice_bitcast_fusion), channel_id=1, source_target_pairs={{0,1},{1,0},{2,3},{3,2},{4,5},{5,4},{6,7},{7,6},{8,9},{9,8},{10,11... | collective-permute-start | bytes 25165832 | tf_op jit(solution)/shard_map/ppermute | solution.py:445
  465.9 4.1 copy-start.1
  465.9 6.1 copy-start.2
  465.9 8.1 %copy-start.46 = (bf16[4096,1024]{1,0:T(8,128)(2,1)S(1)}, bf16[4096,1024]{1,0:T(8,128)(2,1)}, u32[]{:S(2)}) copy-start(bf16[4096,1024]{1,0:T(8,128)(2,1)} %get-tuple-element.74) | copy-start | bytes 25165828
  472.0 111.0 %collective-permute-start.1 = (f32[2,64,4096]{2,1,0:T(8,128)}, f32[2,64,4096]{2,1,0:T(8,128)S(1)}, u32[]{:S(2)}, u32[]{:S(2)}) collective-permute-start(f32[2,64,4096]{2,1,0:T(8,128)} %dynamic-slice_bitcast_fusion.2), channel_id=1, source_target_pairs={{0,2},{1,3},{2,0},{3,1},{4,6},{5,7},{6,4},{7,5},{8,10},{9,11},{10,... | collective-permute-start | bytes 6291464 | tf_op jit(solution)/shard_map/ppermute | solution.py:445
  473.5 109.5 %collective-permute-start.2 = (f32[2,64,4096]{2,1,0:T(8,128)}, f32[2,64,4096]{2,1,0:T(8,128)}, u32[]{:S(2)}, u32[]{:S(2)}) collective-permute-start(f32[2,64,4096]{2,1,0:T(8,128)} %dynamic-slice_bitcast_fusion.1), channel_id=1, source_target_pairs={{0,4},{1,5},{2,6},{3,7},{4,0},{5,1},{6,2},{7,3},{8,12},{9,13},{10,... | collective-permute-start | bytes 6291464 | tf_op jit(solution)/shard_map/ppermute | solution.py:445
  486.8 210.0 %reduce-scatter.8.cloned.1.call-start = ((), (), s32[]{:S(2)}) async-start(), calls=%async_computation.9 | async-start | bytes 14155776 | tf_op jit(solution)/shard_map/reduce_scatter | solution.py:438
  486.9 94.3 %collective-permute-start.3 = (f32[512,1024]{1,0:T(8,128)}, f32[512,1024]{1,0:T(8,128)S(1)}, u32[]{:S(2)}, u32[]{:S(2)}) collective-permute-start(f32[512,1024]{1,0:T(8,128)} %reduce-scatter.4.cloned.1.call-done), channel_id=1, source_target_pairs={{0,8},{8,0},{1,9},{9,1},{2,10},{10,2},{3,11},{11,3},{4,12},{12,4},... | collective-permute-start | bytes 6291464 | tf_op jit(solution)/shard_map/ppermute | solution.py:435
  488.4 92.8 %copy-start.9 = (f32[512,1024]{1,0:T(8,128)S(1)}, f32[512,1024]{1,0:T(8,128)}, u32[]{:S(2)}) copy-start(f32[512,1024]{1,0:T(8,128)} %reduce-scatter.4.cloned.1.call-done) | copy-start | bytes 6291460
  583.0 1.3 copy-start.10
  588.3 1.3 copy-start.3
  588.3 3.0 copy-start.8
  593.7 2.7 copy-start.4
  607.2 2.2 copy-start.19
  607.2 2.2 copy-start.27
  607.2 2.3 copy-start.26
  607.2 2.3 copy-start.25
  607.2 2.3 copy-start.24
  607.2 157.3 %all-reduce.3.cloned.1.call-start = ((), (), s32[]{:S(2)}) async-start(), calls=%async_computation.10 | async-start | bytes 376832 | tf_op jit(solution)/shard_map/psum | solution.py:495
  607.3 24.6 %collective-permute-start.4 = (f32[64,4096]{1,0:T(8,128)}, f32[64,4096]{1,0:T(8,128)}, u32[]{:S(2)}, u32[]{:S(2)}) collective-permute-start(f32[64,4096]{1,0:T(8,128)} %dynamic-slice_bitcast_fusion.4), channel_id=1, source_target_pairs={{0,4},{1,5},{2,6},{3,7},{4,0},{5,1},{6,2},{7,3},{8,12},{9,13},{10,... | collective-permute-start | bytes 3145736 | tf_op jit(solution)/shard_map/ppermute | solution.py:445
  608.8 25.4 %collective-permute-start.5 = (f32[64,4096]{1,0:T(8,128)S(1)}, f32[64,4096]{1,0:T(8,128)}, u32[]{:S(2)}, u32[]{:S(2)}) collective-permute-start(f32[64,4096]{1,0:T(8,128)S(1)} %dynamic-slice_bitcast_fusion.3), channel_id=1, source_target_pairs={{0,2},{1,3},{2,0},{3,1},{4,6},{5,7},{6,4},{7,5},{8,10},{9,11},{10,... | collective-permute-start | bytes 3145736 | tf_op jit(solution)/shard_map/ppermute | solution.py:445
  611.4 88.2 %collective-permute-start.7 = (f32[128,1024]{1,0:T(8,128)}, f32[128,1024]{1,0:T(8,128)}, u32[]{:S(2)}, u32[]{:S(2)}) collective-permute-start(f32[128,1024]{1,0:T(8,128)} %reduce-scatter.6.cloned.1.call-done), channel_id=1, source_target_pairs={{0,8},{8,0},{1,9},{9,1},{2,10},{10,2},{3,11},{11,3},{4,12},{12,4},... | collective-permute-start | bytes 1572872 | tf_op jit(solution)/shard_map/ppermute | solution.py:435
  635.8 3.1 copy-start.5
  638.9 9.1 %copy-start.7 = (f32[32,1024]{1,0:T(8,128)S(1)}, f32[32,1024]{1,0:T(8,128)}, u32[]{:S(2)}) copy-start(f32[32,1024]{1,0:T(8,128)} %copy-done.6) | copy-start | bytes 393220
  638.9 9.1 %copy-start.23 = (f32[8,1,128]{2,1,0:T(1,128)S(1)}, f32[8,1,128]{2,1,0:T(1,128)}, u32[]{:S(2)}) copy-start(f32[8,1,128]{2,1,0:T(1,128)} %copy-done.22) | copy-start | bytes 12292
  638.9 9.1 %copy-start.29 = (f32[512]{0:T(512)S(1)}, f32[512]{0:T(512)}, u32[]{:S(2)}) copy-start(f32[512]{0:T(512)} %copy-done.28) | copy-start | bytes 6148
  638.9 9.1 %copy-start.31 = (f32[512]{0:T(512)S(1)}, f32[512]{0:T(512)}, u32[]{:S(2)}) copy-start(f32[512]{0:T(512)} %copy-done.30) | copy-start | bytes 6148
  638.9 9.1 %copy-start.33 = (f32[512]{0:T(512)S(1)}, f32[512]{0:T(512)}, u32[]{:S(2)}) copy-start(f32[512]{0:T(512)} %copy-done.32) | copy-start | bytes 6148
  648.0 2.6 copy-start.16
  648.0 2.6 copy-start.18
  648.0 2.6 copy-start.21
  650.4 3.4 copy-start.36
  653.8 116.2 %collective-permute-start.8 = (f32[128,4096]{1,0:T(8,128)S(1)}, f32[128,4096]{1,0:T(8,128)}, u32[]{:S(2)}, u32[]{:S(2)}) collective-permute-start(f32[128,4096]{1,0:T(8,128)S(1)} %pad_maximum_fusion.1), channel_id=1, source_target_pairs={{0,8},{8,0},{1,9},{9,1},{2,10},{10,2},{3,11},{11,3},{4,12},{12,4},... | collective-permute-start | bytes 6291464 | tf_op jit(solution)/shard_map/ppermute | solution.py:435
  653.8 45.8 %copy-start.14 = (f32[128,1024]{1,0:T(8,128)S(1)}, f32[128,1024]{1,0:T(8,128)}, u32[]{:S(2)}) copy-start(f32[128,1024]{1,0:T(8,128)} %reduce-scatter.6.cloned.1.call-done) | copy-start | bytes 1572868
  696.8 76.3 %collective-permute-start.6 = (f32[128,3072]{1,0:T(8,128)}, f32[128,3072]{1,0:T(8,128)}, u32[]{:S(2)}, u32[]{:S(2)}) collective-permute-start(f32[128,3072]{1,0:T(8,128)} %reduce-scatter.8.cloned.1.call-done), channel_id=1, source_target_pairs={{0,8},{8,0},{1,9},{9,1},{2,10},{10,2},{3,11},{11,3},{4,12},{12,4},... | collective-permute-start | bytes 4718600 | tf_op jit(solution)/shard_map/ppermute | solution.py:435
  698.9 0.7 copy-start.13
  769.9 3.3 copy-start.11
Sparse Core Ops, SparseCore 0:
  9.9 44.2 all-gather.6
  56.0 23.8 all-gather.8
  81.8 50.2 all-gather.10
  133.8 50.1 all-gather.12
  329.6 109.6 reduce-scatter.3
  486.9 56.7 reduce-scatter.5
  607.3 84.3 reduce-scatter.7
  699.7 64.7 all-reduce.2

commit v2 on v1

--- a/solution.py
+++ b/solution.py
@@ -204,13 +204,17 @@
     return centered * inv_std, inv_std
 
 
+def flat(ref):
+    return ref[...].reshape(-1, ref.shape[-1])
+
+
 def mid_kernel(tok_ref, ctx_ref, w_ref, tab_ref, bias_ref, gain_ref, shift_ref, xmid_ref, h_ref):
     seq = tok_ref.shape[2]
     for part in range(tok_ref.shape[0]):
         rows = slice(part * seq, (part + 1) * seq)
         hot = one_hot_t(tok_ref[part], TAB)
         x_in = dot(hot, tab_ref[part], 0, 0)
-        x_mid = x_in + dot(ctx_ref[rows, :], w_ref[...]) + bias_ref[...]
+        x_mid = x_in + dot(ctx_ref[rows, :], flat(w_ref)) + bias_ref[...]
         xmid_ref[rows, :] = x_mid
         x_hat, _ = row_stats(x_mid)
         h_ref[rows, :] = (x_hat * gain_ref[...] + shift_ref[...]).astype(BF16)
@@ -227,7 +231,7 @@
     for start in range(0, width, tile):
         cols = slice(start, start + tile)
         pre = dot(h_ref[...], w1_ref[:, cols]) + b1_ref[:, cols]
-        d_act = dot(dy_ref[...], w2_ref[cols, :], 1, 1)
+        d_act = dot(dy_ref[...], w2_ref[start // tile], 1, 1)
         phi = 0.5 + 0.5 * lax.erf(pre * (2.0 ** -0.5))
         act_ref[:, cols] = (pre * phi).astype(BF16)
         slope = phi + pre * (jnp.exp(pre * pre * -0.5) * 0.3989422804014327)
@@ -236,7 +240,7 @@
         dpre_ref[:, cols] = d_pre.astype(BF16)
 
 
-def back_kernel(tok_ref, dpre_ref, w1_ref, xmid_ref, dy_ref, wout_ref, gain_ref,
+def back_kernel(tok_ref, dpre_a, dpre_b, w1_a, w1_b, xmid_ref, dy_ref, wout_ref, gain_ref,
                 dmid_ref, dctx_ref, seg_ref, ggain_ref, gshift_ref, gbout_ref, gbfc2_ref):
     seq = tok_ref.shape[2]
 
@@ -247,7 +251,7 @@
 
     for part in range(tok_ref.shape[0]):
         rows = slice(part * seq, (part + 1) * seq)
-        d_two = dot(dpre_ref[rows, :], w1_ref[...], 1, 1)
+        d_two = dot(dpre_a[rows, :], w1_a[...], 1, 1) + dot(dpre_b[rows, :], w1_b[...], 1, 1)
         x_hat, inv_std = row_stats(xmid_ref[rows, :])
         grad_y = dy_ref[rows, :].astype(F32)
         d_hat = d_two * gain_ref[...]
@@ -262,11 +266,15 @@
         dmid_ref[rows, :] = high
         hot = one_hot_t(tok_ref[part], TAB)
         seg_ref[part] = dot(hot, high) + dot(hot, low)
-        dctx_ref[rows, :] = dot(high, wout_ref[...], 1, 1).astype(BF16)
+        dctx_ref[rows, :] = dot(high, flat(wout_ref), 1, 1).astype(BF16)
 
 
 def whole(shape):
     return pl.BlockSpec(shape, lambda *_: (0,) * len(shape), pipeline_mode=pl.Buffered(1))
+
+
+def out_block(model):
+    return pl.BlockSpec((8, 128, model), lambda *_: (0, 2, 0), pipeline_mode=pl.Buffered(1))
 
 
 def cost(flops, nbytes):
@@ -329,7 +337,7 @@
         mid_kernel, grid=(batch // group,), name='mid',
         in_specs=[pl.BlockSpec((group, 1, seq), lambda b: (b, 0, 0)),
                   pl.BlockSpec((tile, model), lambda b: (b, 0)),
-                  whole((model, model)),
+                  out_block(model),
                   pl.BlockSpec((group, TAB, model), lambda b: (b, 0, 0)),
                   whole((1, model)), whole((1, model)), whole((1, model))],
         out_specs=[pl.BlockSpec((tile, model), lambda b: (b, 0)),
@@ -339,29 +347,29 @@
         compiler_params=params(('arbitrary',)))(tok_rows, ctx, w_out, x_tab, b_out, gain, shift)
 
 
-def run_mlp(h_two, grad_y, w_fc1, w_fc2, b_fc1):
+def run_mlp(h_two, grad_y, w_fc1, w_fc2, b_fc1, name):
     rows, model = h_two.shape
     width = w_fc1.shape[1]
     tile, cols = 512, 1024
     return pl.pallas_call(
-        mlp_kernel, grid=(width // cols, rows // tile), name='mlp',
+        mlp_kernel, grid=(width // cols, rows // tile), name=name,
         in_specs=[pl.BlockSpec((tile, model), lambda f, r: (r, 0)),
                   pl.BlockSpec((tile, model), lambda f, r: (r, 0)),
                   pl.BlockSpec((model, cols), lambda f, r: (0, f)),
-                  pl.BlockSpec((cols, model), lambda f, r: (f, 0)),
+                  pl.BlockSpec((cols // 256, 256, model), lambda f, r: (f, 0, 0)),
                   pl.BlockSpec((1, cols), lambda f, r: (0, f))],
         out_specs=[pl.BlockSpec((tile, cols), lambda f, r: (r, f)),
                    pl.BlockSpec((tile, cols), lambda f, r: (r, f)),
                    pl.BlockSpec((8, cols), lambda f, r: (0, f))],
         out_shape=[jax.ShapeDtypeStruct((rows, width), BF16), jax.ShapeDtypeStruct((rows, width), BF16),
                    jax.ShapeDtypeStruct((8, width), F32)],
-        cost_estimate=cost(4 * rows * model * width, 134e6),
+        cost_estimate=cost(4 * rows * model * width, 67e6),
         compiler_params=params(('arbitrary', 'arbitrary')))(h_two, grad_y, w_fc1, w_fc2, b_fc1)
 
 
-def run_back(tok_rows, d_pre, w_fc1, x_mid, grad_y, w_out, gain, seq, model):
+def run_back(tok_rows, pre_a, pre_b, w1_a, w1_b, x_mid, grad_y, w_out, gain, seq, model):
     batch = tok_rows.shape[0]
-    rows, width = d_pre.shape
+    rows, width = pre_a.shape
     group = 2
     tile = group * seq
     vec = jax.ShapeDtypeStruct((8, model), F32)
@@ -370,14 +378,38 @@
     return pl.pallas_call(
         back_kernel, grid=(batch // group,), name='back',
         in_specs=[pl.BlockSpec((group, 1, seq), lambda b: (b, 0, 0)),
-                  pl.BlockSpec((tile, width), lambda b: (b, 0)),
-                  whole((model, width)), row_spec, row_spec, whole((model, model)), whole((1, model))],
+                  pl.BlockSpec((tile, width), lambda b: (b, 0)), pl.BlockSpec((tile, width), lambda b: (b, 0)),
+                  whole((model, width)), whole((model, width)), row_spec, row_spec, out_block(model), whole((1, model))],
         out_specs=[row_spec, row_spec, pl.BlockSpec((group, TAB, model), lambda b: (b, 0, 0)),
                    vec_spec, vec_spec, vec_spec, vec_spec],
         out_shape=[jax.ShapeDtypeStruct((rows, model), BF16), jax.ShapeDtypeStruct((rows, model), BF16),
                    jax.ShapeDtypeStruct((batch, TAB, model), F32), vec, vec, vec, vec],
-        cost_estimate=cost(2 * rows * model * (width + model), 90e6),
-        compiler_params=params(('arbitrary',)))(tok_rows, d_pre, w_fc1, x_mid, grad_y, w_out, gain)
+        cost_estimate=cost(2 * rows * model * (2 * width + model), 90e6),
+        compiler_params=params(('arbitrary',)))(
+            tok_rows, pre_a, pre_b, w1_a, w1_b, x_mid, grad_y, w_out, gain)
+
+
+def out_kernel(act_a, act_b, w2_a, w2_b, xmid_ref, bias_ref, out_ref):
+    width = 512
+    for start in range(0, out_ref.shape[1], width):
+        cols = slice(start, start + width)
+        total = dot(act_a[...], w2_a[:, :, cols].reshape(-1, width)) + dot(act_b[...], w2_b[:, :, cols].reshape(-1, width))
+        out_ref[:, cols] = (xmid_ref[:, cols] + total + bias_ref[:, cols]).astype(BF16)
+
+
+def run_out(act_a, act_b, w2_a, w2_b, x_mid, b_fc2):
+    rows, model = x_mid.shape
+    width = act_a.shape[1]
+    tile = 512
+    weight = pl.BlockSpec((8, 256, model), lambda r: (0, 0, 0), pipeline_mode=pl.Buffered(1))
+    act_spec = pl.BlockSpec((tile, width), lambda r: (r, 0))
+    row_spec = pl.BlockSpec((tile, model), lambda r: (r, 0))
+    return pl.pallas_call(
+        out_kernel, grid=(rows // tile,), name='out',
+        in_specs=[act_spec, act_spec, weight, weight, row_spec, whole((1, model))],
+        out_specs=row_spec, out_shape=jax.ShapeDtypeStruct((rows, model), BF16),
+        cost_estimate=cost(4 * rows * model * width, 70e6),
+        compiler_params=params(('arbitrary',)))(act_a, act_b, w2_a, w2_b, x_mid, b_fc2)
 
 
 def solution(mesh):
@@ -399,7 +431,11 @@
         smalls = (gain1_part, shift1_part, bout_part, gain2_part, shift2_part, bfc2_part, bqkv_part, bfc1_part)
         packed = jnp.concatenate([e_part] + [part.reshape(-1, 128) for part in smalls], axis=0)
         packed = lax.all_gather(packed, 'fsdp', axis=0, tiled=False)
-        w_qkv, w_out, w_fc1, w_fc2 = (gather(part) for part in (wqkv_part, wout_part, wfc1_part, wfc2_part))
+        w_qkv = gather(wqkv_part)
+        joint = lax.all_gather(jnp.concatenate([wfc2_part[:256], wout_part], axis=0), 'fsdp', axis=0, tiled=False)
+        wfc1_cut = wfc1_part.reshape(-1, 8, 2, 256)
+        w1_a, w1_b = (gather(wfc1_cut[:, :, half].reshape(wfc1_part.shape[0], -1)) for half in range(2))
+        w2_b = lax.all_gather(wfc2_part[256:], 'fsdp', axis=0, tiled=False)
         table = packed[:, :vocab].transpose(1, 0, 2).reshape(vocab, model)[:TAB]
         vecs, at = [], vocab
         for part in smalls:
@@ -425,60 +461,45 @@
         cos_tab, sin_tab = jnp.cos(angles), jnp.sin(angles)
 
         qkv_t, ctx, lse = run_attn_fwd(lengths, tok_rows, qkv_tab, cos_tab, sin_tab, seq, model)
-        x_mid, h_two = run_mid(tok_rows, ctx, w_out, x_tab, b_out, gain2, shift2, seq, model)
-        act, d_pre, gb_fc1 = run_mlp(h_two, grad_y, w_fc1, w_fc2, b_fc1)
-
-        me = lax.axis_index('fsdp')
-        spot = {1: me & 1, 2: (me >> 1) & 1, 4: me >> 2}
-
+        x_mid, h_two = run_mid(tok_rows, ctx, joint, x_tab, b_out, gain2, shift2, seq, model)
+        b1_cut = b_fc1.reshape(8, 2, 256)
+        b1_a, b1_b = b1_cut[:, 0].reshape(1, -1), b1_cut[:, 1].reshape(1, -1)
         def over_dp(part):
             return part + lax.ppermute(part, 'dp', swap)
 
         def scatter(grad):
             return lax.psum_scatter(grad, 'fsdp', scatter_dimension=0, tiled=True)
 
-        def parts_of(val, bit, axis):
-            send = lax.dynamic_index_in_dim(val, 1 - spot[bit], axis, keepdims=False)
-            return send, lax.dynamic_index_in_dim(val, spot[bit], axis, keepdims=False)
-
-        def trade(send, bit):
-            return lax.ppermute(send, 'fsdp', [(dev, dev ^ bit) for dev in range(8)])
-
         after = lax.optimization_barrier
-        raw_fc2 = dot(act, grad_y, 0, 0)
-        part_fc2 = scatter(raw_fc2)
-        h_two, d_pre, raw_fc2 = after((h_two, d_pre, raw_fc2))
-        raw_fc1 = dot(h_two, d_pre, 0, 0)
-        rows = raw_fc1.shape[0] // 8
-        send, held = parts_of(raw_fc1.reshape(2, 2, 2, rows, raw_fc1.shape[1]), 1, 2)
-        d_pre, send = after((d_pre, send))
-        got = trade(send, 1)
+        act_a, pre_a, gb1_a = run_mlp(h_two, grad_y, w1_a, joint, b1_a, 'mlp_a')
+        raw_fc2a = dot(act_a, grad_y, 0, 0)
+        part_fc2a = scatter(raw_fc2a)
+        h_two, raw_fc2a = after((h_two, raw_fc2a))
+        act_b, pre_b, gb1_b = run_mlp(h_two, grad_y, w1_b, w2_b, b1_b, 'mlp_b')
+        pre_a, pre_b, act_b = after((pre_a, pre_b, act_b))
+        raw_fc1a = dot(h_two, pre_a, 0, 0)
+        part_fc1a = scatter(raw_fc1a)
+        act_b, raw_fc1a = after((act_b, raw_fc1a))
+        raw_fc2b = dot(act_b, grad_y, 0, 0)
+        part_fc2b = scatter(raw_fc2b)
+        pre_b, raw_fc2b = after((pre_b, raw_fc2b))
+        raw_fc1b = dot(h_two, pre_b, 0, 0)
+        part_fc1b = scatter(raw_fc1b)
+        pre_a, pre_b, raw_fc1b, part_fc2a = after((pre_a, pre_b, raw_fc1b, part_fc2a))
         d_mid, d_ctx, seg_mid, gg2, gs2, gb_out, gb_fc2 = run_back(
-            tok_rows, d_pre, w_fc1, x_mid, grad_y, w_out, gain2, seq, model)
-        d_mid, got = after((d_mid, got))
-        total = held + got
-        send_a, held_a = parts_of(total[:, :, :rows // 2], 2, 1)
-        send_b, held_b = parts_of(total[:, :, rows // 2:], 4, 0)
-        d_mid, send_a, send_b = after((d_mid, send_a, send_b))
-        got_a, got_b = trade(send_a, 2), trade(send_b, 4)
+            tok_rows, pre_a, pre_b, w1_a, w1_b, x_mid, grad_y, joint, gain2, seq, model)
+        g_fc2a = over_dp(part_fc2a)
         raw_out = dot(ctx, d_mid, 0, 0)
         part_out = scatter(raw_out)
-        d_ctx, raw_out, part_fc2 = after((d_ctx, raw_out, part_fc2))
-        g_w_fc2 = over_dp(part_fc2)
+        d_ctx, raw_out, part_fc1a, g_fc2a = after((d_ctx, raw_out, part_fc1a, g_fc2a))
+        g_fc1a = over_dp(part_fc1a)
         d_high, d_low, gb_qkv = run_attn_bwd(lengths, tok_rows, qkv_t, lse, d_ctx, cos_tab, sin_tab, seq, model)
-        d_high, got_a, got_b, part_out, g_w_fc2 = after((d_high, got_a, got_b, part_out, g_w_fc2))
-        g_w_out = over_dp(part_out)
-        send_a, held_a = parts_of(held_a + got_a, 4, 0)
-        send_b, held_b = parts_of(held_b + got_b, 2, 0)
-        d_high, send_a, send_b = after((d_high, send_a, send_b))
-        got_a, got_b = trade(send_a, 4), trade(send_b, 2)
+        d_high, part_fc2b, part_fc1b, g_fc1a = after((d_high, part_fc2b, part_fc1b, g_fc1a))
+        g_fc2b, g_fc1b = over_dp(part_fc2b), over_dp(part_fc1b)
         d_tab = jnp.concatenate([d_high, d_low], axis=0).reshape(2 * batch * TAB, 3 * model)
         raw_qkv = dot(jnp.concatenate([h_tab, h_tab], axis=0), d_tab, 0, 0)
         part_qkv = scatter(raw_qkv)
-        d_tab, raw_qkv, got_a, got_b = after((d_tab, raw_qkv, got_a, got_b))
-        part_fc1 = jnp.concatenate([held_a + got_a, held_b + got_b], axis=0)
-        d_tab, part_fc1, act = after((d_tab, part_fc1, act))
-        g_w_fc1 = over_dp(part_fc1)
+        d_tab, raw_qkv, act_a, act_b = after((d_tab, raw_qkv, act_a, act_b))
         d_one = dot(d_tab, w_qkv, 1, 1).reshape(2, batch, TAB, model)
         d_one = d_one[0] + d_one[1]
         d_hat = d_one * gain1
@@ -488,22 +509,26 @@
         g_table = jnp.concatenate([g_table, jnp.zeros((vocab - TAB, model), F32)], axis=0)
         vec_grads = (jnp.sum(d_one * hat_one, axis=(0, 1)), jnp.sum(d_one, axis=(0, 1)), jnp.sum(gb_out, axis=0),
                      jnp.sum(gg2, axis=0), jnp.sum(gs2, axis=0), jnp.sum(gb_fc2, axis=0),
-                     jnp.sum(gb_qkv, axis=1), jnp.sum(gb_fc1, axis=0))
+                     jnp.sum(gb_qkv, axis=1),
+                     jnp.concatenate([jnp.sum(gb, axis=0).reshape(8, 1, 256) for gb in (gb1_a, gb1_b)], axis=1))
         small = jnp.concatenate(
             [g_table.reshape(vocab, 8, 128).transpose(1, 0, 2)]
             + [vec.reshape(8, -1, 128) for vec in vec_grads], axis=1)
-        small = lax.psum(small, ('dp', 'fsdp'))
-        small = lax.dynamic_index_in_dim(small, me, 0, keepdims=False)
+        act_a, act_b, small = after((act_a, act_b, small))
+        small = jnp.sum(lax.all_to_all(small, 'fsdp', 0, 0, tiled=True), axis=0)
+        hidden = run_out(act_a, act_b, joint, w2_b, x_mid, b_fc2)
+        hidden, part_qkv, part_out, small = after((hidden, part_qkv, part_out, small))
+        g_w_qkv, g_w_out, small = over_dp(part_qkv), over_dp(part_out), over_dp(small)
         g_small, at = [], vocab
         for part in smalls:
             count = part.shape[0] // 128
             g_small.append(small[at:at + count].reshape(-1))
             at += count
         gg1, gs1, gbo, ggn2, gsh2, gb2, gbq, gb1 = g_small
-        hidden = (x_mid + dot(act, w_fc2) + b_fc2).astype(BF16)
-        hidden, part_qkv = after((hidden, part_qkv))
-        g_w_qkv = over_dp(part_qkv)
         hidden = hidden.reshape(grad_y3.shape)
+        g_w_fc2 = jnp.concatenate([g_fc2a, g_fc2b], axis=0)
+        g_w_fc1 = jnp.concatenate([part.reshape(-1, 8, 1, 256) for part in (g_fc1a, g_fc1b)],
+                                  axis=2).reshape(wfc1_part.shape)
         return (hidden, small[:vocab], gg1, gs1, g_w_qkv, gbq, g_w_out, gbo, ggn2, gsh2, g_w_fc1, gb1, g_w_fc2, gb2)
 
     return jax.shard_map(local_step, mesh=mesh, in_specs=(row_spec, act_spec) + param_specs,

time: 791 us -> 697 us (0.88)
  waiting for transfers between devices: 159 us -> 79.5 us
  Pallas kernels: 341 us -> 386 us
  matrix products: 171 us -> 140 us
  other arithmetic: 42.6 us -> 23.4 us
  local copies, waits for them, and re-layouts: 34.4 us -> 25 us
    psum x1 -> x0, waiting for transfers between devices: 63 us -> none  [local_step(): small = lax.psum(small, ('dp', 'fsdp'))]
    all_gather x4 -> x3, waiting for transfers between devices: 71.2 us -> 17 us  [gather(): return lax.all_gather(part, 'fsdp', axis=0, tiled=True)]
    pallas_call x1 -> x3, Pallas kernels: 102 us -> 148 us  [the longest x2 105 us: run_mlp(): pl.pallas_call(mlp_kernel, grid=(width // cols, rows // tile), name=name,...]
    ppermute x4 -> x7, waiting for transfers between devices: 0.01 us -> 32.3 us  [over_dp(): return part + lax.ppermute(part, 'dp', swap)]
    dot_general x7 -> x8, matrix products: 171 us -> 140 us  [dot(): lax.dot_general(lhs, rhs, (((lhs_dim,), (rhs_dim,)), ((), ())), preferred...]
    reduce_scatter x3 -> x6, waiting for transfers between devices: 0.05 us -> 28.1 us  [scatter(): return lax.psum_scatter(grad, 'fsdp', scatter_dimension=0, tiled=True)]
    ppermute x5 -> x0, waiting for transfers between devices: 22.1 us -> none  [trade(): return lax.ppermute(send, 'fsdp', [(dev, dev ^ bit) for dev in range(8)])]
    add x4 -> x0, other arithmetic: 18.3 us -> none  [the longest x1 11.2 us: local_step(): total = held + got]
  transfers between devices with their start and end apart: 17 -> 19, of which waited for: 5 -> 4; matrix products, arithmetic and copies ran while one was open for 21% -> 26% of each run, Pallas kernels for 31% -> 56%
where the time goes in v2:
time: 697 us; the launch traced here: 692 us
  Pallas kernels  386 us (55%)
  matrix products  140 us (20%)
  waiting for transfers between devices  79.5 us (11%)
  local copies, waits for them, and re-layouts  25 us (4%)
  other arithmetic  23.4 us (3%)
  between operations  15 us (2%)
  starting transfers between devices  11.7 us (2%)
  blocking collectives  11.1 us (2%)
    dot_general x8, matrix products, dot(): lax.dot_general(lhs, rhs, (((lhs_dim,), (rhs_dim,)), ((), ())), preferred...  140 us
    pallas_call x2, Pallas kernels, run_mlp(): pl.pallas_call(mlp_kernel, grid=(width // cols, rows // tile), name=name,...  105 us
    pallas_call x1, Pallas kernels, run_attn_bwd(): pl.pallas_call(attn_bwd_kernel, grid=(batch,), name='attn_bwd', in_specs=...  93 us
    pallas_call x1, Pallas kernels, run_back(): pl.pallas_call(back_kernel, grid=(batch // group,), name='back', in_specs...  67.9 us
    pallas_call x1, Pallas kernels, run_attn_fwd(): pl.pallas_call(attn_fwd_kernel, grid=(batch,), name='attn_fwd', in_specs=...  58.2 us
    pallas_call x1, Pallas kernels, run_out(): pl.pallas_call(out_kernel, grid=(rows // tile,), name='out', in_specs=[ac...  42.5 us
    ppermute x7, waiting for transfers between devices, over_dp(): return part + lax.ppermute(part, 'dp', swap)  32.3 us
    reduce_scatter x6, waiting for transfers between devices, scatter(): return lax.psum_scatter(grad, 'fsdp', scatter_dimension=0, tiled=True)  28.1 us
  transfers between devices with their start and end apart: 19, of which 4 were waited for; matrix products, arithmetic and copies ran while one was open for 26% of the time, Pallas kernels for 56%

profile of v2, /device:TPU:0, one launch (start us, length us, event | category | flops | bytes accessed | tf_op | source)
XLA Modules:
  0.0 691.9 jit_solution(8376586503783706953)
XLA Ops:
  7.2 0.7 all-gather.10.cloned.1.call-update
  8.0 2.1 fusion.24
  10.0 1.9 pad_maximum_fusion.3
  12.1 0.8 reshape.367
  12.9 4.3 slice_reduce_fusion
  17.3 1.0 copy.62
  18.3 0.9 copy.63
  19.3 0.5 all-gather.18.cloned.1.call-update
  20.2 11.1 %all-gather.3 = bf16[8,46,128]{2,1,0:T(8,128)(2,1)S(1)} all-gather(bf16[1,46,128]{2,1,0:T(8,128)(2,1)S(1)} %bitcast.139), channel_id=2, replica_groups=mesh['dp'=2,'fsdp'=8] {'fsdp'}, dimensions={0}, use_global_device_ids=true | all-gather | bytes 105984 | tf_op jit(solution)/shard_map/all_gather | solution.py:433
  31.2 0.6 fusion.19
  32.5 1.3 multiply_convert_fusion
  34.1 0.6 broadcast_in_dim.51.tok_ref
  34.7 0.8 fusion.15
  35.6 0.6 fusion.25
  36.3 0.5 copy-done.17
  36.9 0.5 add_convert_fusion
  37.4 17.0 %all-gather.10.cloned.1.call-done = bf16[1024,3072]{1,0:T(8,128)(2,1)} async-done(((bf16[128,3072]{1,0:T(8,128)(2,1)}), bf16[1024,3072]{1,0:T(8,128)(2,1)}) %all-gather.10.cloned.1.call-update) | async-done | bytes 6291472 | tf_op jit(solution)/shard_map/all_gather | solution.py:429
  54.4 8.6 %add_multiply_fusion = f32[512,3072]{1,0:T(8,128)} fusion(bf16[512,1024]{1,0:T(8,128)(2,1)S(1)} %add_convert_fusion, bf16[1024,3072]{1,0:T(8,128)(2,1)} %all-gather.10.cloned.1.call-done, f32[3072]{0:T(1024)S(1)} %fusion.18, f32[3072]{0:T(1024)S(1)} %reshape.395), kind=kOutput, calls=%fused_computation.1 | convolution fusion | flops 3224371200 | bytes 13656064 | tf_op jit(solution)/shard_map/dot_general | solution.py:24
  63.0 58.2 %attn_fwd.1 = (bf16[16,3072,256]{2,1,0:T(8,128)(2,1)}, bf16[4096,1024]{1,0:T(8,128)(2,1)}, f32[16,16,256]{2,1,0:T(8,128)}) custom-call(s32[16]{0:T(128)} %copy-done.43, s32[16,1,256]{2,1,0:T(1,128)} %broadcast_in_dim.51.tok_ref, f32[16,32,3072]{2,1,0:T(8,128)} %bitcast.165, f32[32,256]{1,0:T(8,128)} %get-tuple-element.137.cos_ref, ...), custom_call_target="tpu_custom_call" | custom-call | flops 44999999488 | bytes 60000000 | tf_op jit(solution)/shard_map/attn_fwd/pallas_call | solution.py:291
  121.2 19.3 %mid.1 = (f32[4096,1024]{1,0:T(8,128)}, bf16[4096,1024]{1,0:T(8,128)(2,1)}) custom-call(s32[16,1,256]{2,1,0:T(1,128)} %broadcast_in_dim.51.tok_ref, bf16[4096,1024]{1,0:T(8,128)(2,1)} %get-tuple-element.63.ctx_ref, bf16[8,384,1024]{2,1,0:T(8,128)(2,1)} %bitcast.158, bf16[16,32,1024]{2,1,0:T(8,128)(2,1)} %get-tuple-element.119.tab_ref, ...), custom_call_target="tpu_custom_call" | custom-call | flops 8589934592 | bytes 33554432 | tf_op jit(solution)/shard_map/mid/pallas_call | solution.py:336
  140.5 52.6 %mlp_a.1 = (bf16[4096,2048]{1,0:T(8,128)(2,1)}, bf16[4096,2048]{1,0:T(8,128)(2,1)}, f32[8,2048]{1,0:T(8,128)}) custom-call(bf16[4096,1024]{1,0:T(8,128)(2,1)} %get-tuple-element.67.h_ref, bf16[4096,1024]{1,0:T(8,128)(2,1)} %bitcast.153, bf16[1024,2048]{1,0:T(8,128)(2,1)} %all-gather.12.cloned.1.call-done.w1_ref.w1_a, bf16[8,384,1024]{2,1,0:T(8,128)(2,1)} %bitcast.159, ...), custom_call_target="tpu_custom_call" | custom-call | flops 34359738368 | bytes 67000000 | tf_op jit(solution)/shard_map/mlp_a/pallas_call | solution.py:354
  193.1 24.0 %fusion.26 = f32[2048,1024]{1,0:T(8,128)} fusion(bf16[4096,2048]{1,0:T(8,128)(2,1)} %get-tuple-element.97.act_a, bf16[4096,1024]{1,0:T(8,128)(2,1)} %bitcast.154), kind=kOutput, calls=%fused_computation.87 | convolution fusion | flops 17179869184 | bytes 33554432 | tf_op jit(solution)/shard_map/dot_general | solution.py:24
  217.2 52.8 %mlp_b.1 = (bf16[4096,2048]{1,0:T(8,128)(2,1)}, bf16[4096,2048]{1,0:T(8,128)(2,1)}, f32[8,2048]{1,0:T(8,128)}) custom-call(bf16[4096,1024]{1,0:T(8,128)(2,1)} %get-tuple-element.67.h_ref, bf16[4096,1024]{1,0:T(8,128)(2,1)} %bitcast.155, bf16[1024,2048]{1,0:T(8,128)(2,1)} %all-gather.14.cloned.1.call-done.w1_ref.w1_b, bf16[8,256,1024]{2,1,0:T(8,128)(2,1)} %bitcast.162, ...), custom_call_target="tpu_custom_call" | custom-call | flops 34359738368 | bytes 67000000 | tf_op jit(solution)/shard_map/mlp_b/pallas_call | solution.py:354
  270.1 24.2 %fusion.27 = f32[1024,2048]{1,0:T(8,128)} fusion(bf16[4096,1024]{1,0:T(8,128)(2,1)} %get-tuple-element.67.h_ref, bf16[4096,2048]{1,0:T(8,128)(2,1)} %get-tuple-element.75.dpre_a), kind=kOutput, calls=%fused_computation.88 | convolution fusion | flops 17179869184 | bytes 33554432 | tf_op jit(solution)/shard_map/dot_general | solution.py:24
  294.3 24.0 %fusion.28 = f32[2048,1024]{1,0:T(8,128)} fusion(bf16[4096,2048]{1,0:T(8,128)(2,1)} %get-tuple-element.98.act_b, bf16[4096,1024]{1,0:T(8,128)(2,1)} %bitcast.156), kind=kOutput, calls=%fused_computation.89 | convolution fusion | flops 17179869184 | bytes 33554432 | tf_op jit(solution)/shard_map/dot_general | solution.py:24
  318.3 24.2 %fusion.29 = f32[1024,2048]{1,0:T(8,128)} fusion(bf16[4096,1024]{1,0:T(8,128)(2,1)} %get-tuple-element.67.h_ref, bf16[4096,2048]{1,0:T(8,128)(2,1)} %get-tuple-element.76.dpre_b), kind=kOutput, calls=%fused_computation.90 | convolution fusion | flops 17179869184 | bytes 33554432 | tf_op jit(solution)/shard_map/dot_general | solution.py:24
  342.5 0.7 reduce-scatter.11.cloned.1.call-update
  343.3 1.5 collective-permute-start
  344.8 67.9 %back.1 = (bf16[4096,1024]{1,0:T(8,128)(2,1)}, bf16[4096,1024]{1,0:T(8,128)(2,1)}, f32[16,32,1024]{2,1,0:T(8,128)}, f32[8,1024]{1,0:T(8,128)}, f32[8,1024]{1,0:T...) custom-call(s32[16,1,256]{2,1,0:T(1,128)} %broadcast_in_dim.51.tok_ref, bf16[4096,2048]{1,0:T(8,128)(2,1)} %get-tuple-element.75.dpre_a, ...), custom_call_target="tpu_custom_call" | custom-call | flops 42949672960 | bytes 90000000 | tf_op jit(solution)/shard_map/back/pallas_call | solution.py:378
  412.7 15.1 %fusion.30 = f32[1024,1024]{1,0:T(8,128)} fusion(bf16[4096,1024]{1,0:T(8,128)(2,1)} %get-tuple-element.63.ctx_ref, bf16[4096,1024]{1,0:T(8,128)(2,1)} %get-tuple-element.79), kind=kOutput, calls=%fused_computation.91 | convolution fusion | flops 8589934592 | bytes 20971520 | tf_op jit(solution)/shard_map/dot_general | solution.py:24
  427.9 1.1 copy-done.8
  429.0 1.2 add.84
  430.2 0.6 collective-permute-start.1
  430.8 93.0 %attn_bwd.1 = (bf16[16,32,3072]{2,1,0:T(8,128)(2,1)}, bf16[16,32,3072]{2,1,0:T(8,128)(2,1)}, f32[3072,128]{1,0:T(8,128)}) custom-call(s32[16]{0:T(128)} %copy-done.43, s32[16,1,256]{2,1,0:T(1,128)} %broadcast_in_dim.51.tok_ref, bf16[16,3072,256]{2,1,0:T(8,128)(2,1)} %get-tuple-element.61.qkv_ref, f32[16,16,256]{2,1,0:T(8,128)} %get-tuple-element.62.lse_ref, ...), custom_call_target="tpu_custom_call" | custom-call | flops 82500001792 | bytes 60000000 | tf_op jit(solution)/shard_map/attn_bwd/pallas_call | solution.py:311
  524.0 3.5 pad_maximum_fusion
  527.5 2.7 copy-done
  530.2 9.2 %fusion.9 = f32[1024,3072]{1,0:T(8,128)} fusion(bf16[1024,3072]{1,0:T(8,128)(2,1)S(1)} %bitcast.124, bf16[512,1024]{1,0:T(8,128)(2,1)S(1)} %copy-done.10), kind=kOutput, calls=%fused_computation.14 | convolution fusion | flops 6446645248 | bytes 19922944 | tf_op jit(solution)/shard_map/dot_general | solution.py:24
  539.5 0.8 copy-done.19
  540.5 0.5 copy-done.4
  541.5 1.5 collective-permute-start.5
  543.0 0.6 collective-permute-start.6
  543.6 10.7 %fusion.31 = f32[1024,1024]{1,0:T(8,128)S(1)} fusion(bf16[1024,3072]{1,0:T(8,128)(2,1)} %bitcast.125, bf16[1024,3072]{1,0:T(8,128)(2,1)} %all-gather.10.cloned.1.call-done), kind=kOutput, calls=%fused_computation.92 | convolution fusion | flops 6442450944 | bytes 16777216 | tf_op jit(solution)/shard_map/dot_general | solution.py:24
  554.3 1.3 multiply_reduce_fusion
  555.8 2.4 fusion.8
  558.4 0.7 copy.55
  559.2 3.6 all-to-all-start
  562.7 42.5 %out.1 = bf16[4096,1024]{1,0:T(8,128)(2,1)} custom-call(bf16[4096,2048]{1,0:T(8,128)(2,1)} %get-tuple-element.97.act_a, bf16[4096,2048]{1,0:T(8,128)(2,1)} %get-tuple-element.98.act_b, bf16[8,384,1024]{2,1,0:T(8,128)(2,1)} %bitcast.161, bf16[8,256,1024]{2,1,0:T(8,128)(2,1)} %bitcast.163, f32[4096,1024]{1,0:T(8,128)} %get-tuple-element.77.xmid_ref, ...), custom_call_target="tpu_custom_call" | custom-call | flops 34359738368 | bytes 70000000 | tf_op jit(solution)/shard_map/out/pallas_call | solution.py:407
  605.4 28.1 %reduce-scatter.15.cloned.1.call-done = f32[128,3072]{1,0:T(8,128)} async-done(((f32[1024,3072]{1,0:T(8,128)}), f32[128,3072]{1,0:T(8,128)}) %reduce-scatter.15.cloned.1.call-update) | async-done | bytes 1572880 | tf_op jit(solution)/shard_map/reduce_scatter | solution.py:471
  633.4 1.5 collective-permute-start.3
  635.2 1.3 add.92
  637.0 1.4 add.93
  638.6 0.6 collective-permute-start.2
  639.2 1.5 pad_maximum_fusion.2
  640.6 1.6 copy.56
  642.3 2.7 reshape.389
  645.0 1.5 collective-permute-start.4
  646.4 24.8 %collective-permute-done.2 = f32[46,128]{1,0:T(8,128)S(1)} collective-permute-done((f32[46,128]{1,0:T(8,128)S(1)}, f32[46,128]{1,0:T(8,128)S(1)}, u32[]{:S(2)}, u32[]{:S(2)}) %collective-permute-start.2) | collective-permute-done | bytes 23584 | tf_op jit(solution)/shard_map/ppermute | solution.py:468
  671.2 0.6 slice_bitcast_fusion.7
  671.8 0.6 slice.127
  672.4 0.6 slice_bitcast_fusion.6
  673.0 0.5 slice_bitcast_fusion.8
  673.5 7.5 %collective-permute-done.4 = f32[128,1024]{1,0:T(8,128)S(1)} collective-permute-done((f32[128,1024]{1,0:T(8,128)S(1)}, f32[128,1024]{1,0:T(8,128)S(1)}, u32[]{:S(2)}, u32[]{:S(2)}) %collective-permute-start.4) | collective-permute-done | bytes 524320 | tf_op jit(solution)/shard_map/ppermute | solution.py:468
  681.1 0.9 add.91
  681.9 3.2 add.90
  (170 shorter events, 4.0 us)
Async XLA Ops:
  7.2 4.9 copy-start.11
  7.2 47.2 %all-gather.10.cloned.1.call-start = ((), (), s32[]{:S(2)}) async-start(), calls=%async_computation.7 | async-start | bytes 7077888 | tf_op jit(solution)/shard_map/all_gather | solution.py:429
  7.9 113.3 %all-gather.16.cloned.1.call-start = ((), (), s32[]{:S(2)}) async-start(), calls=%async_computation.16 | async-start | bytes 7077888 | tf_op jit(solution)/shard_map/all_gather | solution.py:435
  11.9 8.0 %copy-start.34 = (bf16[33,128]{1,0:T(8,128)(2,1)S(1)}, bf16[33,128]{1,0:T(8,128)(2,1)}, u32[]{:S(2)}) copy-start(bf16[33,128]{1,0:T(8,128)(2,1)} %param.17) | copy-start | bytes 25348
  11.9 8.0 %copy-start.35 = (bf16[384]{0:T(512)(128)(2,1)S(1)}, bf16[384]{0:T(512)(128)(2,1)}, u32[]{:S(2)}) copy-start(bf16[384]{0:T(512)(128)(2,1)} %param.21) | copy-start | bytes 2308
  12.0 8.0 %copy-start.36 = (bf16[512]{0:T(512)(128)(2,1)S(1)}, bf16[512]{0:T(512)(128)(2,1)}, u32[]{:S(2)}) copy-start(bf16[512]{0:T(512)(128)(2,1)} %param.27) | copy-start | bytes 3076
  12.0 8.0 %copy-start.37 = (bf16[128]{0:T(256)(128)(2,1)S(1)}, bf16[128]{0:T(256)(128)(2,1)}, u32[]{:S(2)}) copy-start(bf16[128]{0:T(256)(128)(2,1)} %param.18) | copy-start | bytes 772
  12.0 8.0 %copy-start.38 = (bf16[128]{0:T(256)(128)(2,1)S(1)}, bf16[128]{0:T(256)(128)(2,1)}, u32[]{:S(2)}) copy-start(bf16[128]{0:T(256)(128)(2,1)} %param.19) | copy-start | bytes 772
  12.0 8.0 %copy-start.39 = (bf16[128]{0:T(256)(128)(2,1)S(1)}, bf16[128]{0:T(256)(128)(2,1)}, u32[]{:S(2)}) copy-start(bf16[128]{0:T(256)(128)(2,1)} %param.23) | copy-start | bytes 772
  12.0 8.0 %copy-start.40 = (bf16[128]{0:T(256)(128)(2,1)S(1)}, bf16[128]{0:T(256)(128)(2,1)}, u32[]{:S(2)}) copy-start(bf16[128]{0:T(256)(128)(2,1)} %param.24) | copy-start | bytes 772
  12.0 8.0 %copy-start.41 = (bf16[128]{0:T(256)(128)(2,1)S(1)}, bf16[128]{0:T(256)(128)(2,1)}, u32[]{:S(2)}) copy-start(bf16[128]{0:T(256)(128)(2,1)} %param.25) | copy-start | bytes 772
  12.0 8.0 %copy-start.42 = (bf16[128]{0:T(256)(128)(2,1)S(1)}, bf16[128]{0:T(256)(128)(2,1)}, u32[]{:S(2)}) copy-start(bf16[128]{0:T(256)(128)(2,1)} %param.29) | copy-start | bytes 772
  12.0 19.8 %copy-start.33 = (s32[16,256]{1,0:T(8,128)S(1)}, s32[16,256]{1,0:T(8,128)}, u32[]{:S(2)}) copy-start(s32[16,256]{1,0:T(8,128)} %param.15) | copy-start | bytes 49156
  12.1 128.4 %all-gather.12.cloned.1.call-start = ((), (), s32[]{:S(2)}) async-start(), calls=%async_computation.8 | async-start | bytes 4718592 | tf_op jit(solution)/shard_map/all_gather | solution.py:429
  18.3 198.9 %all-gather.14.cloned.1.call-start = ((), (), s32[]{:S(2)}) async-start(), calls=%async_computation.9 | async-start | bytes 4718592 | tf_op jit(solution)/shard_map/all_gather | solution.py:429
  19.2 198.0 %all-gather.18.cloned.1.call-start = ((), (), s32[]{:S(2)}) async-start(), calls=%async_computation.17 | async-start | bytes 4718592 | tf_op jit(solution)/shard_map/all_gather | solution.py:438
  19.8 323.5 %reduce-scatter.7.cloned.1.call-start = ((), (), s32[]{:S(2)}) async-start(), calls=%async_computation.10 | async-start | bytes 9437184 | tf_op jit(solution)/shard_map/reduce_scatter | solution.py:471
  31.9 31.1 %copy-start.21 = (f32[8,1,128]{2,1,0:T(1,128)}, f32[8,1,128]{2,1,0:T(1,128)S(1)}, u32[]{:S(2)}) copy-start(f32[8,1,128]{2,1,0:T(1,128)S(1)} %get-tuple-element.126) | copy-start | bytes 12292
  32.0 31.0 %copy-start.43 = (s32[16]{0:T(128)}, s32[16]{0:T(128)S(1)}, u32[]{:S(2)}) copy-start(s32[16]{0:T(128)S(1)} %get-tuple-element.115.len_ref) | copy-start | bytes 196
  32.0 31.0 %copy-start.1 = (f32[32,1024]{1,0:T(8,128)}, f32[32,1024]{1,0:T(8,128)S(1)}, u32[]{:S(2)}) copy-start(f32[32,1024]{1,0:T(8,128)S(1)} %copy_bitcast_fusion) | copy-start | bytes 393220
  32.1 4.2 copy-start.13
  32.4 3.9 copy-start.15
  32.5 30.5 %copy-start.27 = (f32[512]{0:T(512)}, f32[512]{0:T(512)S(1)}, u32[]{:S(2)}) copy-start(f32[512]{0:T(512)S(1)} %div.49) | copy-start | bytes 6148
  36.2 0.6 copy-start.17
  36.3 26.7 %copy-start.29 = (f32[512]{0:T(512)}, f32[512]{0:T(512)S(1)}, u32[]{:S(2)}) copy-start(f32[512]{0:T(512)S(1)} %rsqrt.13) | copy-start | bytes 6148
  36.3 0.6 copy-start.31
  37.4 25.6 %copy-start.9 = (bf16[512,1024]{1,0:T(8,128)(2,1)}, bf16[512,1024]{1,0:T(8,128)(2,1)S(1)}, u32[]{:S(2)}) copy-start(bf16[512,1024]{1,0:T(8,128)(2,1)S(1)} %add_convert_fusion) | copy-start | bytes 3145732
  217.1 213.1 %reduce-scatter.9.cloned.1.call-start = ((), (), s32[]{:S(2)}) async-start(), calls=%async_computation.11 | async-start | bytes 9437184 | tf_op jit(solution)/shard_map/reduce_scatter | solution.py:471
  294.2 229.7 %reduce-scatter.13.cloned.1.call-start = ((), (), s32[]{:S(2)}) async-start(), calls=%async_computation.13 | async-start | bytes 9437184 | tf_op jit(solution)/shard_map/reduce_scatter | solution.py:471
  342.5 181.5 %reduce-scatter.11.cloned.1.call-start = ((), (), s32[]{:S(2)}) async-start(), calls=%async_computation.12 | async-start | bytes 9437184 | tf_op jit(solution)/shard_map/reduce_scatter | solution.py:471
  343.2 262.1 %reduce-scatter.17.cloned.1.call-start = ((), (), s32[]{:S(2)}) async-start(), calls=%async_computation.15 | async-start | bytes 4718592 | tf_op jit(solution)/shard_map/reduce_scatter | solution.py:471
  343.3 84.6 %collective-permute-start = (f32[256,1024]{1,0:T(8,128)}, f32[256,1024]{1,0:T(8,128)S(1)}, u32[]{:S(2)}, u32[]{:S(2)}) collective-permute-start(f32[256,1024]{1,0:T(8,128)} %reduce-scatter.7.cloned.1.call-done), channel_id=1, source_target_pairs={{0,8},{8,0},{1,9},{9,1},{2,10},{10,2},{3,11},{11,3},{4,12},{12,4},... | collective-permute-start | bytes 3145736 | tf_op jit(solution)/shard_map/ppermute | solution.py:468
  427.8 1.2 copy-start.8
  427.8 205.6 %reduce-scatter.15.cloned.1.call-start = ((), (), s32[]{:S(2)}) async-start(), calls=%async_computation.14 | async-start | bytes 14155776 | tf_op jit(solution)/shard_map/reduce_scatter | solution.py:471
  430.2 93.6 %collective-permute-start.1 = (f32[128,2048]{1,0:T(8,128)}, f32[128,2048]{1,0:T(8,128)S(1)}, u32[]{:S(2)}, u32[]{:S(2)}) collective-permute-start(f32[128,2048]{1,0:T(8,128)} %reduce-scatter.9.cloned.1.call-done), channel_id=1, source_target_pairs={{0,8},{8,0},{1,9},{9,1},{2,10},{10,2},{3,11},{11,3},{4,12},{12,4},... | collective-permute-start | bytes 3145736 | tf_op jit(solution)/shard_map/ppermute | solution.py:468
  430.8 93.0 %copy-start.7 = (f32[128,2048]{1,0:T(8,128)S(1)}, f32[128,2048]{1,0:T(8,128)}, u32[]{:S(2)}) copy-start(f32[128,2048]{1,0:T(8,128)} %reduce-scatter.9.cloned.1.call-done) | copy-start | bytes 3145732
  524.0 6.2 copy-start.10
  527.5 2.7 copy-start
  539.4 0.8 copy-start.19
  539.4 0.9 copy-start.20
  539.4 1.0 copy-start.26
  539.4 1.0 copy-start.25
  539.4 1.0 copy-start.24
  539.4 1.0 copy-start.23
  539.4 1.5 copy-start.4
  541.5 12.8 %copy-start.2 = (f32[32,1024]{1,0:T(8,128)S(1)}, f32[32,1024]{1,0:T(8,128)}, u32[]{:S(2)}) copy-start(f32[32,1024]{1,0:T(8,128)} %copy-done.1) | copy-start | bytes 393220
  541.5 12.8 %copy-start.22 = (f32[8,1,128]{2,1,0:T(1,128)S(1)}, f32[8,1,128]{2,1,0:T(1,128)}, u32[]{:S(2)}) copy-start(f32[8,1,128]{2,1,0:T(1,128)} %copy-done.21) | copy-start | bytes 12292
  541.5 12.8 %copy-start.28 = (f32[512]{0:T(512)S(1)}, f32[512]{0:T(512)}, u32[]{:S(2)}) copy-start(f32[512]{0:T(512)} %copy-done.27) | copy-start | bytes 6148
  541.5 12.8 %copy-start.30 = (f32[512]{0:T(512)S(1)}, f32[512]{0:T(512)}, u32[]{:S(2)}) copy-start(f32[512]{0:T(512)} %copy-done.29) | copy-start | bytes 6148
  541.5 12.8 %copy-start.32 = (f32[512]{0:T(512)S(1)}, f32[512]{0:T(512)}, u32[]{:S(2)}) copy-start(f32[512]{0:T(512)} %copy-done.31) | copy-start | bytes 6148
  541.5 93.7 %collective-permute-start.5 = (f32[128,2048]{1,0:T(8,128)}, f32[128,2048]{1,0:T(8,128)}, u32[]{:S(2)}, u32[]{:S(2)}) collective-permute-start(f32[128,2048]{1,0:T(8,128)} %reduce-scatter.13.cloned.1.call-done), channel_id=1, source_target_pairs={{0,8},{8,0},{1,9},{9,1},{2,10},{10,2},{3,11},{11,3},{4,12},{12,4},... | collective-permute-start | bytes 3145736 | tf_op jit(solution)/shard_map/ppermute | solution.py:468
  543.0 93.9 %collective-permute-start.6 = (f32[256,1024]{1,0:T(8,128)}, f32[256,1024]{1,0:T(8,128)}, u32[]{:S(2)}, u32[]{:S(2)}) collective-permute-start(f32[256,1024]{1,0:T(8,128)} %reduce-scatter.11.cloned.1.call-done), channel_id=1, source_target_pairs={{0,8},{8,0},{1,9},{9,1},{2,10},{10,2},{3,11},{11,3},{4,12},{12,4},... | collective-permute-start | bytes 3145736 | tf_op jit(solution)/shard_map/ppermute | solution.py:468
  554.3 1.5 copy-start.14
  554.3 1.5 copy-start.16
  554.3 1.5 copy-start.18
  559.2 46.1 %all-to-all-start = ((f32[8,46,128]{2,1,0:T(8,128)}), f32[8,46,128]{2,1,0:T(8,128)S(1)}, u32[]{:S(2)}, u32[]{:S(2)}) async-start(f32[8,46,128]{2,1,0:T(8,128)} %copy.55), calls=%async_computation.6 | async-start | bytes 393216 | tf_op jit(solution)/shard_map/all_to_all | solution.py:518
  562.7 72.5 %copy-start.5 = (f32[128,2048]{1,0:T(8,128)S(1)}, f32[128,2048]{1,0:T(8,128)}, u32[]{:S(2)}) copy-start(f32[128,2048]{1,0:T(8,128)} %reduce-scatter.13.cloned.1.call-done) | copy-start | bytes 3145732
  605.3 31.7 %copy-start.6 = (f32[256,1024]{1,0:T(8,128)S(1)}, f32[256,1024]{1,0:T(8,128)}, u32[]{:S(2)}) copy-start(f32[256,1024]{1,0:T(8,128)} %reduce-scatter.11.cloned.1.call-done) | copy-start | bytes 3145732
  633.4 48.5 %collective-permute-start.3 = (f32[128,3072]{1,0:T(8,128)}, f32[128,3072]{1,0:T(8,128)}, u32[]{:S(2)}, u32[]{:S(2)}) collective-permute-start(f32[128,3072]{1,0:T(8,128)} %reduce-scatter.15.cloned.1.call-done), channel_id=1, source_target_pairs={{0,8},{8,0},{1,9},{9,1},{2,10},{10,2},{3,11},{11,3},{4,12},{12,4},... | collective-permute-start | bytes 4718600 | tf_op jit(solution)/shard_map/ppermute | solution.py:468
  636.9 2.2 copy-start.3
  638.6 32.6 %collective-permute-start.2 = (f32[46,128]{1,0:T(8,128)S(1)}, f32[46,128]{1,0:T(8,128)S(1)}, u32[]{:S(2)}, u32[]{:S(2)}) collective-permute-start(f32[46,128]{1,0:T(8,128)S(1)} %reduce_sum.169), channel_id=1, source_target_pairs={{0,8},{8,0},{1,9},{9,1},{2,10},{10,2},{3,11},{11,3},{4,12},{12,4},... | collective-permute-start | bytes 70664 | tf_op jit(solution)/shard_map/ppermute | solution.py:468
  640.6 4.3 copy-start.12
  645.0 36.1 %collective-permute-start.4 = (f32[128,1024]{1,0:T(8,128)S(1)}, f32[128,1024]{1,0:T(8,128)S(1)}, u32[]{:S(2)}, u32[]{:S(2)}) collective-permute-start(f32[128,1024]{1,0:T(8,128)S(1)} %copy-done.12), channel_id=1, source_target_pairs={{0,8},{8,0},{1,9},{9,1},{2,10},{10,2},{3,11},{11,3},{4,12},{12,4},... | collective-permute-start | bytes 1572872 | tf_op jit(solution)/shard_map/ppermute | solution.py:468
Sparse Core Ops, SparseCore 0:
  9.8 44.5 all-gather.9
  56.8 41.4 all-gather.15
  100.1 32.5 all-gather.11
  134.4 32.5 all-gather.13
  169.3 32.5 all-gather.17
  217.3 64.9 reduce-scatter.6
  294.4 64.9 reduce-scatter.8
  362.8 64.9 reduce-scatter.12
  431.2 65.0 reduce-scatter.10
  499.5 45.1 reduce-scatter.16
  548.2 85.2 reduce-scatter.14

commit v3 on v2

--- a/solution.py
+++ b/solution.py
@@ -1,4 +1,3 @@
-import functools
 import jax
 import jax.numpy as jnp
 from jax import lax
@@ -17,7 +16,6 @@
 F32 = jnp.float32
 BF16 = jnp.bfloat16
 NEG = -1e30
-MIB = 1024 * 1024
 
 
 def dot(lhs, rhs, lhs_dim=1, rhs_dim=0):
@@ -27,6 +25,10 @@
 def split_two(val):
     high = val.astype(BF16)
     return high, (val - high.astype(F32)).astype(BF16)
+
+
+def col_sum(val):
+    return jnp.sum(val, axis=0, keepdims=True)
 
 
 def one_hot_t(tok_row, rows):
@@ -83,7 +85,7 @@
             last = jnp.where(key_ok, src[sub, split:], NEG)
             top = jnp.maximum(jnp.max(first, axis=0, keepdims=True), jnp.max(last, axis=0, keepdims=True))
             first, last = jnp.exp(first - top), jnp.exp(last - top)
-            total = jnp.sum(first, axis=0, keepdims=True) + jnp.sum(last, axis=0, keepdims=True)
+            total = col_sum(first) + col_sum(last)
             inverse = 1.0 / total
             dst[sub, :split] = (first * inverse).astype(BF16)
             dst[sub, split:] = (last * inverse).astype(BF16)
@@ -109,7 +111,7 @@
     context(p_b, pairs - 1)
 
 
-def attn_bwd_kernel(len_ref, tok_ref, qkv_ref, lse_ref, dctx_ref, cos_ref, sin_ref, high_ref, low_ref, bias_ref,
+def attn_bwd_kernel(len_ref, tok_ref, q_ref, k_ref, v_ref, lse_ref, dctx_ref, cos_ref, sin_ref, high_ref, low_ref, bias_ref,
                     s_a, s_b, d_a, d_b, p_a, p_b, g_a, g_b, dct):
     model = dctx_ref.shape[1]
     seq = dctx_ref.shape[0]
@@ -132,8 +134,8 @@
 
     lax.fori_loop(0, pairs, flip, 0, unroll=4)
 
-    def head_rows(part, step, sub):
-        return pl.ds(pl.multiple_of(part * model + step * 128 + sub * HEAD_DIM, HEAD_DIM), HEAD_DIM)
+    def head_rows(step, sub):
+        return pl.ds(pl.multiple_of(step * 128 + sub * HEAD_DIM, HEAD_DIM), HEAD_DIM)
 
     def unrope(val):
         low, high = val[:HALF], val[HALF:]
@@ -152,8 +154,8 @@
 
     def score(dst_s, dst_d, step):
         for sub in range(2):
-            dst_s[sub] = dot(qkv_ref[0, head_rows(1, step, sub), :], qkv_ref[0, head_rows(0, step, sub), :], 0, 0)
-            dst_d[sub] = dot(qkv_ref[0, head_rows(2, step, sub), :], dct[head_rows(0, step, sub), :], 0, 0)
+            dst_s[sub] = dot(k_ref[0, head_rows(step, sub), :], q_ref[0, head_rows(step, sub), :], 0, 0)
+            dst_d[sub] = dot(v_ref[0, head_rows(step, sub), :], dct[head_rows(step, sub), :], 0, 0)
 
     def soften(src_s, src_d, dst_p, dst_g, step):
         key_ok = lax.broadcasted_iota(jnp.int32, (seq - split, seq), 0) + split < length
@@ -164,16 +166,16 @@
             dst_p[sub, :split] = first.astype(BF16)
             dst_p[sub, split:] = last.astype(BF16)
             d_first, d_last = src_d[sub, :split], src_d[sub, split:]
-            delta = jnp.sum(d_first * first, axis=0, keepdims=True) + jnp.sum(d_last * last, axis=0, keepdims=True)
+            delta = col_sum(d_first * first) + col_sum(d_last * last)
             dst_g[sub, :split] = (first * (d_first - delta)).astype(BF16)
             dst_g[sub, split:] = (last * (d_last - delta)).astype(BF16)
 
     def grads(src_p, src_g, step, fresh):
         dq, dk, dv = [], [], []
         for sub in range(2):
-            dv.append(dot(dct[head_rows(0, step, sub), :], src_p[sub], 1, 1))
-            dq.append(unrope(dot(qkv_ref[0, head_rows(1, step, sub), :], src_g[sub])) * (HEAD_DIM ** -0.5))
-            dk.append(unrope(dot(qkv_ref[0, head_rows(0, step, sub), :], src_g[sub], 1, 1)))
+            dv.append(dot(dct[head_rows(step, sub), :], src_p[sub], 1, 1))
+            dq.append(unrope(dot(k_ref[0, head_rows(step, sub), :], src_g[sub])) * (HEAD_DIM ** -0.5))
+            dk.append(unrope(dot(q_ref[0, head_rows(step, sub), :], src_g[sub], 1, 1)))
         put(step * 128, jnp.concatenate(dq, axis=0), fresh)
         put(model + step * 128, jnp.concatenate(dk, axis=0), fresh)
         put(2 * model + step * 128, jnp.concatenate(dv, axis=0), fresh)
@@ -281,8 +283,8 @@
     return pl.CostEstimate(flops=int(flops), bytes_accessed=int(nbytes), transcendentals=0)
 
 
-def params(dims, limit=56):
-    return pltpu.CompilerParams(dimension_semantics=dims, vmem_limit_bytes=limit * MIB)
+def params(dims):
+    return pltpu.CompilerParams(dimension_semantics=dims, vmem_limit_bytes=58720256)
 
 
 def run_attn_fwd(lengths, tok_rows, tab, cos_tab, sin_tab, seq, model):
@@ -305,27 +307,32 @@
         compiler_params=params(('arbitrary',)))(lengths, tok_rows, tab, cos_tab, sin_tab)
 
 
-def run_attn_bwd(lengths, tok_rows, qkv_t, lse, d_ctx, cos_tab, sin_tab, seq, model):
+def run_attn_bwd(lengths, tok_rows, qkv_t, lse, d_ctx, cos_tab, sin_tab, seq, model, part, parts):
     batch = tok_rows.shape[0]
-    heads = model // HEAD_DIM
+    width = model // parts
+    heads = width // HEAD_DIM
+
+    def slab(kind):
+        return pl.BlockSpec((1, width, seq), lambda b: (b, kind * parts + part, 0))
+
+    tab_spec = pl.BlockSpec((1, TAB, 3 * width), lambda b: (b, 0, 0))
     return pl.pallas_call(
-        attn_bwd_kernel, grid=(batch,), name='attn_bwd',
+        attn_bwd_kernel, grid=(batch,),
         in_specs=[pl.BlockSpec(memory_space=pltpu.SMEM),
                   pl.BlockSpec((1, 1, seq), lambda b: (b, 0, 0)),
-                  pl.BlockSpec((1, 3 * model, seq), lambda b: (b, 0, 0)),
-                  pl.BlockSpec((1, heads, seq), lambda b: (b, 0, 0)),
-                  pl.BlockSpec((seq, model), lambda b: (b, 0)),
+                  slab(0), slab(1), slab(2),
+                  pl.BlockSpec((1, heads, seq), lambda b: (b, part, 0)),
+                  pl.BlockSpec((seq, width), lambda b: (b, part)),
                   whole((HALF, seq)), whole((HALF, seq))],
-        out_specs=[pl.BlockSpec((1, TAB, 3 * model), lambda b: (b, 0, 0)),
-                   pl.BlockSpec((1, TAB, 3 * model), lambda b: (b, 0, 0)),
-                   pl.BlockSpec((3 * model, 128), lambda b: (0, 0))],
-        out_shape=[jax.ShapeDtypeStruct((batch, TAB, 3 * model), BF16),
-                   jax.ShapeDtypeStruct((batch, TAB, 3 * model), BF16),
-                   jax.ShapeDtypeStruct((3 * model, 128), F32)],
+        out_specs=[tab_spec, tab_spec, pl.BlockSpec((3 * width, 128), lambda b: (0, 0))],
+        out_shape=[jax.ShapeDtypeStruct((batch, TAB, 3 * width), BF16),
+                   jax.ShapeDtypeStruct((batch, TAB, 3 * width), BF16),
+                   jax.ShapeDtypeStruct((3 * width, 128), F32)],
         scratch_shapes=[pltpu.VMEM((2, seq, seq), F32)] * 4 + [pltpu.VMEM((2, seq, seq), BF16)] * 4
-        + [pltpu.VMEM((model, seq), BF16)],
-        cost_estimate=cost(110e9 * 0.75, 60e6),
-        compiler_params=params(('arbitrary',)))(lengths, tok_rows, qkv_t, lse, d_ctx, cos_tab, sin_tab)
+        + [pltpu.VMEM((width, seq), BF16)],
+        cost_estimate=cost(82e9 / parts, 60e6 / parts),
+        compiler_params=params(('arbitrary',)))(
+            lengths, tok_rows, qkv_t, qkv_t, qkv_t, lse, d_ctx, cos_tab, sin_tab)
 
 
 def run_mid(tok_rows, ctx, w_out, x_tab, b_out, gain, shift, seq, model):
@@ -347,12 +354,12 @@
         compiler_params=params(('arbitrary',)))(tok_rows, ctx, w_out, x_tab, b_out, gain, shift)
 
 
-def run_mlp(h_two, grad_y, w_fc1, w_fc2, b_fc1, name):
+def run_mlp(h_two, grad_y, w_fc1, w_fc2, b_fc1):
     rows, model = h_two.shape
     width = w_fc1.shape[1]
     tile, cols = 512, 1024
     return pl.pallas_call(
-        mlp_kernel, grid=(width // cols, rows // tile), name=name,
+        mlp_kernel, grid=(width // cols, rows // tile),
         in_specs=[pl.BlockSpec((tile, model), lambda f, r: (r, 0)),
                   pl.BlockSpec((tile, model), lambda f, r: (r, 0)),
                   pl.BlockSpec((model, cols), lambda f, r: (0, f)),
@@ -412,6 +419,11 @@
         compiler_params=params(('arbitrary',)))(act_a, act_b, w2_a, w2_b, x_mid, b_fc2)
 
 
+def interleave(first, second, width):
+    return jnp.concatenate([part[:, at:at + width] for at in range(0, first.shape[1], width)
+                            for part in (first, second)], axis=1)
+
+
 def solution(mesh):
     row_spec = P(('dp', 'fsdp'), None)
     act_spec = P(('dp', 'fsdp'), None, None)
@@ -464,6 +476,7 @@
         x_mid, h_two = run_mid(tok_rows, ctx, joint, x_tab, b_out, gain2, shift2, seq, model)
         b1_cut = b_fc1.reshape(8, 2, 256)
         b1_a, b1_b = b1_cut[:, 0].reshape(1, -1), b1_cut[:, 1].reshape(1, -1)
+
         def over_dp(part):
             return part + lax.ppermute(part, 'dp', swap)
 
@@ -471,35 +484,49 @@
             return lax.psum_scatter(grad, 'fsdp', scatter_dimension=0, tiled=True)
 
         after = lax.optimization_barrier
-        act_a, pre_a, gb1_a = run_mlp(h_two, grad_y, w1_a, joint, b1_a, 'mlp_a')
+        act_a, pre_a, gb1_a = run_mlp(h_two, grad_y, w1_a, joint, b1_a)
         raw_fc2a = dot(act_a, grad_y, 0, 0)
         part_fc2a = scatter(raw_fc2a)
-        h_two, raw_fc2a = after((h_two, raw_fc2a))
-        act_b, pre_b, gb1_b = run_mlp(h_two, grad_y, w1_b, w2_b, b1_b, 'mlp_b')
-        pre_a, pre_b, act_b = after((pre_a, pre_b, act_b))
+        pre_a, raw_fc2a = after((pre_a, raw_fc2a))
         raw_fc1a = dot(h_two, pre_a, 0, 0)
         part_fc1a = scatter(raw_fc1a)
-        act_b, raw_fc1a = after((act_b, raw_fc1a))
+        h_two, raw_fc1a = after((h_two, raw_fc1a))
+        act_b, pre_b, gb1_b = run_mlp(h_two, grad_y, w1_b, w2_b, b1_b)
         raw_fc2b = dot(act_b, grad_y, 0, 0)
         part_fc2b = scatter(raw_fc2b)
         pre_b, raw_fc2b = after((pre_b, raw_fc2b))
         raw_fc1b = dot(h_two, pre_b, 0, 0)
         part_fc1b = scatter(raw_fc1b)
         pre_a, pre_b, raw_fc1b, part_fc2a = after((pre_a, pre_b, raw_fc1b, part_fc2a))
+        g_fc2a = over_dp(part_fc2a)
         d_mid, d_ctx, seg_mid, gg2, gs2, gb_out, gb_fc2 = run_back(
             tok_rows, pre_a, pre_b, w1_a, w1_b, x_mid, grad_y, joint, gain2, seq, model)
-        g_fc2a = over_dp(part_fc2a)
         raw_out = dot(ctx, d_mid, 0, 0)
         part_out = scatter(raw_out)
         d_ctx, raw_out, part_fc1a, g_fc2a = after((d_ctx, raw_out, part_fc1a, g_fc2a))
         g_fc1a = over_dp(part_fc1a)
-        d_high, d_low, gb_qkv = run_attn_bwd(lengths, tok_rows, qkv_t, lse, d_ctx, cos_tab, sin_tab, seq, model)
-        d_high, part_fc2b, part_fc1b, g_fc1a = after((d_high, part_fc2b, part_fc1b, g_fc1a))
-        g_fc2b, g_fc1b = over_dp(part_fc2b), over_dp(part_fc1b)
-        d_tab = jnp.concatenate([d_high, d_low], axis=0).reshape(2 * batch * TAB, 3 * model)
-        raw_qkv = dot(jnp.concatenate([h_tab, h_tab], axis=0), d_tab, 0, 0)
-        part_qkv = scatter(raw_qkv)
-        d_tab, raw_qkv, act_a, act_b = after((d_tab, raw_qkv, act_a, act_b))
+
+        def attn_grads(part, d_ctx):
+            high, low, bias = run_attn_bwd(
+                lengths, tok_rows, qkv_t, lse, d_ctx, cos_tab, sin_tab, seq, model, part, 2)
+            return jnp.concatenate([high, low], axis=0).reshape(2 * batch * TAB, -1), bias
+
+        h_pair = jnp.concatenate([h_tab, h_tab], axis=0)
+        d_tab0, bias0 = attn_grads(0, d_ctx)
+        raw_qkv0 = dot(h_pair, d_tab0, 0, 0)
+        part_qkv0 = scatter(raw_qkv0)
+        d_ctx, raw_qkv0, part_fc2b, g_fc1a = after((d_ctx, raw_qkv0, part_fc2b, g_fc1a))
+        g_fc2b = over_dp(part_fc2b)
+        d_tab1, bias1 = attn_grads(1, d_ctx)
+        raw_qkv1 = dot(h_pair, d_tab1, 0, 0)
+        part_qkv1 = scatter(raw_qkv1)
+        d_tab1, raw_qkv1, act_a, act_b, part_fc1b, g_fc2b = after((d_tab1, raw_qkv1, act_a, act_b, part_fc1b, g_fc2b))
+        g_fc1b = over_dp(part_fc1b)
+        hidden = run_out(act_a, act_b, joint, w2_b, x_mid, b_fc2)
+        d_tab1, hidden, g_fc1b, part_out, part_qkv0 = after((d_tab1, hidden, g_fc1b, part_out, part_qkv0))
+        g_w_out, g_qkv0 = over_dp(part_out), over_dp(part_qkv0)
+        d_tab = interleave(d_tab0, d_tab1, model // 2)
+        gb_qkv = jnp.concatenate([jnp.sum(val, axis=1).reshape(3, 1, model // 2) for val in (bias0, bias1)], axis=1)
         d_one = dot(d_tab, w_qkv, 1, 1).reshape(2, batch, TAB, model)
         d_one = d_one[0] + d_one[1]
         d_hat = d_one * gain1
@@ -509,16 +536,16 @@
         g_table = jnp.concatenate([g_table, jnp.zeros((vocab - TAB, model), F32)], axis=0)
         vec_grads = (jnp.sum(d_one * hat_one, axis=(0, 1)), jnp.sum(d_one, axis=(0, 1)), jnp.sum(gb_out, axis=0),
                      jnp.sum(gg2, axis=0), jnp.sum(gs2, axis=0), jnp.sum(gb_fc2, axis=0),
-                     jnp.sum(gb_qkv, axis=1),
+                     gb_qkv,
                      jnp.concatenate([jnp.sum(gb, axis=0).reshape(8, 1, 256) for gb in (gb1_a, gb1_b)], axis=1))
         small = jnp.concatenate(
             [g_table.reshape(vocab, 8, 128).transpose(1, 0, 2)]
             + [vec.reshape(8, -1, 128) for vec in vec_grads], axis=1)
-        act_a, act_b, small = after((act_a, act_b, small))
         small = jnp.sum(lax.all_to_all(small, 'fsdp', 0, 0, tiled=True), axis=0)
-        hidden = run_out(act_a, act_b, joint, w2_b, x_mid, b_fc2)
-        hidden, part_qkv, part_out, small = after((hidden, part_qkv, part_out, small))
-        g_w_qkv, g_w_out, small = over_dp(part_qkv), over_dp(part_out), over_dp(small)
+        small, g_qkv0, g_w_out = after((small, g_qkv0, g_w_out))
+        small = over_dp(small)
+        g_qkv1 = over_dp(part_qkv1)
+        g_w_qkv = interleave(g_qkv0, g_qkv1, model // 2)
         g_small, at = [], vocab
         for part in smalls:
             count = part.shape[0] // 128

time: 697 us -> 754 us (1.082)
  Pallas kernels: 386 us -> 402 us
  waiting for transfers between devices: 79.5 us -> 91.9 us
  local copies, waits for them, and re-layouts: 25 us -> 36.6 us
  other arithmetic: 23.4 us -> 32.1 us
    ppermute x7 -> x8, waiting for transfers between devices: 32.3 us -> 72.9 us  [over_dp(): return part + lax.ppermute(part, 'dp', swap)]
    reduce_scatter x6 -> x7, waiting for transfers between devices: 28.1 us -> 0.03 us  [scatter(): return lax.psum_scatter(grad, 'fsdp', scatter_dimension=0, tiled=True)]
    pallas_call x3 -> x4, Pallas kernels: 198 us -> 212 us  [the longest x2 107 us: run_mlp(): pl.pallas_call(mlp_kernel, grid=(width // cols, rows // tile), in_specs=[...]
    unnamed x101 -> x115, local copies, waits for them, and re-layouts: 8.49 us -> 18.9 us
    dot_general x8 -> x9, matrix products: 140 us -> 145 us  [dot(): lax.dot_general(lhs, rhs, (((lhs_dim,), (rhs_dim,)), ((), ())), preferred...]
  transfers between devices with their start and end apart: 19 -> 21, of which waited for: 4 -> 7; matrix products, arithmetic and copies ran while one was open for 26% -> 28% of each run, Pallas kernels for 56% -> 54%
where the time goes in v3:
time: 754 us; the launch traced here: 749 us
  Pallas kernels  402 us (53%)
  matrix products  145 us (19%)
  waiting for transfers between devices  91.9 us (12%)
  local copies, waits for them, and re-layouts  36.6 us (5%)
  other arithmetic  32.1 us (4%)
  between operations  15.5 us (2%)
  starting transfers between devices  14.7 us (2%)
  blocking collectives  11.1 us (1%)
    dot_general x9, matrix products, dot(): lax.dot_general(lhs, rhs, (((lhs_dim,), (rhs_dim,)), ((), ())), preferred...  145 us
    pallas_call x2, Pallas kernels, run_mlp(): pl.pallas_call(mlp_kernel, grid=(width // cols, rows // tile), in_specs=[...  107 us
    pallas_call x2, Pallas kernels, run_attn_bwd(): pl.pallas_call(attn_bwd_kernel, grid=(batch,), in_specs=[pl.BlockSpec(mem...  106 us
    ppermute x8, waiting for transfers between devices, over_dp(): return part + lax.ppermute(part, 'dp', swap)  72.9 us
    pallas_call x1, Pallas kernels, run_back(): pl.pallas_call(back_kernel, grid=(batch // group,), name='back', in_specs...  68 us
    pallas_call x1, Pallas kernels, run_attn_fwd(): pl.pallas_call(attn_fwd_kernel, grid=(batch,), name='attn_fwd', in_specs=...  58.2 us
    pallas_call x1, Pallas kernels, run_out(): pl.pallas_call(out_kernel, grid=(rows // tile,), name='out', in_specs=[ac...  43.6 us
    pallas_call x1, Pallas kernels, run_mid(): pl.pallas_call(mid_kernel, grid=(batch // group,), name='mid', in_specs=[...  19.4 us
  transfers between devices with their start and end apart: 21, of which 7 were waited for; matrix products, arithmetic and copies ran while one was open for 28% of the time, Pallas kernels for 54%

profile of v3, /device:TPU:0, one launch (start us, length us, event | category | flops | bytes accessed | tf_op | source)
XLA Modules:
  0.0 748.5 jit_solution(1773472510143089096)
XLA Ops:
  8.0 2.1 fusion.23
  10.0 1.9 pad_maximum_fusion.7
  12.9 4.3 slice_reduce_fusion
  18.2 0.9 copy.63
  20.1 11.1 %all-gather.3 = bf16[8,46,128]{2,1,0:T(8,128)(2,1)S(1)} all-gather(bf16[1,46,128]{2,1,0:T(8,128)(2,1)S(1)} %bitcast.147), channel_id=2, replica_groups=mesh['dp'=2,'fsdp'=8] {'fsdp'}, dimensions={0}, use_global_device_ids=true | all-gather | bytes 105984 | tf_op jit(solution)/shard_map/all_gather | solution.py:445
  32.6 1.3 multiply_convert_fusion
  37.5 17.1 %all-gather.10.cloned.1.call-done = bf16[1024,3072]{1,0:T(8,128)(2,1)} async-done(((bf16[128,3072]{1,0:T(8,128)(2,1)}), bf16[1024,3072]{1,0:T(8,128)(2,1)}) %all-gather.10.cloned.1.call-update) | async-done | bytes 6291472 | tf_op jit(solution)/shard_map/all_gather | solution.py:441
  54.6 8.3 %add_multiply_fusion = f32[512,3072]{1,0:T(8,128)} fusion(bf16[512,1024]{1,0:T(8,128)(2,1)S(1)} %add_convert_fusion, bf16[1024,3072]{1,0:T(8,128)(2,1)} %all-gather.10.cloned.1.call-done, f32[3072]{0:T(1024)S(1)} %fusion.16, f32[3072]{0:T(1024)S(1)} %reshape.407), kind=kOutput, calls=%fused_computation | convolution fusion | flops 3224371200 | bytes 13656064 | tf_op jit(solution)/shard_map/dot_general | solution.py:22
  62.9 58.2 %attn_fwd.1 = (bf16[16,3072,256]{2,1,0:T(8,128)(2,1)}, bf16[4096,1024]{1,0:T(8,128)(2,1)}, f32[16,16,256]{2,1,0:T(8,128)}) custom-call(s32[16]{0:T(128)} %copy-done.45, s32[16,1,256]{2,1,0:T(1,128)} %broadcast_in_dim.51.tok_ref, f32[16,32,3072]{2,1,0:T(8,128)} %bitcast.173, f32[32,256]{1,0:T(8,128)} %get-tuple-element.141.cos_ref, ...), custom_call_target="tpu_custom_call" | custom-call | flops 44999999488 | bytes 60000000 | tf_op jit(solution)/shard_map/attn_fwd/pallas_call | solution.py:293
  121.1 19.4 %mid.1 = (f32[4096,1024]{1,0:T(8,128)}, bf16[4096,1024]{1,0:T(8,128)(2,1)}) custom-call(s32[16,1,256]{2,1,0:T(1,128)} %broadcast_in_dim.51.tok_ref, bf16[4096,1024]{1,0:T(8,128)(2,1)} %get-tuple-element.65.ctx_ref, bf16[8,384,1024]{2,1,0:T(8,128)(2,1)} %bitcast.166, bf16[16,32,1024]{2,1,0:T(8,128)(2,1)} %get-tuple-element.123.tab_ref, ...), custom_call_target="tpu_custom_call" | custom-call | flops 8589934592 | bytes 33554432 | tf_op jit(solution)/shard_map/mid/pallas_call | solution.py:343
  140.5 52.8 %shard_map.254 = (bf16[4096,2048]{1,0:T(8,128)(2,1)}, bf16[4096,2048]{1,0:T(8,128)(2,1)}, f32[8,2048]{1,0:T(8,128)}) custom-call(bf16[4096,1024]{1,0:T(8,128)(2,1)} %get-tuple-element.70.h_ref, bf16[4096,1024]{1,0:T(8,128)(2,1)} %bitcast.161, bf16[1024,2048]{1,0:T(8,128)(2,1)} %all-gather.12.cloned.1.call-done.w1_ref.w1_a, bf16[8,384,1024]{2,1,0:T(8,128)(2,1)} %bitcast.167, ...), custom_call_target="tpu_custom_call" | custom-call | flops 34359738368 | bytes 67000000 | tf_op jit(solution)/shard_map/pallas_call | solution.py:361
  193.3 24.1 %fusion.25 = f32[2048,1024]{1,0:T(8,128)} fusion(bf16[4096,2048]{1,0:T(8,128)(2,1)} %get-tuple-element.89.act_a, bf16[4096,1024]{1,0:T(8,128)(2,1)} %bitcast.162), kind=kOutput, calls=%fused_computation.101 | convolution fusion | flops 17179869184 | bytes 33554432 | tf_op jit(solution)/shard_map/dot_general | solution.py:22
  217.5 25.3 %fusion.26 = f32[1024,2048]{1,0:T(8,128)} fusion(bf16[4096,1024]{1,0:T(8,128)(2,1)} %get-tuple-element.70.h_ref, bf16[4096,2048]{1,0:T(8,128)(2,1)} %get-tuple-element.74.dpre_a), kind=kOutput, calls=%fused_computation.102 | convolution fusion | flops 17179869184 | bytes 33554432 | tf_op jit(solution)/shard_map/dot_general | solution.py:22
  243.0 54.0 %shard_map.255 = (bf16[4096,2048]{1,0:T(8,128)(2,1)}, bf16[4096,2048]{1,0:T(8,128)(2,1)}, f32[8,2048]{1,0:T(8,128)}) custom-call(bf16[4096,1024]{1,0:T(8,128)(2,1)} %get-tuple-element.70.h_ref, bf16[4096,1024]{1,0:T(8,128)(2,1)} %bitcast.163, bf16[1024,2048]{1,0:T(8,128)(2,1)} %all-gather.14.cloned.1.call-done.w1_ref.w1_b, bf16[8,256,1024]{2,1,0:T(8,128)(2,1)} %bitcast.170, ...), custom_call_target="tpu_custom_call" | custom-call | flops 34359738368 | bytes 67000000 | tf_op jit(solution)/shard_map/pallas_call | solution.py:361
  297.0 25.5 %fusion.27 = f32[2048,1024]{1,0:T(8,128)} fusion(bf16[4096,2048]{1,0:T(8,128)(2,1)} %get-tuple-element.90.act_b, bf16[4096,1024]{1,0:T(8,128)(2,1)} %bitcast.164), kind=kOutput, calls=%fused_computation.103 | convolution fusion | flops 17179869184 | bytes 33554432 | tf_op jit(solution)/shard_map/dot_general | solution.py:22
  322.6 24.6 %fusion.28 = f32[1024,2048]{1,0:T(8,128)} fusion(bf16[4096,1024]{1,0:T(8,128)(2,1)} %get-tuple-element.70.h_ref, bf16[4096,2048]{1,0:T(8,128)(2,1)} %get-tuple-element.75.dpre_b), kind=kOutput, calls=%fused_computation.104 | convolution fusion | flops 17179869184 | bytes 33554432 | tf_op jit(solution)/shard_map/dot_general | solution.py:22
  347.3 68.0 %back.1 = (bf16[4096,1024]{1,0:T(8,128)(2,1)}, bf16[4096,1024]{1,0:T(8,128)(2,1)}, f32[16,32,1024]{2,1,0:T(8,128)}, f32[8,1024]{1,0:T(8,128)}, f32[8,1024]{1,0:T...) custom-call(s32[16,1,256]{2,1,0:T(1,128)} %broadcast_in_dim.51.tok_ref, bf16[4096,2048]{1,0:T(8,128)(2,1)} %get-tuple-element.74.dpre_a, ...), custom_call_target="tpu_custom_call" | custom-call | flops 42949672960 | bytes 90000000 | tf_op jit(solution)/shard_map/back/pallas_call | solution.py:385
  415.3 15.2 %fusion.29 = f32[1024,1024]{1,0:T(8,128)} fusion(bf16[4096,1024]{1,0:T(8,128)(2,1)} %get-tuple-element.65.ctx_ref, bf16[4096,1024]{1,0:T(8,128)(2,1)} %get-tuple-element.78), kind=kOutput, calls=%fused_computation.105 | convolution fusion | flops 8589934592 | bytes 20971520 | tf_op jit(solution)/shard_map/dot_general | solution.py:22
  430.6 1.2 copy-done.8
  431.7 1.7 collective-permute-start
  433.5 23.6 %collective-permute-done = f32[256,1024]{1,0:T(8,128)S(1)} collective-permute-done((f32[256,1024]{1,0:T(8,128)S(1)}, f32[256,1024]{1,0:T(8,128)S(1)}, u32[]{:S(2)}, u32[]{:S(2)}) %collective-permute-start) | collective-permute-done | bytes 1048608 | tf_op jit(solution)/shard_map/ppermute | solution.py:481
  457.1 1.1 add.89
  458.2 52.8 %shard_map.256 = (bf16[16,32,1536]{2,1,0:T(8,128)(2,1)}, bf16[16,32,1536]{2,1,0:T(8,128)(2,1)}, f32[1536,128]{1,0:T(8,128)}) custom-call(s32[16]{0:T(128)} %copy-done.45, s32[16,1,256]{2,1,0:T(1,128)} %broadcast_in_dim.51.tok_ref, bf16[16,3072,256]{2,1,0:T(8,128)(2,1)} %get-tuple-element.63.q_ref.k_ref.v_ref, ...), custom_call_target="tpu_custom_call" | custom-call | flops 41000001536 | bytes 30000000 | tf_op jit(solution)/shard_map/pallas_call | solution.py:319
  511.0 2.2 pad_maximum_fusion
  513.2 5.4 fusion.11
  518.7 1.7 collective-permute-start.1
  520.7 1.4 reduce_sum.175
  522.1 1.1 slice_dynamic-update-slice_fusion.2
  523.2 20.5 %collective-permute-done.1 = f32[128,2048]{1,0:T(8,128)} collective-permute-done((f32[128,2048]{1,0:T(8,128)}, f32[128,2048]{1,0:T(8,128)}, u32[]{:S(2)}, u32[]{:S(2)}) %collective-permute-start.1) | collective-permute-done | bytes 1048608 | tf_op jit(solution)/shard_map/ppermute | solution.py:481
  543.7 2.6 add.90
  546.4 2.8 copy.65
  549.2 52.8 %shard_map.257 = (bf16[16,32,1536]{2,1,0:T(8,128)(2,1)}, bf16[16,32,1536]{2,1,0:T(8,128)(2,1)}, f32[1536,128]{1,0:T(8,128)}) custom-call(s32[16]{0:T(128)} %copy-done.45, s32[16,1,256]{2,1,0:T(1,128)} %broadcast_in_dim.51.tok_ref, bf16[16,3072,256]{2,1,0:T(8,128)(2,1)} %get-tuple-element.63.q_ref.k_ref.v_ref, ...), custom_call_target="tpu_custom_call" | custom-call | flops 41000001536 | bytes 30000000 | tf_op jit(solution)/shard_map/pallas_call | solution.py:319
  602.0 1.4 reduce_sum.176
  603.5 1.2 collective-permute-start.2
  604.7 2.2 pad_maximum_fusion.1
  606.9 1.6 copy-done
  608.5 5.4 fusion.10
  614.0 13.1 %collective-permute-done.2 = f32[256,1024]{1,0:T(8,128)} collective-permute-done((f32[256,1024]{1,0:T(8,128)}, f32[256,1024]{1,0:T(8,128)}, u32[]{:S(2)}, u32[]{:S(2)}) %collective-permute-start.2) | collective-permute-done | bytes 1048608 | tf_op jit(solution)/shard_map/ppermute | solution.py:481
  627.1 2.8 add.91
  629.9 1.3 collective-permute-start.3
  631.2 43.6 %out.1 = bf16[4096,1024]{1,0:T(8,128)(2,1)} custom-call(bf16[4096,2048]{1,0:T(8,128)(2,1)} %get-tuple-element.89.act_a, bf16[4096,2048]{1,0:T(8,128)(2,1)} %get-tuple-element.90.act_b, bf16[8,384,1024]{2,1,0:T(8,128)(2,1)} %bitcast.169, bf16[8,256,1024]{2,1,0:T(8,128)(2,1)} %bitcast.171, f32[4096,1024]{1,0:T(8,128)} %get-tuple-element.76.xmid_ref, ...), custom_call_target="tpu_custom_call" | custom-call | flops 34359738368 | bytes 70000000 | tf_op jit(solution)/shard_map/out/pallas_call | solution.py:414
  674.8 1.6 pad_maximum_fusion.4
  676.4 1.1 add.92
  677.5 2.7 copy.66
  680.9 1.3 collective-permute-start.4
  682.2 2.3 slice_dynamic-update-slice_fusion.5
  684.5 1.1 slice_dynamic-update-slice_fusion.1
  685.6 1.1 slice_dynamic-update-slice_fusion.4
  686.7 1.1 slice_dynamic-update-slice_fusion
  687.8 1.1 slice_dynamic-update-slice_fusion.3
  688.9 11.0 %fusion.30 = f32[1024,1024]{1,0:T(8,128)S(1)} fusion(bf16[1024,3072]{1,0:T(8,128)(2,1)} %slice_dynamic-update-slice_fusion.3, bf16[1024,3072]{1,0:T(8,128)(2,1)} %all-gather.10.cloned.1.call-done), kind=kOutput, calls=%fused_computation.106 | convolution fusion | flops 6442450944 | bytes 16777216 | tf_op jit(solution)/shard_map/dot_general | solution.py:22
  700.0 1.3 multiply_reduce_fusion
  701.5 2.5 fusion.8
  704.9 4.2 all-to-all-start
  709.1 1.4 pad_maximum_fusion.3
  710.5 1.6 copy.56
  712.2 2.7 reshape.401
  715.4 2.1 add.97
  717.4 1.2 add.96
  719.0 1.7 collective-permute-start.7
  720.7 2.0 collective-permute-done.6
  725.1 13.6 %collective-permute-done.7 = f32[128,1536]{1,0:T(8,128)S(1)} collective-permute-done((f32[128,1536]{1,0:T(8,128)}, f32[128,1536]{1,0:T(8,128)S(1)}, u32[]{:S(2)}, u32[]{:S(2)}) %collective-permute-start.7) | collective-permute-done | bytes 786464 | tf_op jit(solution)/shard_map/ppermute | solution.py:481
  738.7 1.2 add.99
  740.1 1.1 copy-done.24
  (199 shorter events, 13.9 us)
Async XLA Ops:
  7.2 4.8 copy-start.12
  7.2 47.4 %all-gather.10.cloned.1.call-start = ((), (), s32[]{:S(2)}) async-start(), calls=%async_computation.8 | async-start | bytes 7077888 | tf_op jit(solution)/shard_map/all_gather | solution.py:441
  7.9 113.2 %all-gather.16.cloned.1.call-start = ((), (), s32[]{:S(2)}) async-start(), calls=%async_computation.18 | async-start | bytes 7077888 | tf_op jit(solution)/shard_map/all_gather | solution.py:447
  11.9 128.6 %all-gather.12.cloned.1.call-start = ((), (), s32[]{:S(2)}) async-start(), calls=%async_computation.9 | async-start | bytes 4718592 | tf_op jit(solution)/shard_map/all_gather | solution.py:441
  12.8 7.1 copy-start.36
  12.8 7.1 copy-start.37
  12.8 7.1 copy-start.38
  12.8 7.1 copy-start.39
  12.9 7.1 copy-start.40
  12.9 7.1 copy-start.41
  12.9 7.1 copy-start.42
  12.9 7.0 copy-start.43
  12.9 7.0 copy-start.44
  12.9 19.0 %copy-start.35 = (s32[16,256]{1,0:T(8,128)S(1)}, s32[16,256]{1,0:T(8,128)}, u32[]{:S(2)}) copy-start(s32[16,256]{1,0:T(8,128)} %param.15) | copy-start | bytes 49156
  18.2 224.8 %all-gather.14.cloned.1.call-start = ((), (), s32[]{:S(2)}) async-start(), calls=%async_computation.10 | async-start | bytes 4718592 | tf_op jit(solution)/shard_map/all_gather | solution.py:441
  19.2 223.8 %all-gather.18.cloned.1.call-start = ((), (), s32[]{:S(2)}) async-start(), calls=%async_computation.19 | async-start | bytes 4718592 | tf_op jit(solution)/shard_map/all_gather | solution.py:450
  19.8 327.5 %reduce-scatter.8.cloned.1.call-start = ((), (), s32[]{:S(2)}) async-start(), calls=%async_computation.11 | async-start | bytes 9437184 | tf_op jit(solution)/shard_map/reduce_scatter | solution.py:484
  31.9 31.0 %copy-start.22 = (f32[8,1,128]{2,1,0:T(1,128)}, f32[8,1,128]{2,1,0:T(1,128)S(1)}, u32[]{:S(2)}) copy-start(f32[8,1,128]{2,1,0:T(1,128)S(1)} %get-tuple-element.130) | copy-start | bytes 12292
  32.0 30.9 %copy-start.45 = (s32[16]{0:T(128)}, s32[16]{0:T(128)S(1)}, u32[]{:S(2)}) copy-start(s32[16]{0:T(128)S(1)} %get-tuple-element.119.len_ref) | copy-start | bytes 196
  32.1 30.8 %copy-start.2 = (f32[32,1024]{1,0:T(8,128)}, f32[32,1024]{1,0:T(8,128)S(1)}, u32[]{:S(2)}) copy-start(f32[32,1024]{1,0:T(8,128)S(1)} %copy_bitcast_fusion) | copy-start | bytes 393220
  32.2 4.2 copy-start.14
  32.5 3.9 copy-start.16
  32.6 30.4 %copy-start.29 = (f32[512]{0:T(512)}, f32[512]{0:T(512)S(1)}, u32[]{:S(2)}) copy-start(f32[512]{0:T(512)S(1)} %div.53) | copy-start | bytes 6148
  36.4 26.6 %copy-start.31 = (f32[512]{0:T(512)}, f32[512]{0:T(512)S(1)}, u32[]{:S(2)}) copy-start(f32[512]{0:T(512)S(1)} %rsqrt.13) | copy-start | bytes 6148
  37.5 25.5 %copy-start.9 = (bf16[512,1024]{1,0:T(8,128)(2,1)}, bf16[512,1024]{1,0:T(8,128)(2,1)S(1)}, u32[]{:S(2)}) copy-start(bf16[512,1024]{1,0:T(8,128)(2,1)S(1)} %add_convert_fusion) | copy-start | bytes 3145732
  217.5 240.7 %reduce-scatter.10.cloned.1.call-start = ((), (), s32[]{:S(2)}) async-start(), calls=%async_computation.12 | async-start | bytes 9437184 | tf_op jit(solution)/shard_map/reduce_scatter | solution.py:484
  242.9 303.5 %reduce-scatter.12.cloned.1.call-start = ((), (), s32[]{:S(2)}) async-start(), calls=%async_computation.13 | async-start | bytes 9437184 | tf_op jit(solution)/shard_map/reduce_scatter | solution.py:484
  322.6 307.3 %reduce-scatter.14.cloned.1.call-start = ((), (), s32[]{:S(2)}) async-start(), calls=%async_computation.14 | async-start | bytes 9437184 | tf_op jit(solution)/shard_map/reduce_scatter | solution.py:484
  347.2 330.3 %reduce-scatter.16.cloned.1.call-start = ((), (), s32[]{:S(2)}) async-start(), calls=%async_computation.15 | async-start | bytes 4718592 | tf_op jit(solution)/shard_map/reduce_scatter | solution.py:484
  430.5 1.2 copy-start.8
  430.5 247.0 %reduce-scatter.18.cloned.1.call-start = ((), (), s32[]{:S(2)}) async-start(), calls=%async_computation.16 | async-start | bytes 7077888 | tf_op jit(solution)/shard_map/reduce_scatter | solution.py:484
  431.7 25.3 %collective-permute-start = (f32[256,1024]{1,0:T(8,128)S(1)}, f32[256,1024]{1,0:T(8,128)S(1)}, u32[]{:S(2)}, u32[]{:S(2)}) collective-permute-start(f32[256,1024]{1,0:T(8,128)S(1)} %copy-done.8), channel_id=1, source_target_pairs={{0,8},{8,0},{1,9},{9,1},{2,10},{10,2},{3,11},{11,3},{4,12},{12,4},... | collective-permute-start | bytes 3145736 | tf_op jit(solution)/shard_map/ppermute | solution.py:481
  511.0 2.3 copy-start.10
  518.6 1.8 copy-start.20
  518.6 1.8 copy-start.21
  518.6 1.9 copy-start.28
  518.6 1.9 copy-start.27
  518.7 2.0 copy-start.26
  518.7 2.0 copy-start.25
  518.7 200.3 %reduce-scatter.20.cloned.1.call-start = ((), (), s32[]{:S(2)}) async-start(), calls=%async_computation.17 | async-start | bytes 7077888 | tf_op jit(solution)/shard_map/reduce_scatter | solution.py:484
  518.7 25.0 %collective-permute-start.1 = (f32[128,2048]{1,0:T(8,128)}, f32[128,2048]{1,0:T(8,128)}, u32[]{:S(2)}, u32[]{:S(2)}) collective-permute-start(f32[128,2048]{1,0:T(8,128)} %reduce-scatter.10.cloned.1.call-done), channel_id=1, source_target_pairs={{0,8},{8,0},{1,9},{9,1},{2,10},{10,2},{3,11},{11,3},{4,12},{12,4},... | collective-permute-start | bytes 3145736 | tf_op jit(solution)/shard_map/ppermute | solution.py:481
  603.5 23.6 %collective-permute-start.2 = (f32[256,1024]{1,0:T(8,128)}, f32[256,1024]{1,0:T(8,128)}, u32[]{:S(2)}, u32[]{:S(2)}) collective-permute-start(f32[256,1024]{1,0:T(8,128)} %reduce-scatter.12.cloned.1.call-done), channel_id=1, source_target_pairs={{0,8},{8,0},{1,9},{9,1},{2,10},{10,2},{3,11},{11,3},{4,12},{12,4},... | collective-permute-start | bytes 3145736 | tf_op jit(solution)/shard_map/ppermute | solution.py:481
  604.7 3.9 copy-start.11
  606.9 1.6 copy-start
  629.9 46.6 %collective-permute-start.3 = (f32[128,2048]{1,0:T(8,128)}, f32[128,2048]{1,0:T(8,128)S(1)}, u32[]{:S(2)}, u32[]{:S(2)}) collective-permute-start(f32[128,2048]{1,0:T(8,128)} %reduce-scatter.14.cloned.1.call-done), channel_id=1, source_target_pairs={{0,8},{8,0},{1,9},{9,1},{2,10},{10,2},{3,11},{11,3},{4,12},{12,4},... | collective-permute-start | bytes 3145736 | tf_op jit(solution)/shard_map/ppermute | solution.py:481
  631.2 43.6 %copy-start.4 = (f32[256,1024]{1,0:T(8,128)S(1)}, f32[256,1024]{1,0:T(8,128)}, u32[]{:S(2)}) copy-start(f32[256,1024]{1,0:T(8,128)} %add.89) | copy-start | bytes 3145732
  631.2 43.6 %copy-start.5 = (f32[256,1024]{1,0:T(8,128)S(1)}, f32[256,1024]{1,0:T(8,128)}, u32[]{:S(2)}) copy-start(f32[256,1024]{1,0:T(8,128)} %add.91) | copy-start | bytes 3145732
  674.8 1.6 copy-start.7
  677.5 8.1 %copy-start.1 = (bf16[32,32,1536]{2,1,0:T(8,128)(2,1)S(1)}, bf16[32,32,1536]{2,1,0:T(8,128)(2,1)}, u32[]{:S(2)}) copy-start(bf16[32,32,1536]{2,1,0:T(8,128)(2,1)} %copy-done) | copy-start | bytes 9437188
  680.2 35.2 %collective-permute-start.5 = (f32[128,1024]{1,0:T(8,128)}, f32[128,1024]{1,0:T(8,128)}, u32[]{:S(2)}, u32[]{:S(2)}) collective-permute-start(f32[128,1024]{1,0:T(8,128)} %reduce-scatter.16.cloned.1.call-done), channel_id=1, source_target_pairs={{0,8},{8,0},{1,9},{9,1},{2,10},{10,2},{3,11},{11,3},{4,12},{12,4},... | collective-permute-start | bytes 1572872 | tf_op jit(solution)/shard_map/ppermute | solution.py:481
  680.9 36.5 %collective-permute-start.4 = (f32[128,1536]{1,0:T(8,128)}, f32[128,1536]{1,0:T(8,128)}, u32[]{:S(2)}, u32[]{:S(2)}) collective-permute-start(f32[128,1536]{1,0:T(8,128)} %reduce-scatter.18.cloned.1.call-done), channel_id=1, source_target_pairs={{0,8},{8,0},{1,9},{9,1},{2,10},{10,2},{3,11},{11,3},{4,12},{12,4},... | collective-permute-start | bytes 2359304 | tf_op jit(solution)/shard_map/ppermute | solution.py:481
  688.9 11.0 %copy-start.3 = (f32[32,1024]{1,0:T(8,128)S(1)}, f32[32,1024]{1,0:T(8,128)}, u32[]{:S(2)}) copy-start(f32[32,1024]{1,0:T(8,128)} %copy-done.2) | copy-start | bytes 393220
  688.9 11.0 %copy-start.23 = (f32[8,1,128]{2,1,0:T(1,128)S(1)}, f32[8,1,128]{2,1,0:T(1,128)}, u32[]{:S(2)}) copy-start(f32[8,1,128]{2,1,0:T(1,128)} %copy-done.22) | copy-start | bytes 12292
  688.9 11.0 %copy-start.30 = (f32[512]{0:T(512)S(1)}, f32[512]{0:T(512)}, u32[]{:S(2)}) copy-start(f32[512]{0:T(512)} %copy-done.29) | copy-start | bytes 6148
  688.9 11.0 %copy-start.32 = (f32[512]{0:T(512)S(1)}, f32[512]{0:T(512)}, u32[]{:S(2)}) copy-start(f32[512]{0:T(512)} %copy-done.31) | copy-start | bytes 6148
  688.9 11.0 %copy-start.34 = (f32[512]{0:T(512)S(1)}, f32[512]{0:T(512)}, u32[]{:S(2)}) copy-start(f32[512]{0:T(512)} %copy-done.33) | copy-start | bytes 6148
  699.9 1.5 copy-start.15
  700.0 1.5 copy-start.17
  700.0 1.5 copy-start.19
  701.5 7.6 %copy-start.6 = (f32[16,8,8,256]{3,2,1,0:T(8,128)S(1)}, f32[16,8,8,256]{3,2,1,0:T(8,128)}, u32[]{:S(2)}) copy-start(f32[16,8,8,256]{3,2,1,0:T(8,128)} %copy.65) | copy-start | bytes 3145732
  704.9 10.4 %all-to-all-start = ((f32[8,46,128]{2,1,0:T(8,128)}), f32[8,46,128]{2,1,0:T(8,128)S(1)}, u32[]{:S(2)}, u32[]{:S(2)}) async-start(f32[8,46,128]{2,1,0:T(8,128)} %copy.55), calls=%async_computation.6 | async-start | bytes 393216 | tf_op jit(solution)/shard_map/all_to_all | solution.py:544
  712.2 5.3 copy-start.13
  718.7 4.1 collective-permute-start.6
  719.0 19.7 %collective-permute-start.7 = (f32[128,1536]{1,0:T(8,128)}, f32[128,1536]{1,0:T(8,128)S(1)}, u32[]{:S(2)}, u32[]{:S(2)}) collective-permute-start(f32[128,1536]{1,0:T(8,128)} %reduce-scatter.20.cloned.1.call-done), channel_id=1, source_target_pairs={{0,8},{8,0},{1,9},{9,1},{2,10},{10,2},{3,11},{11,3},{4,12},{12,4},... | collective-permute-start | bytes 2359304 | tf_op jit(solution)/shard_map/ppermute | solution.py:481
  (3 other events, 2.3 us)
Sparse Core Ops, SparseCore 0:
  9.8 44.6 all-gather.9
  57.0 41.7 all-gather.15
  101.2 32.9 all-gather.11
  135.8 32.8 all-gather.13
  171.0 32.8 all-gather.17
  217.6 65.9 reduce-scatter.7
  287.1 65.8 reduce-scatter.9
  356.4 65.8 reduce-scatter.11
  425.7 65.9 reduce-scatter.13
  494.9 45.5 reduce-scatter.15
  543.8 56.1 reduce-scatter.17
  614.1 55.9 reduce-scatter.19

commit v4 on v3

--- a/solution.py
+++ b/solution.py
@@ -502,8 +502,8 @@
         d_mid, d_ctx, seg_mid, gg2, gs2, gb_out, gb_fc2 = run_back(
             tok_rows, pre_a, pre_b, w1_a, w1_b, x_mid, grad_y, joint, gain2, seq, model)
         raw_out = dot(ctx, d_mid, 0, 0)
-        part_out = scatter(raw_out)
         d_ctx, raw_out, part_fc1a, g_fc2a = after((d_ctx, raw_out, part_fc1a, g_fc2a))
+        moved_out = lax.all_to_all(raw_out.reshape(8, -1, model), 'fsdp', 0, 0, tiled=True)
         g_fc1a = over_dp(part_fc1a)
 
         def attn_grads(part, d_ctx):
@@ -515,7 +515,8 @@
         d_tab0, bias0 = attn_grads(0, d_ctx)
         raw_qkv0 = dot(h_pair, d_tab0, 0, 0)
         part_qkv0 = scatter(raw_qkv0)
-        d_ctx, raw_qkv0, part_fc2b, g_fc1a = after((d_ctx, raw_qkv0, part_fc2b, g_fc1a))
+        d_ctx, raw_qkv0, part_fc2b, g_fc1a, moved_out = after((d_ctx, raw_qkv0, part_fc2b, g_fc1a, moved_out))
+        part_out = jnp.sum(moved_out, axis=0)
         g_fc2b = over_dp(part_fc2b)
         d_tab1, bias1 = attn_grads(1, d_ctx)
         raw_qkv1 = dot(h_pair, d_tab1, 0, 0)

time: 754 us -> 775 us (1.028)
  waiting for transfers between devices: 91.9 us -> 108 us
    all_to_all x0 -> x1, waiting for transfers between devices: none -> 37.5 us  [local_step(): lax.all_to_all(raw_out.reshape(8, -1, model), 'fsdp', 0, 0, tiled=True)]
    ppermute x8, waiting for transfers between devices: 72.9 us -> 51.7 us  [over_dp(): return part + lax.ppermute(part, 'dp', swap)]
    unnamed x115 -> x117, local copies, waits for them, and re-layouts: 18.9 us -> 17.5 us
  transfers between devices with their start and end apart: 21 -> 21, of which waited for: 7 -> 7; matrix products, arithmetic and copies ran while one was open for 28% -> 27% of each run, Pallas kernels for 54% -> 52%
where the time goes in v4:
time: 775 us; the launch traced here: 769 us
  Pallas kernels  402 us (52%)
  matrix products  145 us (19%)
  waiting for transfers between devices  108 us (14%)
  local copies, waits for them, and re-layouts  35.2 us (5%)
  other arithmetic  35.2 us (5%)
  starting transfers between devices  17.6 us (2%)
  between operations  15.3 us (2%)
  blocking collectives  11.1 us (1%)
    dot_general x9, matrix products, dot(): lax.dot_general(lhs, rhs, (((lhs_dim,), (rhs_dim,)), ((), ())), preferred...  145 us
    pallas_call x2, Pallas kernels, run_mlp(): pl.pallas_call(mlp_kernel, grid=(width // cols, rows // tile), in_specs=[...  107 us
    pallas_call x2, Pallas kernels, run_attn_bwd(): pl.pallas_call(attn_bwd_kernel, grid=(batch,), in_specs=[pl.BlockSpec(mem...  106 us
    pallas_call x1, Pallas kernels, run_back(): pl.pallas_call(back_kernel, grid=(batch // group,), name='back', in_specs...  68 us
    pallas_call x1, Pallas kernels, run_attn_fwd(): pl.pallas_call(attn_fwd_kernel, grid=(batch,), name='attn_fwd', in_specs=...  58.2 us
    ppermute x8, waiting for transfers between devices, over_dp(): return part + lax.ppermute(part, 'dp', swap)  51.7 us
    pallas_call x1, Pallas kernels, run_out(): pl.pallas_call(out_kernel, grid=(rows // tile,), name='out', in_specs=[ac...  43.6 us
    all_to_all x1, waiting for transfers between devices, local_step(): lax.all_to_all(raw_out.reshape(8, -1, model), 'fsdp', 0, 0, tiled=True)  37.5 us
  transfers between devices with their start and end apart: 21, of which 7 were waited for; matrix products, arithmetic and copies ran while one was open for 27% of the time, Pallas kernels for 52%

profile of v4, /device:TPU:0, one launch (start us, length us, event | category | flops | bytes accessed | tf_op | source)
XLA Modules:
  0.0 769.3 jit_solution(11413174860786354996)
XLA Ops:
  8.0 2.1 fusion.23
  10.0 1.9 pad_maximum_fusion.7
  12.9 4.3 slice_reduce_fusion
  17.3 0.9 copy.62
  18.2 0.9 copy.63
  20.1 11.1 %all-gather.3 = bf16[8,46,128]{2,1,0:T(8,128)(2,1)S(1)} all-gather(bf16[1,46,128]{2,1,0:T(8,128)(2,1)S(1)} %bitcast.149), channel_id=2, replica_groups=mesh['dp'=2,'fsdp'=8] {'fsdp'}, dimensions={0}, use_global_device_ids=true | all-gather | bytes 105984 | tf_op jit(solution)/shard_map/all_gather | solution.py:445
  32.6 1.3 multiply_convert_fusion
  34.8 0.8 fusion.13
  37.5 17.1 %all-gather.10.cloned.1.call-done = bf16[1024,3072]{1,0:T(8,128)(2,1)} async-done(((bf16[128,3072]{1,0:T(8,128)(2,1)}), bf16[1024,3072]{1,0:T(8,128)(2,1)}) %all-gather.10.cloned.1.call-update) | async-done | bytes 6291472 | tf_op jit(solution)/shard_map/all_gather | solution.py:441
  54.6 8.3 %add_multiply_fusion = f32[512,3072]{1,0:T(8,128)} fusion(bf16[512,1024]{1,0:T(8,128)(2,1)S(1)} %add_convert_fusion, bf16[1024,3072]{1,0:T(8,128)(2,1)} %all-gather.10.cloned.1.call-done, f32[3072]{0:T(1024)S(1)} %fusion.16, f32[3072]{0:T(1024)S(1)} %reshape.411), kind=kOutput, calls=%fused_computation | convolution fusion | flops 3224371200 | bytes 13656064 | tf_op jit(solution)/shard_map/dot_general | solution.py:22
  62.9 58.2 %attn_fwd.1 = (bf16[16,3072,256]{2,1,0:T(8,128)(2,1)}, bf16[4096,1024]{1,0:T(8,128)(2,1)}, f32[16,16,256]{2,1,0:T(8,128)}) custom-call(s32[16]{0:T(128)} %copy-done.46, s32[16,1,256]{2,1,0:T(1,128)} %broadcast_in_dim.51.tok_ref, f32[16,32,3072]{2,1,0:T(8,128)} %bitcast.175, f32[32,256]{1,0:T(8,128)} %get-tuple-element.145.cos_ref, ...), custom_call_target="tpu_custom_call" | custom-call | flops 44999999488 | bytes 60000000 | tf_op jit(solution)/shard_map/attn_fwd/pallas_call | solution.py:293
  121.1 19.4 %mid.1 = (f32[4096,1024]{1,0:T(8,128)}, bf16[4096,1024]{1,0:T(8,128)(2,1)}) custom-call(s32[16,1,256]{2,1,0:T(1,128)} %broadcast_in_dim.51.tok_ref, bf16[4096,1024]{1,0:T(8,128)(2,1)} %get-tuple-element.67.ctx_ref, bf16[8,384,1024]{2,1,0:T(8,128)(2,1)} %bitcast.168, bf16[16,32,1024]{2,1,0:T(8,128)(2,1)} %get-tuple-element.127.tab_ref, ...), custom_call_target="tpu_custom_call" | custom-call | flops 8589934592 | bytes 33554432 | tf_op jit(solution)/shard_map/mid/pallas_call | solution.py:343
  140.5 52.8 %shard_map.254 = (bf16[4096,2048]{1,0:T(8,128)(2,1)}, bf16[4096,2048]{1,0:T(8,128)(2,1)}, f32[8,2048]{1,0:T(8,128)}) custom-call(bf16[4096,1024]{1,0:T(8,128)(2,1)} %get-tuple-element.72.h_ref, bf16[4096,1024]{1,0:T(8,128)(2,1)} %bitcast.163, bf16[1024,2048]{1,0:T(8,128)(2,1)} %all-gather.12.cloned.1.call-done.w1_ref.w1_a, bf16[8,384,1024]{2,1,0:T(8,128)(2,1)} %bitcast.169, ...), custom_call_target="tpu_custom_call" | custom-call | flops 34359738368 | bytes 67000000 | tf_op jit(solution)/shard_map/pallas_call | solution.py:361
  193.3 24.1 %fusion.25 = f32[2048,1024]{1,0:T(8,128)} fusion(bf16[4096,2048]{1,0:T(8,128)(2,1)} %get-tuple-element.92.act_a, bf16[4096,1024]{1,0:T(8,128)(2,1)} %bitcast.164), kind=kOutput, calls=%fused_computation.101 | convolution fusion | flops 17179869184 | bytes 33554432 | tf_op jit(solution)/shard_map/dot_general | solution.py:22
  217.5 25.3 %fusion.26 = f32[1024,2048]{1,0:T(8,128)} fusion(bf16[4096,1024]{1,0:T(8,128)(2,1)} %get-tuple-element.72.h_ref, bf16[4096,2048]{1,0:T(8,128)(2,1)} %get-tuple-element.76.dpre_a), kind=kOutput, calls=%fused_computation.102 | convolution fusion | flops 17179869184 | bytes 33554432 | tf_op jit(solution)/shard_map/dot_general | solution.py:22
  243.0 54.0 %shard_map.255 = (bf16[4096,2048]{1,0:T(8,128)(2,1)}, bf16[4096,2048]{1,0:T(8,128)(2,1)}, f32[8,2048]{1,0:T(8,128)}) custom-call(bf16[4096,1024]{1,0:T(8,128)(2,1)} %get-tuple-element.72.h_ref, bf16[4096,1024]{1,0:T(8,128)(2,1)} %bitcast.165, bf16[1024,2048]{1,0:T(8,128)(2,1)} %all-gather.14.cloned.1.call-done.w1_ref.w1_b, bf16[8,256,1024]{2,1,0:T(8,128)(2,1)} %bitcast.172, ...), custom_call_target="tpu_custom_call" | custom-call | flops 34359738368 | bytes 67000000 | tf_op jit(solution)/shard_map/pallas_call | solution.py:361
  297.0 25.5 %fusion.27 = f32[2048,1024]{1,0:T(8,128)} fusion(bf16[4096,2048]{1,0:T(8,128)(2,1)} %get-tuple-element.93.act_b, bf16[4096,1024]{1,0:T(8,128)(2,1)} %bitcast.166), kind=kOutput, calls=%fused_computation.103 | convolution fusion | flops 17179869184 | bytes 33554432 | tf_op jit(solution)/shard_map/dot_general | solution.py:22
  322.6 24.6 %fusion.28 = f32[1024,2048]{1,0:T(8,128)} fusion(bf16[4096,1024]{1,0:T(8,128)(2,1)} %get-tuple-element.72.h_ref, bf16[4096,2048]{1,0:T(8,128)(2,1)} %get-tuple-element.77.dpre_b), kind=kOutput, calls=%fused_computation.104 | convolution fusion | flops 17179869184 | bytes 33554432 | tf_op jit(solution)/shard_map/dot_general | solution.py:22
  347.3 1.8 collective-permute-start
  349.0 68.0 %back.1 = (bf16[4096,1024]{1,0:T(8,128)(2,1)}, bf16[4096,1024]{1,0:T(8,128)(2,1)}, f32[16,32,1024]{2,1,0:T(8,128)}, f32[8,1024]{1,0:T(8,128)}, f32[8,1024]{1,0:T...) custom-call(s32[16,1,256]{2,1,0:T(1,128)} %broadcast_in_dim.51.tok_ref, bf16[4096,2048]{1,0:T(8,128)(2,1)} %get-tuple-element.76.dpre_a, ...), custom_call_target="tpu_custom_call" | custom-call | flops 42949672960 | bytes 90000000 | tf_op jit(solution)/shard_map/back/pallas_call | solution.py:385
  417.0 15.3 %fusion.29 = f32[1024,1024]{1,0:T(8,128)} fusion(bf16[4096,1024]{1,0:T(8,128)(2,1)} %get-tuple-element.67.ctx_ref, bf16[4096,1024]{1,0:T(8,128)(2,1)} %get-tuple-element.80), kind=kOutput, calls=%fused_computation.105 | convolution fusion | flops 8589934592 | bytes 20971520 | tf_op jit(solution)/shard_map/dot_general | solution.py:22
  432.3 1.1 add.87
  433.4 53.1 %shard_map.256 = (bf16[16,32,1536]{2,1,0:T(8,128)(2,1)}, bf16[16,32,1536]{2,1,0:T(8,128)(2,1)}, f32[1536,128]{1,0:T(8,128)}) custom-call(s32[16]{0:T(128)} %copy-done.46, s32[16,1,256]{2,1,0:T(1,128)} %broadcast_in_dim.51.tok_ref, bf16[16,3072,256]{2,1,0:T(8,128)(2,1)} %get-tuple-element.65.q_ref.k_ref.v_ref, ...), custom_call_target="tpu_custom_call" | custom-call | flops 41000001536 | bytes 30000000 | tf_op jit(solution)/shard_map/pallas_call | solution.py:319
  486.5 2.2 pad_maximum_fusion
  488.8 5.4 fusion.11
  494.3 4.7 all-to-all-start
  499.9 1.5 reduce_sum.185
  501.4 1.1 slice_dynamic-update-slice_fusion.2
  502.5 22.3 %collective-permute-done.1 = f32[128,2048]{1,0:T(8,128)} collective-permute-done((f32[128,2048]{1,0:T(8,128)}, f32[128,2048]{1,0:T(8,128)}, u32[]{:S(2)}, u32[]{:S(2)}) %collective-permute-start.1) | collective-permute-done | bytes 1048608 | tf_op jit(solution)/shard_map/ppermute | solution.py:481
  524.8 2.6 add.88
  527.5 37.5 %all-to-all-done = f32[8,128,1024]{2,1,0:T(8,128)} async-done(((f32[8,128,1024]{2,1,0:T(8,128)}), f32[8,128,1024]{2,1,0:T(8,128)}, u32[]{:S(2)}, u32[]{:S(2)}) %all-to-all-start) | async-done | bytes 4194336 | tf_op jit(solution)/shard_map/all_to_all | solution.py:506
  565.0 52.5 %shard_map.257 = (bf16[16,32,1536]{2,1,0:T(8,128)(2,1)}, bf16[16,32,1536]{2,1,0:T(8,128)(2,1)}, f32[1536,128]{1,0:T(8,128)}) custom-call(s32[16]{0:T(128)} %copy-done.46, s32[16,1,256]{2,1,0:T(1,128)} %broadcast_in_dim.51.tok_ref, bf16[16,3072,256]{2,1,0:T(8,128)(2,1)} %get-tuple-element.65.q_ref.k_ref.v_ref, ...), custom_call_target="tpu_custom_call" | custom-call | flops 41000001536 | bytes 30000000 | tf_op jit(solution)/shard_map/pallas_call | solution.py:319
  617.5 1.4 reduce_sum.186
  619.0 3.4 reduce_sum.175
  622.4 2.7 copy.65
  625.6 1.8 pad_maximum_fusion.1
  627.3 1.6 copy-done
  629.0 5.4 fusion.10
  634.4 12.9 %collective-permute-done.2 = f32[256,1024]{1,0:T(8,128)} collective-permute-done((f32[256,1024]{1,0:T(8,128)}, f32[256,1024]{1,0:T(8,128)}, u32[]{:S(2)}, u32[]{:S(2)}) %collective-permute-start.2) | collective-permute-done | bytes 1048608 | tf_op jit(solution)/shard_map/ppermute | solution.py:481
  647.3 2.7 add.89
  650.6 43.6 %out.1 = bf16[4096,1024]{1,0:T(8,128)(2,1)} custom-call(bf16[4096,2048]{1,0:T(8,128)(2,1)} %get-tuple-element.92.act_a, bf16[4096,2048]{1,0:T(8,128)(2,1)} %get-tuple-element.93.act_b, bf16[8,384,1024]{2,1,0:T(8,128)(2,1)} %bitcast.171, bf16[8,256,1024]{2,1,0:T(8,128)(2,1)} %bitcast.173, f32[4096,1024]{1,0:T(8,128)} %get-tuple-element.78.xmid_ref, ...), custom_call_target="tpu_custom_call" | custom-call | flops 34359738368 | bytes 70000000 | tf_op jit(solution)/shard_map/out/pallas_call | solution.py:414
  694.2 1.6 pad_maximum_fusion.4
  695.8 1.1 add.90
  696.9 2.7 copy.66
  699.6 1.5 collective-permute-start.5
  701.6 2.3 slice_dynamic-update-slice_fusion.5
  703.9 1.1 slice_dynamic-update-slice_fusion.1
  705.0 1.1 slice_dynamic-update-slice_fusion.4
  706.1 1.1 slice_dynamic-update-slice_fusion
  707.2 1.1 slice_dynamic-update-slice_fusion.3
  708.3 11.0 %fusion.30 = f32[1024,1024]{1,0:T(8,128)S(1)} fusion(bf16[1024,3072]{1,0:T(8,128)(2,1)} %slice_dynamic-update-slice_fusion.3, bf16[1024,3072]{1,0:T(8,128)(2,1)} %all-gather.10.cloned.1.call-done), kind=kOutput, calls=%fused_computation.106 | convolution fusion | flops 6442450944 | bytes 16777216 | tf_op jit(solution)/shard_map/dot_general | solution.py:22
  719.4 1.3 multiply_reduce_fusion
  720.9 2.5 fusion.8
  724.3 5.0 all-to-all-start.1
  729.3 1.4 pad_maximum_fusion.3
  730.7 1.6 copy.56
  732.3 2.7 reshape.405
  735.5 1.9 add.95
  737.4 1.5 add.94
  738.9 1.5 collective-permute-start.6
  741.0 1.8 collective-permute-done.6
  745.1 14.7 %collective-permute-done.7 = f32[128,1536]{1,0:T(8,128)S(1)} collective-permute-done((f32[128,1536]{1,0:T(8,128)}, f32[128,1536]{1,0:T(8,128)S(1)}, u32[]{:S(2)}, u32[]{:S(2)}) %collective-permute-start.7) | collective-permute-done | bytes 786464 | tf_op jit(solution)/shard_map/ppermute | solution.py:481
  759.8 1.2 add.97
  761.2 1.1 copy-done.25
  (201 shorter events, 13.7 us)
Async XLA Ops:
  7.2 4.8 copy-start.14
  7.2 47.4 %all-gather.10.cloned.1.call-start = ((), (), s32[]{:S(2)}) async-start(), calls=%async_computation.8 | async-start | bytes 7077888 | tf_op jit(solution)/shard_map/all_gather | solution.py:441
  7.9 113.2 %all-gather.16.cloned.1.call-start = ((), (), s32[]{:S(2)}) async-start(), calls=%async_computation.17 | async-start | bytes 7077888 | tf_op jit(solution)/shard_map/all_gather | solution.py:447
  11.9 128.6 %all-gather.12.cloned.1.call-start = ((), (), s32[]{:S(2)}) async-start(), calls=%async_computation.9 | async-start | bytes 4718592 | tf_op jit(solution)/shard_map/all_gather | solution.py:441
  12.8 7.1 copy-start.37
  12.8 7.1 copy-start.38
  12.8 7.1 copy-start.39
  12.8 7.1 copy-start.40
  12.9 7.1 copy-start.41
  12.9 7.1 copy-start.42
  12.9 7.1 copy-start.43
  12.9 7.0 copy-start.44
  12.9 7.0 copy-start.45
  12.9 19.0 %copy-start.36 = (s32[16,256]{1,0:T(8,128)S(1)}, s32[16,256]{1,0:T(8,128)}, u32[]{:S(2)}) copy-start(s32[16,256]{1,0:T(8,128)} %param.15) | copy-start | bytes 49156
  18.2 224.8 %all-gather.14.cloned.1.call-start = ((), (), s32[]{:S(2)}) async-start(), calls=%async_computation.10 | async-start | bytes 4718592 | tf_op jit(solution)/shard_map/all_gather | solution.py:441
  19.2 223.8 %all-gather.18.cloned.1.call-start = ((), (), s32[]{:S(2)}) async-start(), calls=%async_computation.18 | async-start | bytes 4718592 | tf_op jit(solution)/shard_map/all_gather | solution.py:450
  19.8 327.5 %reduce-scatter.7.cloned.1.call-start = ((), (), s32[]{:S(2)}) async-start(), calls=%async_computation.11 | async-start | bytes 9437184 | tf_op jit(solution)/shard_map/reduce_scatter | solution.py:484
  31.9 31.0 %copy-start.23 = (f32[8,1,128]{2,1,0:T(1,128)}, f32[8,1,128]{2,1,0:T(1,128)S(1)}, u32[]{:S(2)}) copy-start(f32[8,1,128]{2,1,0:T(1,128)S(1)} %get-tuple-element.134) | copy-start | bytes 12292
  32.0 30.9 %copy-start.46 = (s32[16]{0:T(128)}, s32[16]{0:T(128)S(1)}, u32[]{:S(2)}) copy-start(s32[16]{0:T(128)S(1)} %get-tuple-element.123.len_ref) | copy-start | bytes 196
  32.1 30.8 %copy-start.2 = (f32[32,1024]{1,0:T(8,128)}, f32[32,1024]{1,0:T(8,128)S(1)}, u32[]{:S(2)}) copy-start(f32[32,1024]{1,0:T(8,128)S(1)} %copy_bitcast_fusion) | copy-start | bytes 393220
  32.2 4.2 copy-start.15
  32.5 3.9 copy-start.17
  32.6 30.4 %copy-start.30 = (f32[512]{0:T(512)}, f32[512]{0:T(512)S(1)}, u32[]{:S(2)}) copy-start(f32[512]{0:T(512)S(1)} %div.53) | copy-start | bytes 6148
  36.4 26.6 %copy-start.32 = (f32[512]{0:T(512)}, f32[512]{0:T(512)S(1)}, u32[]{:S(2)}) copy-start(f32[512]{0:T(512)S(1)} %rsqrt.13) | copy-start | bytes 6148
  37.5 25.5 %copy-start.11 = (bf16[512,1024]{1,0:T(8,128)(2,1)}, bf16[512,1024]{1,0:T(8,128)(2,1)S(1)}, u32[]{:S(2)}) copy-start(bf16[512,1024]{1,0:T(8,128)(2,1)S(1)} %add_convert_fusion) | copy-start | bytes 3145732
  217.5 216.0 %reduce-scatter.9.cloned.1.call-start = ((), (), s32[]{:S(2)}) async-start(), calls=%async_computation.12 | async-start | bytes 9437184 | tf_op jit(solution)/shard_map/reduce_scatter | solution.py:484
  242.9 284.6 %reduce-scatter.11.cloned.1.call-start = ((), (), s32[]{:S(2)}) async-start(), calls=%async_computation.13 | async-start | bytes 9437184 | tf_op jit(solution)/shard_map/reduce_scatter | solution.py:484
  322.6 327.5 %reduce-scatter.13.cloned.1.call-start = ((), (), s32[]{:S(2)}) async-start(), calls=%async_computation.14 | async-start | bytes 9437184 | tf_op jit(solution)/shard_map/reduce_scatter | solution.py:484
  347.2 349.7 %reduce-scatter.15.cloned.1.call-start = ((), (), s32[]{:S(2)}) async-start(), calls=%async_computation.15 | async-start | bytes 7077888 | tf_op jit(solution)/shard_map/reduce_scatter | solution.py:484
  347.3 85.0 %collective-permute-start = (f32[256,1024]{1,0:T(8,128)}, f32[256,1024]{1,0:T(8,128)S(1)}, u32[]{:S(2)}, u32[]{:S(2)}) collective-permute-start(f32[256,1024]{1,0:T(8,128)} %reduce-scatter.7.cloned.1.call-done), channel_id=1, source_target_pairs={{0,8},{8,0},{1,9},{9,1},{2,10},{10,2},{3,11},{11,3},{4,12},{12,4},... | collective-permute-start | bytes 3145736 | tf_op jit(solution)/shard_map/ppermute | solution.py:481
  417.0 15.3 %copy-start.10 = (f32[256,1024]{1,0:T(8,128)S(1)}, f32[256,1024]{1,0:T(8,128)}, u32[]{:S(2)}) copy-start(f32[256,1024]{1,0:T(8,128)} %reduce-scatter.7.cloned.1.call-done) | copy-start | bytes 3145732
  486.5 2.3 copy-start.12
  494.2 5.4 copy-start.21
  494.2 5.4 copy-start.22
  494.3 5.5 copy-start.29
  494.3 5.5 copy-start.28
  494.3 5.5 copy-start.27
  494.3 5.6 copy-start.26
  494.3 70.7 %all-to-all-start = ((f32[8,128,1024]{2,1,0:T(8,128)}), f32[8,128,1024]{2,1,0:T(8,128)}, u32[]{:S(2)}, u32[]{:S(2)}) async-start(f32[8,128,1024]{2,1,0:T(8,128)} %bitcast.137), calls=%async_computation.3 | async-start | bytes 8388608 | tf_op jit(solution)/shard_map/all_to_all | solution.py:506
  499.0 241.3 %reduce-scatter.17.cloned.1.call-start = ((), (), s32[]{:S(2)}) async-start(), calls=%async_computation.16 | async-start | bytes 7077888 | tf_op jit(solution)/shard_map/reduce_scatter | solution.py:484
  499.1 25.7 %collective-permute-start.1 = (f32[128,2048]{1,0:T(8,128)}, f32[128,2048]{1,0:T(8,128)}, u32[]{:S(2)}, u32[]{:S(2)}) collective-permute-start(f32[128,2048]{1,0:T(8,128)} %reduce-scatter.9.cloned.1.call-done), channel_id=1, source_target_pairs={{0,8},{8,0},{1,9},{9,1},{2,10},{10,2},{3,11},{11,3},{4,12},{12,4},... | collective-permute-start | bytes 3145736 | tf_op jit(solution)/shard_map/ppermute | solution.py:481
  622.4 3.2 copy-start.8
  625.0 22.2 %collective-permute-start.2 = (f32[256,1024]{1,0:T(8,128)}, f32[256,1024]{1,0:T(8,128)}, u32[]{:S(2)}, u32[]{:S(2)}) collective-permute-start(f32[256,1024]{1,0:T(8,128)} %reduce-scatter.11.cloned.1.call-done), channel_id=1, source_target_pairs={{0,8},{8,0},{1,9},{9,1},{2,10},{10,2},{3,11},{11,3},{4,12},{12,4},... | collective-permute-start | bytes 3145736 | tf_op jit(solution)/shard_map/ppermute | solution.py:481
  625.6 3.4 copy-start.13
  627.3 1.6 copy-start
  650.0 45.8 %collective-permute-start.3 = (f32[128,2048]{1,0:T(8,128)}, f32[128,2048]{1,0:T(8,128)S(1)}, u32[]{:S(2)}, u32[]{:S(2)}) collective-permute-start(f32[128,2048]{1,0:T(8,128)} %reduce-scatter.13.cloned.1.call-done), channel_id=1, source_target_pairs={{0,8},{8,0},{1,9},{9,1},{2,10},{10,2},{3,11},{11,3},{4,12},{12,4},... | collective-permute-start | bytes 3145736 | tf_op jit(solution)/shard_map/ppermute | solution.py:481
  650.6 43.6 %copy-start.4 = (f32[256,1024]{1,0:T(8,128)S(1)}, f32[256,1024]{1,0:T(8,128)}, u32[]{:S(2)}) copy-start(f32[256,1024]{1,0:T(8,128)} %add.87) | copy-start | bytes 3145732
  650.6 43.6 %copy-start.5 = (f32[256,1024]{1,0:T(8,128)S(1)}, f32[256,1024]{1,0:T(8,128)}, u32[]{:S(2)}) copy-start(f32[256,1024]{1,0:T(8,128)} %add.89) | copy-start | bytes 3145732
  694.2 1.6 copy-start.9
  696.9 8.1 %copy-start.1 = (bf16[32,32,1536]{2,1,0:T(8,128)(2,1)S(1)}, bf16[32,32,1536]{2,1,0:T(8,128)(2,1)}, u32[]{:S(2)}) copy-start(bf16[32,32,1536]{2,1,0:T(8,128)(2,1)} %copy-done) | copy-start | bytes 9437188
  699.6 35.9 %collective-permute-start.5 = (f32[128,1024]{1,0:T(8,128)}, f32[128,1024]{1,0:T(8,128)}, u32[]{:S(2)}, u32[]{:S(2)}) collective-permute-start(f32[128,1024]{1,0:T(8,128)} %reduce_sum.175), channel_id=1, source_target_pairs={{0,8},{8,0},{1,9},{9,1},{2,10},{10,2},{3,11},{11,3},{4,12},{12,4},... | collective-permute-start | bytes 1572872 | tf_op jit(solution)/shard_map/ppermute | solution.py:481
  701.1 36.3 %collective-permute-start.4 = (f32[128,1536]{1,0:T(8,128)}, f32[128,1536]{1,0:T(8,128)}, u32[]{:S(2)}, u32[]{:S(2)}) collective-permute-start(f32[128,1536]{1,0:T(8,128)} %reduce-scatter.15.cloned.1.call-done), channel_id=1, source_target_pairs={{0,8},{8,0},{1,9},{9,1},{2,10},{10,2},{3,11},{11,3},{4,12},{12,4},... | collective-permute-start | bytes 2359304 | tf_op jit(solution)/shard_map/ppermute | solution.py:481
  708.3 11.0 %copy-start.3 = (f32[32,1024]{1,0:T(8,128)S(1)}, f32[32,1024]{1,0:T(8,128)}, u32[]{:S(2)}) copy-start(f32[32,1024]{1,0:T(8,128)} %copy-done.2) | copy-start | bytes 393220
  708.3 11.0 %copy-start.24 = (f32[8,1,128]{2,1,0:T(1,128)S(1)}, f32[8,1,128]{2,1,0:T(1,128)}, u32[]{:S(2)}) copy-start(f32[8,1,128]{2,1,0:T(1,128)} %copy-done.23) | copy-start | bytes 12292
  708.3 11.0 %copy-start.31 = (f32[512]{0:T(512)S(1)}, f32[512]{0:T(512)}, u32[]{:S(2)}) copy-start(f32[512]{0:T(512)} %copy-done.30) | copy-start | bytes 6148
  708.3 11.0 %copy-start.33 = (f32[512]{0:T(512)S(1)}, f32[512]{0:T(512)}, u32[]{:S(2)}) copy-start(f32[512]{0:T(512)} %copy-done.32) | copy-start | bytes 6148
  708.3 11.0 %copy-start.35 = (f32[512]{0:T(512)S(1)}, f32[512]{0:T(512)}, u32[]{:S(2)}) copy-start(f32[512]{0:T(512)} %copy-done.34) | copy-start | bytes 6148
  719.3 1.5 copy-start.16
  719.4 1.5 copy-start.18
  720.9 8.4 %copy-start.6 = (f32[16,8,8,256]{3,2,1,0:T(8,128)S(1)}, f32[16,8,8,256]{3,2,1,0:T(8,128)}, u32[]{:S(2)}) copy-start(f32[16,8,8,256]{3,2,1,0:T(8,128)} %copy.65) | copy-start | bytes 3145732
  724.3 11.2 %all-to-all-start.1 = ((f32[8,46,128]{2,1,0:T(8,128)}), f32[8,46,128]{2,1,0:T(8,128)S(1)}, u32[]{:S(2)}, u32[]{:S(2)}) async-start(f32[8,46,128]{2,1,0:T(8,128)} %copy.55), calls=%async_computation.6 | async-start | bytes 393216 | tf_op jit(solution)/shard_map/all_to_all | solution.py:545
  732.3 3.2 copy-start.7
  738.9 3.9 collective-permute-start.6
  740.4 19.4 %collective-permute-start.7 = (f32[128,1536]{1,0:T(8,128)}, f32[128,1536]{1,0:T(8,128)S(1)}, u32[]{:S(2)}, u32[]{:S(2)}) collective-permute-start(f32[128,1536]{1,0:T(8,128)} %reduce-scatter.17.cloned.1.call-done), channel_id=1, source_target_pairs={{0,8},{8,0},{1,9},{9,1},{2,10},{10,2},{3,11},{11,3},{4,12},{12,4},... | collective-permute-start | bytes 2359304 | tf_op jit(solution)/shard_map/ppermute | solution.py:481
  (4 other events, 3.9 us)
Sparse Core Ops, SparseCore 0:
  9.8 44.6 all-gather.9
  57.0 41.7 all-gather.15
  101.2 32.9 all-gather.11
  135.8 32.8 all-gather.13
  171.0 32.8 all-gather.17
  217.6 65.9 reduce-scatter.6
  287.1 65.8 reduce-scatter.8
  356.4 65.8 reduce-scatter.10
  425.7 65.9 reduce-scatter.12
  495.0 84.3 reduce-scatter.14
  634.5 55.3 reduce-scatter.16
